TPU v7x, 256 devices: a whole 4x4x8 slice. The times are simulated.
256 devices in a mesh: ens: 8 (over z_lo, core), gy: 4 (over y), gz: 8 (over z_hi, x).
Axes of the slice: x: 4, y: 4, z: 8 (z_hi: 2, z_lo: 4; z = z_hi * 4 + z_lo), core: 2. Of those that a mesh axis runs over, the one named last changes fastest.
Arguments:
- state: float32 [8, 4, 16, 64, 1024], P('ens', None, None, 'gy', 'gz'), parts along dimension 0, may hold values from -32 to 32
- member_set: int32 [8], P('ens'), parts along dimension 0, may hold values from 0 to 15
- courant_table: float32 [16, 3], replicated, may hold values from -0.3 to 0.3
- diffusion_table: float32 [16, 4], replicated, may hold values from 0.05 to 1
- reaction_table: float32 [16, 4, 4], replicated, may hold values from -3 to 3
- quadratic_table: float32 [16, 4], replicated, may hold values from -1 to 1
Outputs:
- state_out: float32 [8, 4, 16, 64, 1024], P('ens', None, None, 'gy', 'gz'), parts along dimension 0
There are 8 independent parts, one for each index of `ens`. A program takes and returns all parts, laid end to end along the dimension named above; an argument that names none is the same for every part. Nothing has to cross between parts.
All inputs are finite; a program needn't handle non-finite values.
Results may differ from a plain program's by a relative error of at most 0.00024.
Values sent between devices are 32-bit elements; how exact they have to be, the bound alone decides.
No kernel may reach another device: no remote copies, remote signals or barrier semaphores. Data moves between devices by JAX's collectives and lax.ppermute only.
A program may use at most 64 MiB of HBM per device.

v0:
```python
import jax
import jax.numpy as jnp
from jax import lax
from jax.sharding import PartitionSpec as P

ITERS = 4


def extended(x, sides, width):
    edges = {}
    for axis, dim in sides:
        devices, length = (lax.axis_size(axis), x.shape[dim])
        up = [(i, (i + 1) % devices) for i in range(devices - 1)]
        last = lax.slice_in_dim(x, length - width, length, axis=dim)
        first = lax.slice_in_dim(x, 0, width, axis=dim)
        edges[dim] = (
            lax.ppermute(last, axis, up),
            lax.ppermute(first, axis, [(b, a) for a, b in up]),
        )
    done = []
    for _, dim in sides:
        low, high = edges[dim]
        around = [(width, width) if d in done else (0, 0) for d in range(x.ndim)]
        x = jnp.concatenate([jnp.pad(low, around), x, jnp.pad(high, around)], axis=dim)
        done.append(dim)
    return x


def extended_2(cells, sides, width):
    for axis, dim in sides:
        count = lax.axis_size(axis)
        ends = count - 1
        head = lax.slice_in_dim(cells, 0, width, axis=dim)
        tail = lax.slice_in_dim(cells, cells.shape[dim] - width, cells.shape[dim], axis=dim)
        cells = jnp.concatenate(
            [
                lax.ppermute(tail, axis, [(i, (i + 1) % count) for i in range(ends)]),
                cells,
                lax.ppermute(head, axis, [((i + 1) % count, i) for i in range(ends)]),
            ],
            axis=dim,
        )
    return cells


def copy_for_each(x, axis):
    copies = jnp.broadcast_to(x, (lax.axis_size(axis), *x.shape))
    return lax.all_to_all(copies, axis, split_axis=0, concat_axis=0, tiled=True)


def taken_together(x, axis):
    return copy_for_each(x, axis).sum(axis=0)


def in_one(arrays, axis):
    ends = [0]
    for a in arrays:
        ends.append(ends[-1] + a.size)
    so_far = taken_together(jnp.concatenate([a.ravel() for a in arrays]), axis)
    return tuple((so_far[b:e].reshape(a.shape) for a, b, e in zip(arrays, ends, ends[1:])))


def lookup(member_set, coeff_table):
    onehot = (
        member_set[:, None] == jnp.arange(coeff_table.shape[0], dtype=jnp.int32)[None, :]
    ).astype(coeff_table.dtype)
    flattened = coeff_table.reshape(coeff_table.shape[0], -1)
    picked = jnp.sum(onehot[:, :, None] * flattened[None, :, :], axis=1)
    return picked.reshape((member_set.shape[0],) + coeff_table.shape[1:])


def spread_out(values):
    return values[:, None, None, None, None]


def beside_all(padded, spatial, offset):
    slicer = [slice(None), slice(None), slice(1, -1), slice(1, -1), slice(1, -1)]
    slicer[spatial] = slice(offset, padded.shape[spatial] - 2 + offset)
    return padded[tuple(slicer)]


def explicit_section(padded, current, courant, reaction, quadratic):
    running = current
    for spatial in range(3):
        velocity = spread_out(courant[:, spatial])
        behind = beside_all(padded, spatial + 2, 0)
        beyond = beside_all(padded, spatial + 2, 2)
        running = (
            running
            - jnp.maximum(velocity, 0.0) * (current - behind)
            - jnp.minimum(velocity, 0.0) * (beyond - current)
        )
    linear = jnp.einsum("mkl,mlxyz->mkxyz", reaction, current, precision=lax.Precision.HIGHEST)
    leading = current[:, 0]
    partner = current[:, 1]
    coupled = leading * partner / (1.0 + leading * leading + partner * partner)
    return running + linear + quadratic[:, :, None, None, None] * coupled[:, None]


def implicit_apply(padded, current, diffuse):
    beside = beside_all(padded, 2, 0) + beside_all(padded, 2, 2)
    beside = beside + beside_all(padded, 3, 0) + beside_all(padded, 3, 2)
    beside = beside + beside_all(padded, 4, 0) + beside_all(padded, 4, 2)
    strength = diffuse[:, :, None, None, None]
    return (1.0 + 6.0 * strength) * current - strength * beside


def inner_product(left_side, right_side):
    return jnp.sum(left_side * right_side, axis=(1, 2, 3, 4))


def least_squares(hessen, beta, iters):
    target = [beta] + [jnp.zeros_like(beta)] * iters
    cosines = []
    sine_list = []
    triangle = []
    for column in range(iters):
        entries = list(hessen[column])
        for earlier in range(column):
            rotated = (
                cosines[earlier] * entries[earlier] + sine_list[earlier] * entries[earlier + 1]
            )
            entries[earlier + 1] = (
                -sine_list[earlier] * entries[earlier] + cosines[earlier] * entries[earlier + 1]
            )
            entries[earlier] = rotated
        radius = jnp.sqrt(
            entries[column] * entries[column] + entries[column + 1] * entries[column + 1]
        )
        cosine = entries[column] / radius
        sine_val = entries[column + 1] / radius
        entries[column] = radius
        target[column + 1] = -sine_val * target[column]
        target[column] = cosine * target[column]
        cosines.append(cosine)
        sine_list.append(sine_val)
        triangle.append(entries[: column + 1])
    coeffs = [None] * iters
    for column in reversed(range(iters)):
        running = target[column]
        for further in range(column + 1, iters):
            running = running - triangle[further][column] * coeffs[further]
        coeffs[column] = running / triangle[column][column]
    return coeffs


def pad_first_dim(padded):
    return jnp.pad(padded, ((0, 0), (0, 0), (1, 1), (0, 0), (0, 0)))


def exchange_rim(current):
    padded = extended(current, (("gy", 3), ("gz", 4)), 1)
    return pad_first_dim(padded)


def normalized(unscaled, factor):
    rimmed = exchange_rim(unscaled) * spread_out(factor)
    vector = unscaled * spread_out(factor)
    return (vector, rimmed)


def shards(state, member_set, courant_table, diffusion_table, reaction_table, quadratic_table):
    courant = lookup(member_set, courant_table)
    diffuse = lookup(member_set, diffusion_table)
    reaction = lookup(member_set, reaction_table)
    quadratic = lookup(member_set, quadratic_table)
    padded = extended_2(state, (("gy", 3), ("gz", 4)), 1)
    source = explicit_section(pad_first_dim(padded), state, courant, reaction, quadratic)
    beta = jnp.sqrt(taken_together(inner_product(source, source), ("gy", "gz")))
    vector, rimmed = normalized(source, 1.0 / beta)
    basis = [vector]
    hessen = []
    for column in range(ITERS):
        image = implicit_apply(rimmed, basis[column], diffuse)
        local_dots = jnp.stack(
            [inner_product(basis[earlier], image) for earlier in range(column + 1)], axis=1
        )
        projections, length_sq = in_one((local_dots, inner_product(image, image)), ("gy", "gz"))
        remainder = image
        for earlier in range(column + 1):
            remainder = remainder - spread_out(projections[:, earlier]) * basis[earlier]
        norm_next = jnp.sqrt(length_sq - jnp.sum(projections * projections, axis=1))
        hessen.append([projections[:, earlier] for earlier in range(column + 1)] + [norm_next])
        if column + 1 < ITERS:
            vector, rimmed = normalized(remainder, 1.0 / norm_next)
            basis.append(vector)
    coeffs = least_squares(hessen, beta, ITERS)
    state_out = spread_out(coeffs[0]) * basis[0]
    for column in range(1, ITERS):
        state_out = state_out + spread_out(coeffs[column]) * basis[column]
    return state_out


def solution(mesh):
    return jax.shard_map(
        shards,
        mesh=mesh,
        in_specs=(P("ens", None, None, "gy", "gz"), P("ens"), P(), P(), P(), P()),
        out_specs=P("ens", None, None, "gy", "gz"),
        check_vma=False,
    )
```

profile of v0, /device:TPU:32, one launch (start us, length us, event | category | flops | bytes accessed | tf_op | source)
XLA Modules:
  0.0 280.7 jit_solution(6096016434201913231)
XLA Ops:
  0.0 1.4 copy.94
  1.5 3.5 %collective-permute-start = (f32[1,4,16,1,128]{4,1,3,2,0:T(4,128)S(1)}, f32[1,4,16,1,128]{4,1,3,2,0:T(4,128)S(1)}, u32[]{:S(2)}, u32[]{:S(2)}) collective-permute-start(f32[1,4,16,1,128]{4,1,3,2,0:T(4,128)S(1)} %get-tuple-element.43), channel_id=1, source_target_pairs={{0,8},{8,16},{16,24},{1,9},{9,17},{17,25},{2,10},{10,18},{18,26},{... | collective-permute-start | bytes 98312 | tf_op jit(solution)/shard_map/ppermute | solution.py:37
  5.0 1.3 collective-permute-start.1
  7.8 3.0 %collective-permute-done.1 = f32[1,4,16,1,128]{4,1,3,2,0:T(4,128)S(1)} collective-permute-done((f32[1,4,16,1,128]{4,1,3,2,0:T(4,128)S(1)}, f32[1,4,16,1,128]{4,1,3,2,0:T(4,128)S(1)}, u32[]{:S(2)}, u32[]{:S(2)}) %collective-permute-start.1) | collective-permute-done | bytes 32800 | tf_op jit(solution)/shard_map/ppermute | solution.py:39
  11.7 3.4 %collective-permute-start.2 = (f32[1,4,16,18,1]{3,2,4,1,0:T(8,128)S(1)}, f32[1,4,16,18,1]{3,2,4,1,0:T(8,128)S(1)}, u32[]{:S(2)}, u32[]{:S(2)}) collective-permute-start(f32[1,4,16,18,1]{3,2,4,1,0:T(8,128)S(1)} %copy.89), channel_id=1, source_target_pairs={{0,1},{1,2},{2,3},{3,4},{4,5},{5,6},{6,7},{8,9},{9,10},{10,11},{11... | collective-permute-start | bytes 13832 | tf_op jit(solution)/shard_map/ppermute | solution.py:37
  15.5 1.3 collective-permute-start.3
  22.3 1.0 select_maximum_fusion
  23.3 3.1 %multiply_reduce_fusion.14 = (f32[]{:T(128)}, f32[1,4,16,16,128]{4,1,3,2,0:T(4,128)S(1)}) fusion(f32[16,16,128]{2,1,0:T(8,128)S(1)} %divide_bitcast_fusion, f32[4]{0:T(128)S(1)} %get-tuple-element.20, f32[4,16,16,128]{3,2,1,0:T(8,128)S(1)} %bitcast.113, f32[4,4,1,1]{1,0,2,3:T(4,128)S(1)} %reshape.261, f32[1,4,16,16,128]{4,1,3,2,0:T(4,128)S(1)} %copy.94, ...), kind=kOutput, calls=%fused_computation.91 | convolution fusion | flops 9830399 | bytes 3417196 | tf_op jit(solution)/shard_map/mkl,mlxyz->mkxyz/dot_general | solution.py:93
  26.8 4.6 %collective-permute-start.4 = (f32[1,4,16,16,1]{4,1,3,2,0:T(4,128)S(1)}, f32[1,4,16,16,1]{4,1,3,2,0:T(4,128)S(1)}, u32[]{:S(2)}, u32[]{:S(2)}) collective-permute-start(f32[1,4,16,16,1]{4,1,3,2,0:T(4,128)S(1)} %get-tuple-element.40), channel_id=1, source_target_pairs={{0,1},{1,2},{2,3},{3,4},{4,5},{5,6},{6,7},{8,9},{9,10},{10,11},{11... | collective-permute-start | bytes 12296 | tf_op jit(solution)/shard_map/ppermute | solution.py:17
  31.4 1.3 collective-permute-start.7
  32.7 3.5 %collective-permute-start.5 = (f32[1,4,16,1,128]{4,1,3,2,0:T(4,128)S(1)}, f32[1,4,16,1,128]{4,1,3,2,0:T(4,128)S(1)}, u32[]{:S(2)}, u32[]{:S(2)}) collective-permute-start(f32[1,4,16,1,128]{4,1,3,2,0:T(4,128)S(1)} %get-tuple-element.38), channel_id=1, source_target_pairs={{0,8},{8,16},{16,24},{1,9},{9,17},{17,25},{2,10},{10,18},{18,26},{... | collective-permute-start | bytes 98312 | tf_op jit(solution)/shard_map/ppermute | solution.py:17
  36.2 1.3 collective-permute-start.6
  37.5 1.2 broadcast_in_dim.10
  38.7 24.5 %all-to-all-start = ((f32[32,1,1]{2,1,0:T(1,128)}), f32[32,1,1]{2,1,0:T(1,128)S(1)}, u32[]{:S(2)}, u32[]{:S(2)}) async-start(f32[32,1,1]{2,1,0:T(1,128)} %broadcast_in_dim.10), calls=%async_computation | async-start | bytes 32768 | tf_op jit(solution)/shard_map/all_to_all | solution.py:48
  63.2 12.1 %all-to-all-done = f32[32,1,1]{2,1,0:T(1,128)S(1)} async-done(((f32[32,1,1]{2,1,0:T(1,128)}), f32[32,1,1]{2,1,0:T(1,128)S(1)}, u32[]{:S(2)}, u32[]{:S(2)}) %all-to-all-start) | async-done | bytes 160 | tf_op jit(solution)/shard_map/all_to_all | solution.py:48
  78.0 2.1 multiply_reduce_fusion.13
  80.0 1.3 pad_maximum_fusion.4
  81.3 17.4 %all_to_all.30 = f32[32,1,2]{2,1,0:T(1,128)S(1)} all-to-all(f32[32,1,2]{2,1,0:T(1,128)S(1)} %broadcast_in_dim.11), channel_id=1, replica_groups=mesh['ens'=8,'gy'=4,'gz'=8] {'gy','gz'}, dimensions={0} | all-to-all | bytes 512 | tf_op jit(solution)/shard_map/all_to_all | solution.py:48
  100.1 1.3 collective-permute-start.10
  101.4 4.5 %collective-permute-start.9 = (f32[1,4,16,1,128]{4,1,3,2,0:T(4,128)S(1)}, f32[1,4,16,1,128]{4,1,3,2,0:T(4,128)S(1)}, u32[]{:S(2)}, u32[]{:S(2)}) collective-permute-start(f32[1,4,16,1,128]{4,1,3,2,0:T(4,128)S(1)} %get-tuple-element.34), channel_id=1, source_target_pairs={{0,8},{8,16},{16,24},{1,9},{9,17},{17,25},{2,10},{10,18},{18,26},{... | collective-permute-start | bytes 98312 | tf_op jit(solution)/shard_map/ppermute | solution.py:17
  106.3 1.3 collective-permute-start.11
  107.6 4.8 %collective-permute-start.8 = (f32[1,4,16,16,1]{4,1,3,2,0:T(4,128)S(1)}, f32[1,4,16,16,1]{4,1,3,2,0:T(4,128)S(1)}, u32[]{:S(2)}, u32[]{:S(2)}) collective-permute-start(f32[1,4,16,16,1]{4,1,3,2,0:T(4,128)S(1)} %get-tuple-element.36), channel_id=1, source_target_pairs={{0,1},{1,2},{2,3},{3,4},{4,5},{5,6},{6,7},{8,9},{9,10},{10,11},{11... | collective-permute-start | bytes 12296 | tf_op jit(solution)/shard_map/ppermute | solution.py:17
  114.2 4.5 %collective-permute-done.11 = f32[1,4,16,16,1]{4,1,3,2,0:T(4,128)S(1)} collective-permute-done((f32[1,4,16,16,1]{4,1,3,2,0:T(4,128)S(1)}, f32[1,4,16,16,1]{4,1,3,2,0:T(4,128)S(1)}, u32[]{:S(2)}, u32[]{:S(2)}) %collective-permute-start.11) | collective-permute-done | bytes 4128 | tf_op jit(solution)/shard_map/ppermute | solution.py:18
  118.7 1.2 collective-permute-done.8
  121.1 2.1 multiply_reduce_fusion.11
  123.2 1.3 maximum_bitcast_fusion
  125.2 34.2 %all_to_all.31 = f32[32,1,3]{2,1,0:T(1,128)S(1)} all-to-all(f32[32,1,3]{2,1,0:T(1,128)S(1)} %broadcast_in_dim.12), channel_id=1, replica_groups=mesh['ens'=8,'gy'=4,'gz'=8] {'gy','gz'}, dimensions={0} | all-to-all | bytes 768 | tf_op jit(solution)/shard_map/all_to_all | solution.py:48
  160.7 1.4 multiply_subtract_fusion.1
  162.1 2.5 collective-permute-start.13
  164.6 1.3 collective-permute-start.14
  166.3 2.6 collective-permute-start.12
  168.9 1.3 collective-permute-start.15
  172.1 3.5 %collective-permute-done.12 = f32[1,4,16,16,1]{4,1,3,2,0:T(4,128)S(1)} collective-permute-done((f32[1,4,16,16,1]{4,1,3,2,0:T(4,128)S(1)}, f32[1,4,16,16,1]{4,1,3,2,0:T(4,128)S(1)}, u32[]{:S(2)}, u32[]{:S(2)}) %collective-permute-start.12) | collective-permute-done | bytes 4128 | tf_op jit(solution)/shard_map/ppermute | solution.py:17
  175.6 4.4 %collective-permute-done.15 = f32[1,4,16,16,1]{4,1,3,2,0:T(4,128)S(1)} collective-permute-done((f32[1,4,16,16,1]{4,1,3,2,0:T(4,128)S(1)}, f32[1,4,16,16,1]{4,1,3,2,0:T(4,128)S(1)}, u32[]{:S(2)}, u32[]{:S(2)}) %collective-permute-start.15) | collective-permute-done | bytes 4128 | tf_op jit(solution)/shard_map/ppermute | solution.py:18
  181.2 2.1 multiply_reduce_fusion.8
  183.3 1.9 maximum_bitcast_fusion.1
  186.0 29.9 %all_to_all.32 = f32[32,1,4]{2,1,0:T(1,128)S(1)} all-to-all(f32[32,1,4]{2,1,0:T(1,128)S(1)} %broadcast_in_dim.13), channel_id=1, replica_groups=mesh['ens'=8,'gy'=4,'gz'=8] {'gy','gz'}, dimensions={0} | all-to-all | bytes 1024 | tf_op jit(solution)/shard_map/all_to_all | solution.py:48
  217.2 2.0 multiply_subtract_fusion
  219.3 2.5 collective-permute-start.17
  221.8 1.3 collective-permute-start.18
  223.5 2.5 collective-permute-start.16
  226.0 1.3 collective-permute-start.19
  232.6 1.5 collective-permute-done.16
  234.1 4.1 %collective-permute-done.19 = f32[1,4,16,16,1]{4,1,3,2,0:T(4,128)S(1)} collective-permute-done((f32[1,4,16,16,1]{4,1,3,2,0:T(4,128)S(1)}, f32[1,4,16,16,1]{4,1,3,2,0:T(4,128)S(1)}, u32[]{:S(2)}, u32[]{:S(2)}) %collective-permute-start.19) | collective-permute-done | bytes 4128 | tf_op jit(solution)/shard_map/ppermute | solution.py:18
  239.4 2.2 multiply_reduce_fusion.4
  241.6 2.6 maximum_bitcast_fusion.2
  245.5 13.6 %all-to-all-start.4 = ((f32[32,1,5]{2,1,0:T(1,128)}), f32[32,1,5]{2,1,0:T(1,128)S(1)}, u32[]{:S(2)}, u32[]{:S(2)}) async-start(f32[32,1,5]{2,1,0:T(1,128)} %broadcast_in_dim.14), calls=%async_computation.4 | async-start | bytes 32768 | tf_op jit(solution)/shard_map/all_to_all | solution.py:48
  262.9 8.4 %all-to-all-done.4 = f32[32,1,5]{2,1,0:T(1,128)S(1)} async-done(((f32[32,1,5]{2,1,0:T(1,128)}), f32[32,1,5]{2,1,0:T(1,128)S(1)}, u32[]{:S(2)}, u32[]{:S(2)}) %all-to-all-start.4) | async-done | bytes 672 | tf_op jit(solution)/shard_map/all_to_all | solution.py:48
  (81 shorter events, 21.7 us)
Async XLA Ops:
  0.0 6.3 %copy-start = (f32[1,4,16,16,128]{4,3,2,1,0:T(8,128)S(1)}, f32[1,4,16,16,128]{4,3,2,1,0:T(8,128)}, u32[]{:S(2)}) copy-start(f32[1,4,16,16,128]{4,3,2,1,0:T(8,128)} %param.6) | copy-start | bytes 1572868
  0.0 7.0 %copy-start.1 = (f32[16,4,4]{0,2,1:T(4,128)S(1)}, f32[16,4,4]{0,2,1:T(4,128)}, u32[]{:S(2)}) copy-start(f32[16,4,4]{0,2,1:T(4,128)} %param.10) | copy-start | bytes 3076
  0.0 7.1 %copy-start.4 = (f32[16,4]{0,1:T(4,128)S(1)}, f32[16,4]{0,1:T(4,128)}, u32[]{:S(2)}) copy-start(f32[16,4]{0,1:T(4,128)} %param.11) | copy-start | bytes 772
  0.0 7.1 %copy-start.3 = (f32[16,4]{0,1:T(4,128)S(1)}, f32[16,4]{0,1:T(4,128)}, u32[]{:S(2)}) copy-start(f32[16,4]{0,1:T(4,128)} %param.9) | copy-start | bytes 772
  0.0 7.3 %copy-start.2 = (f32[16,3]{0,1:T(4,128)S(1)}, f32[16,3]{0,1:T(4,128)}, u32[]{:S(2)}) copy-start(f32[16,3]{0,1:T(4,128)} %param.8) | copy-start | bytes 580
  1.5 5.9 %collective-permute-start = (f32[1,4,16,1,128]{4,1,3,2,0:T(4,128)S(1)}, f32[1,4,16,1,128]{4,1,3,2,0:T(4,128)S(1)}, u32[]{:S(2)}, u32[]{:S(2)}) collective-permute-start(f32[1,4,16,1,128]{4,1,3,2,0:T(4,128)S(1)} %get-tuple-element.43), channel_id=1, source_target_pairs={{0,8},{8,16},{16,24},{1,9},{9,17},{17,25},{2,10},{10,18},{18,26},{... | collective-permute-start | bytes 98312 | tf_op jit(solution)/shard_map/ppermute | solution.py:37
  5.0 5.8 %collective-permute-start.1 = (f32[1,4,16,1,128]{4,1,3,2,0:T(4,128)S(1)}, f32[1,4,16,1,128]{4,1,3,2,0:T(4,128)S(1)}, u32[]{:S(2)}, u32[]{:S(2)}) collective-permute-start(f32[1,4,16,1,128]{4,1,3,2,0:T(4,128)S(1)} %get-tuple-element.42), channel_id=1, source_target_pairs={{8,0},{16,8},{24,16},{9,1},{17,9},{25,17},{10,2},{18,10},{26,18},{... | collective-permute-start | bytes 98312 | tf_op jit(solution)/shard_map/ppermute | solution.py:39
  11.7 9.6 %collective-permute-start.2 = (f32[1,4,16,18,1]{3,2,4,1,0:T(8,128)S(1)}, f32[1,4,16,18,1]{3,2,4,1,0:T(8,128)S(1)}, u32[]{:S(2)}, u32[]{:S(2)}) collective-permute-start(f32[1,4,16,18,1]{3,2,4,1,0:T(8,128)S(1)} %copy.89), channel_id=1, source_target_pairs={{0,1},{1,2},{2,3},{3,4},{4,5},{5,6},{6,7},{8,9},{9,10},{10,11},{11... | collective-permute-start | bytes 13832 | tf_op jit(solution)/shard_map/ppermute | solution.py:37
  15.5 6.2 %collective-permute-start.3 = (f32[1,4,16,18,1]{3,2,4,1,0:T(8,128)S(1)}, f32[1,4,16,18,1]{3,2,4,1,0:T(8,128)S(1)}, u32[]{:S(2)}, u32[]{:S(2)}) collective-permute-start(f32[1,4,16,18,1]{3,2,4,1,0:T(8,128)S(1)} %copy.90), channel_id=1, source_target_pairs={{1,0},{2,1},{3,2},{4,3},{5,4},{6,5},{7,6},{9,8},{10,9},{11,10},{12... | collective-permute-start | bytes 13832 | tf_op jit(solution)/shard_map/ppermute | solution.py:39
  26.8 49.9 %collective-permute-start.4 = (f32[1,4,16,16,1]{4,1,3,2,0:T(4,128)S(1)}, f32[1,4,16,16,1]{4,1,3,2,0:T(4,128)S(1)}, u32[]{:S(2)}, u32[]{:S(2)}) collective-permute-start(f32[1,4,16,16,1]{4,1,3,2,0:T(4,128)S(1)} %get-tuple-element.40), channel_id=1, source_target_pairs={{0,1},{1,2},{2,3},{3,4},{4,5},{5,6},{6,7},{8,9},{9,10},{10,11},{11... | collective-permute-start | bytes 12296 | tf_op jit(solution)/shard_map/ppermute | solution.py:17
  31.4 45.4 %collective-permute-start.7 = (f32[1,4,16,16,1]{4,1,3,2,0:T(4,128)S(1)}, f32[1,4,16,16,1]{4,1,3,2,0:T(4,128)S(1)}, u32[]{:S(2)}, u32[]{:S(2)}) collective-permute-start(f32[1,4,16,16,1]{4,1,3,2,0:T(4,128)S(1)} %get-tuple-element.41), channel_id=1, source_target_pairs={{1,0},{2,1},{3,2},{4,3},{5,4},{6,5},{7,6},{9,8},{10,9},{11,10},{12... | collective-permute-start | bytes 12296 | tf_op jit(solution)/shard_map/ppermute | solution.py:18
  32.7 44.1 %collective-permute-start.5 = (f32[1,4,16,1,128]{4,1,3,2,0:T(4,128)S(1)}, f32[1,4,16,1,128]{4,1,3,2,0:T(4,128)S(1)}, u32[]{:S(2)}, u32[]{:S(2)}) collective-permute-start(f32[1,4,16,1,128]{4,1,3,2,0:T(4,128)S(1)} %get-tuple-element.38), channel_id=1, source_target_pairs={{0,8},{8,16},{16,24},{1,9},{9,17},{17,25},{2,10},{10,18},{18,26},{... | collective-permute-start | bytes 98312 | tf_op jit(solution)/shard_map/ppermute | solution.py:17
  36.2 40.6 %collective-permute-start.6 = (f32[1,4,16,1,128]{4,1,3,2,0:T(4,128)S(1)}, f32[1,4,16,1,128]{4,1,3,2,0:T(4,128)S(1)}, u32[]{:S(2)}, u32[]{:S(2)}) collective-permute-start(f32[1,4,16,1,128]{4,1,3,2,0:T(4,128)S(1)} %get-tuple-element.39), channel_id=1, source_target_pairs={{8,0},{16,8},{24,16},{9,1},{17,9},{25,17},{10,2},{18,10},{26,18},{... | collective-permute-start | bytes 98312 | tf_op jit(solution)/shard_map/ppermute | solution.py:18
  38.7 36.7 %all-to-all-start = ((f32[32,1,1]{2,1,0:T(1,128)}), f32[32,1,1]{2,1,0:T(1,128)S(1)}, u32[]{:S(2)}, u32[]{:S(2)}) async-start(f32[32,1,1]{2,1,0:T(1,128)} %broadcast_in_dim.10), calls=%async_computation | async-start | bytes 32768 | tf_op jit(solution)/shard_map/all_to_all | solution.py:48
  100.1 19.9 %collective-permute-start.10 = (f32[1,4,16,1,128]{4,1,3,2,0:T(4,128)S(1)}, f32[1,4,16,1,128]{4,1,3,2,0:T(4,128)S(1)}, u32[]{:S(2)}, u32[]{:S(2)}) collective-permute-start(f32[1,4,16,1,128]{4,1,3,2,0:T(4,128)S(1)} %get-tuple-element.35), channel_id=1, source_target_pairs={{8,0},{16,8},{24,16},{9,1},{17,9},{25,17},{10,2},{18,10},{26,18},{... | collective-permute-start | bytes 98312 | tf_op jit(solution)/shard_map/ppermute | solution.py:18
  101.4 18.6 %collective-permute-start.9 = (f32[1,4,16,1,128]{4,1,3,2,0:T(4,128)S(1)}, f32[1,4,16,1,128]{4,1,3,2,0:T(4,128)S(1)}, u32[]{:S(2)}, u32[]{:S(2)}) collective-permute-start(f32[1,4,16,1,128]{4,1,3,2,0:T(4,128)S(1)} %get-tuple-element.34), channel_id=1, source_target_pairs={{0,8},{8,16},{16,24},{1,9},{9,17},{17,25},{2,10},{10,18},{18,26},{... | collective-permute-start | bytes 98312 | tf_op jit(solution)/shard_map/ppermute | solution.py:17
  106.3 12.5 %collective-permute-start.11 = (f32[1,4,16,16,1]{4,1,3,2,0:T(4,128)S(1)}, f32[1,4,16,16,1]{4,1,3,2,0:T(4,128)S(1)}, u32[]{:S(2)}, u32[]{:S(2)}) collective-permute-start(f32[1,4,16,16,1]{4,1,3,2,0:T(4,128)S(1)} %get-tuple-element.37), channel_id=1, source_target_pairs={{1,0},{2,1},{3,2},{4,3},{5,4},{6,5},{7,6},{9,8},{10,9},{11,10},{12... | collective-permute-start | bytes 12296 | tf_op jit(solution)/shard_map/ppermute | solution.py:18
  107.6 12.4 %collective-permute-start.8 = (f32[1,4,16,16,1]{4,1,3,2,0:T(4,128)S(1)}, f32[1,4,16,16,1]{4,1,3,2,0:T(4,128)S(1)}, u32[]{:S(2)}, u32[]{:S(2)}) collective-permute-start(f32[1,4,16,16,1]{4,1,3,2,0:T(4,128)S(1)} %get-tuple-element.36), channel_id=1, source_target_pairs={{0,1},{1,2},{2,3},{3,4},{4,5},{5,6},{6,7},{8,9},{9,10},{10,11},{11... | collective-permute-start | bytes 12296 | tf_op jit(solution)/shard_map/ppermute | solution.py:17
  162.1 17.9 %collective-permute-start.13 = (f32[1,4,16,1,128]{4,1,3,2,0:T(4,128)S(1)}, f32[1,4,16,1,128]{4,1,3,2,0:T(4,128)S(1)}, u32[]{:S(2)}, u32[]{:S(2)}) collective-permute-start(f32[1,4,16,1,128]{4,1,3,2,0:T(4,128)S(1)} %get-tuple-element.30), channel_id=1, source_target_pairs={{0,8},{8,16},{16,24},{1,9},{9,17},{17,25},{2,10},{10,18},{18,26},{... | collective-permute-start | bytes 98312 | tf_op jit(solution)/shard_map/ppermute | solution.py:17
  164.6 15.4 %collective-permute-start.14 = (f32[1,4,16,1,128]{4,1,3,2,0:T(4,128)S(1)}, f32[1,4,16,1,128]{4,1,3,2,0:T(4,128)S(1)}, u32[]{:S(2)}, u32[]{:S(2)}) collective-permute-start(f32[1,4,16,1,128]{4,1,3,2,0:T(4,128)S(1)} %get-tuple-element.31), channel_id=1, source_target_pairs={{8,0},{16,8},{24,16},{9,1},{17,9},{25,17},{10,2},{18,10},{26,18},{... | collective-permute-start | bytes 98312 | tf_op jit(solution)/shard_map/ppermute | solution.py:18
  166.3 9.3 %collective-permute-start.12 = (f32[1,4,16,16,1]{4,1,3,2,0:T(4,128)S(1)}, f32[1,4,16,16,1]{4,1,3,2,0:T(4,128)S(1)}, u32[]{:S(2)}, u32[]{:S(2)}) collective-permute-start(f32[1,4,16,16,1]{4,1,3,2,0:T(4,128)S(1)} %get-tuple-element.32), channel_id=1, source_target_pairs={{0,1},{1,2},{2,3},{3,4},{4,5},{5,6},{6,7},{8,9},{9,10},{10,11},{11... | collective-permute-start | bytes 12296 | tf_op jit(solution)/shard_map/ppermute | solution.py:17
  168.9 11.1 %collective-permute-start.15 = (f32[1,4,16,16,1]{4,1,3,2,0:T(4,128)S(1)}, f32[1,4,16,16,1]{4,1,3,2,0:T(4,128)S(1)}, u32[]{:S(2)}, u32[]{:S(2)}) collective-permute-start(f32[1,4,16,16,1]{4,1,3,2,0:T(4,128)S(1)} %get-tuple-element.33), channel_id=1, source_target_pairs={{1,0},{2,1},{3,2},{4,3},{5,4},{6,5},{7,6},{9,8},{10,9},{11,10},{12... | collective-permute-start | bytes 12296 | tf_op jit(solution)/shard_map/ppermute | solution.py:18
  219.3 18.9 %collective-permute-start.17 = (f32[1,4,16,1,128]{4,1,3,2,0:T(4,128)S(1)}, f32[1,4,16,1,128]{4,1,3,2,0:T(4,128)S(1)}, u32[]{:S(2)}, u32[]{:S(2)}) collective-permute-start(f32[1,4,16,1,128]{4,1,3,2,0:T(4,128)S(1)} %get-tuple-element.26), channel_id=1, source_target_pairs={{0,8},{8,16},{16,24},{1,9},{9,17},{17,25},{2,10},{10,18},{18,26},{... | collective-permute-start | bytes 98312 | tf_op jit(solution)/shard_map/ppermute | solution.py:17
  221.8 16.4 %collective-permute-start.18 = (f32[1,4,16,1,128]{4,1,3,2,0:T(4,128)S(1)}, f32[1,4,16,1,128]{4,1,3,2,0:T(4,128)S(1)}, u32[]{:S(2)}, u32[]{:S(2)}) collective-permute-start(f32[1,4,16,1,128]{4,1,3,2,0:T(4,128)S(1)} %get-tuple-element.27), channel_id=1, source_target_pairs={{8,0},{16,8},{24,16},{9,1},{17,9},{25,17},{10,2},{18,10},{26,18},{... | collective-permute-start | bytes 98312 | tf_op jit(solution)/shard_map/ppermute | solution.py:18
  223.5 10.6 %collective-permute-start.16 = (f32[1,4,16,16,1]{4,1,3,2,0:T(4,128)S(1)}, f32[1,4,16,16,1]{4,1,3,2,0:T(4,128)S(1)}, u32[]{:S(2)}, u32[]{:S(2)}) collective-permute-start(f32[1,4,16,16,1]{4,1,3,2,0:T(4,128)S(1)} %get-tuple-element.28), channel_id=1, source_target_pairs={{0,1},{1,2},{2,3},{3,4},{4,5},{5,6},{6,7},{8,9},{9,10},{10,11},{11... | collective-permute-start | bytes 12296 | tf_op jit(solution)/shard_map/ppermute | solution.py:17
  226.0 12.2 %collective-permute-start.19 = (f32[1,4,16,16,1]{4,1,3,2,0:T(4,128)S(1)}, f32[1,4,16,16,1]{4,1,3,2,0:T(4,128)S(1)}, u32[]{:S(2)}, u32[]{:S(2)}) collective-permute-start(f32[1,4,16,16,1]{4,1,3,2,0:T(4,128)S(1)} %get-tuple-element.29), channel_id=1, source_target_pairs={{1,0},{2,1},{3,2},{4,3},{5,4},{6,5},{7,6},{9,8},{10,9},{11,10},{12... | collective-permute-start | bytes 12296 | tf_op jit(solution)/shard_map/ppermute | solution.py:18
  245.5 25.7 %all-to-all-start.4 = ((f32[32,1,5]{2,1,0:T(1,128)}), f32[32,1,5]{2,1,0:T(1,128)S(1)}, u32[]{:S(2)}, u32[]{:S(2)}) async-start(f32[32,1,5]{2,1,0:T(1,128)} %broadcast_in_dim.14), calls=%async_computation.4 | async-start | bytes 32768 | tf_op jit(solution)/shard_map/all_to_all | solution.py:48
where the time goes:
time: 282 us; the launch traced here: 281 us
  starting transfers between devices  85.5 us (30%)
  blocking collectives  81.5 us (29%)
  waiting for transfers between devices  42.7 us (15%)
  other arithmetic  30.9 us (11%)
  between operations  23.7 us (8%)
  local copies, waits for them, and re-layouts  13.3 us (5%)
  matrix products  3.14 us (1%)
    all_to_all x3, blocking collectives, copy_for_each(): return lax.all_to_all(copies, axis, split_axis=0, concat_axis=0, tiled=True)  81.5 us
    all_to_all x2, starting transfers between devices, copy_for_each(): return lax.all_to_all(copies, axis, split_axis=0, concat_axis=0, tiled=True)  38.1 us
    ppermute x8, starting transfers between devices, extended(): lax.ppermute(last, axis, up)  27.6 us
    all_to_all x2, waiting for transfers between devices, copy_for_each(): return lax.all_to_all(copies, axis, split_axis=0, concat_axis=0, tiled=True)  20.5 us
    ppermute x8, waiting for transfers between devices, extended(): lax.ppermute(first, axis, [(b, a) for a, b in up])  13.1 us
    ppermute x8, starting transfers between devices, extended(): lax.ppermute(first, axis, [(b, a) for a, b in up])  10.3 us
    reduce_sum x4, other arithmetic, inner_product(): return jnp.sum(left_side * right_side, axis=(1, 2, 3, 4))  8.4 us
    ppermute x2, starting transfers between devices, extended_2(): lax.ppermute(tail, axis, [(i, (i + 1) % count) for i in range(ends)])  6.87 us
  transfers between devices with their start and end apart: 22, of which 9 were waited for; matrix products, arithmetic and copies ran while one was open for 2% of the time, Pallas kernels for 0%

commit v1 on v0

v1 whole, which is shorter than its diff:
```python
import functools

import jax
import jax.numpy as jnp
from jax import lax
from jax.experimental import pallas as pl
from jax.experimental.pallas import tpu as pltpu
from jax.sharding import PartitionSpec as P

SPECIES = 4
X = 16
Y = 16
Z = 128
HALO = 5
GROUP = 6
PACKS = 3
ROWS = Y + 2 * HALO
DOTS = 13
SLOTS = 16

F32 = jnp.float32
VMEM = pltpu.VMEM
SMEM = pltpu.SMEM


def struct(*shape):
    return jax.ShapeDtypeStruct(shape, F32)


def lanes():
    return lax.broadcasted_iota(jnp.int32, (X, Z), 1)


def shift(v, amount):
    amount %= Z
    return pltpu.roll(v, amount, 1) if amount else v


def own(state_ref, s, y):
    return state_ref[pl.ds(s * X * Y + y, X, stride=Y), :]


def over_rows(count, at_once, body, carry=None):
    def step(i, c):
        for k in range(at_once):
            c = body(i * at_once + k, c)
        return c

    whole = count // at_once
    carry = lax.fori_loop(0, whole, step, carry)
    for row in range(whole * at_once, count):
        carry = body(row, carry)
    return carry


def pack_kernel(state_ref, top_ref, bottom_ref, strip_ref, far_ref, near_ref):
    lane = lanes()
    odd = lax.axis_index("gz") % 2 == 1
    place = lane % 32
    for y in range(Y):
        total = jnp.zeros((X, Z), F32)
        for s in range(SPECIES):
            v = own(state_ref, s, y)
            if y < HALO:
                top_ref[y, s] = v
            if y >= Y - HALO:
                bottom_ref[y - (Y - HALO), s] = v
            low = shift(v, 32 * s + HALO)
            high = shift(v, 32 * s + 16 - (Z - 11))
            total = jnp.where((lane >= 32 * s + HALO) & (lane < 32 * s + 16), low, total)
            total = jnp.where((lane >= 32 * s + 16) & (lane < 32 * s + 27), high, total)
        strip_ref[y] = total
    for g in range(PACKS):
        lows = jnp.zeros((X, Z), F32)
        highs = jnp.zeros((X, Z), F32)
        for i in range(GROUP):
            if g * GROUP + i < Y:
                v = strip_ref[g * GROUP + i]
                here = (place >= i * HALO) & (place < (i + 1) * HALO)
                lows = jnp.where(here, shift(v, i * HALO - HALO), lows)
                highs = jnp.where(here, shift(v, i * HALO - 22), highs)
        far_ref[g] = jnp.where(odd, highs, lows)
        near_ref[g] = jnp.where(odd, lows, highs)


def unpack_kernel(strip_ref, far_ref, near_ref, full_ref, top_ref, bottom_ref):
    place = lanes() % 32
    odd = lax.axis_index("gz") % 2 == 1
    for g in range(PACKS):
        far, near = far_ref[g], near_ref[g]
        after = jnp.where(odd, far, near)
        before = jnp.where(odd, near, far)
        for i in range(GROUP):
            y = g * GROUP + i
            if y < Y:
                v = strip_ref[y]
                v = jnp.where(place < HALO, shift(before, -i * HALO), v)
                v = jnp.where(place >= 27, shift(after, 27 - i * HALO), v)
                full_ref[y] = v
                if y < HALO:
                    top_ref[y] = v
                if y >= Y - HALO:
                    bottom_ref[y - (Y - HALO)] = v


def beside_x(v):
    row = lax.broadcasted_iota(jnp.int32, (X, Z), 0)
    below = jnp.where(row == 0, 0.0, pltpu.roll(v, 1, 0))
    above = jnp.where(row == X - 1, 0.0, pltpu.roll(v, X - 1, 0))
    return below, above


def in_grid():
    low = jnp.where(lax.axis_index("gy") > 0, 1.0, 0.0).astype(F32)
    high = jnp.where(lax.axis_index("gy") < lax.axis_size("gy") - 1, 1.0, 0.0).astype(F32)
    return low, high


def row_flag(row, before, low, high):
    flag = jnp.where(row < before, low, 1.0)
    return jnp.where(row >= before + Y, high, flag)


def one_row(value):
    return jnp.full((1, Z), value, F32)


def largest(diffusion_ref, member):
    d = [diffusion_ref[member, s] for s in range(SPECIES)]
    return d, jnp.maximum(jnp.maximum(d[0], d[1]), jnp.maximum(d[2], d[3]))


def dot_terms(b):
    pairs = ((0, 0), (0, 1), (0, 3), (0, 4), (1, 1), (1, 2), (1, 3), (1, 4), (2, 2), (2, 3), (3, 3), (3, 4), (4, 4))
    out = []
    for i, j in pairs:
        p = b[i] * b[j]
        out.append(p[:8] + p[8:])
    return out


def level_value(k, image, v, before):
    if k < 3:
        return image
    if k == 3:
        return image - v
    return 2.0 * (image - v) - before


def main_kernel(
    state_ref, low_ref, high_ref, member_ref, courant_ref, diffusion_ref, reaction_ref, quadratic_ref,
    basis_ref, dots_ref, wide, b0, b1, b2, b3,
):
    member = member_ref[0]
    low, high = in_grid()
    for r in range(HALO):
        for s in range(SPECIES):
            wide[r, s] = low_ref[r, s] * low
            wide[HALO + Y + r, s] = high_ref[r, s] * high
    for y in range(Y):
        for s in range(SPECIES):
            wide[HALO + y, s] = own(state_ref, s, y)

    courant = [courant_ref[member, d] for d in range(3)]
    plus = [jnp.maximum(c, 0.0) for c in courant]
    minus = [jnp.minimum(c, 0.0) for c in courant]
    kept = 1.0 - (plus[0] - minus[0]) - (plus[1] - minus[1]) - (plus[2] - minus[2])
    linear = [[reaction_ref[member, 4 * k + l] for l in range(SPECIES)] for k in range(SPECIES)]
    for k in range(SPECIES):
        linear[k][k] = linear[k][k] + kept
    quad = [quadratic_ref[member, k] for k in range(SPECIES)]

    def source_row(row, _):
        flag = row_flag(row, HALO - 1, low, high)
        v = [wide[row + 1, s] for s in range(SPECIES)]
        a, b = v[0], v[1]
        coupled = a * b / (1.0 + a * a + b * b)
        for k in range(SPECIES):
            below, above = beside_x(v[k])
            out = plus[0] * below - minus[0] * above
            out = out + (plus[1] * wide[row, k] - minus[1] * wide[row + 2, k])
            out = out + (plus[2] * shift(v[k], 1) - minus[2] * shift(v[k], -1))
            for l in range(SPECIES):
                out = out + linear[k][l] * v[l]
            b0[row, k] = (out + quad[k] * coupled) * flag
        return _

    over_rows(Y + 8, 4, source_row)

    d, most = largest(diffusion_ref, member)
    scale = [one_row(d[s]) / one_row(6.0 * most) for s in range(SPECIES)]

    buffers = [b0, b1, b2, b3]

    def image_of(ref, row, s):
        v = ref[row + 1, s]
        below, above = beside_x(v)
        beside = (below + above) + (ref[row, s] + ref[row + 2, s]) + (shift(v, 1) + shift(v, -1))
        return scale[s] * (6.0 * v - beside), v

    for k in (1, 2, 3):
        before = 4 - k

        def level_row(row, _, k=k, before=before):
            flag = row_flag(row, before, low, high)
            for s in range(SPECIES):
                image, v = image_of(buffers[k - 1], row, s)
                buffers[k][row, s] = level_value(k, image, v, None) * flag
            return _

        over_rows(Y + 2 * before, 4, level_row)

    def last_row(row, sums):
        sums = list(sums)
        for s in range(SPECIES):
            image, v = image_of(b3, row, s)
            b = [buffers[k][row + 4 - k, s] for k in range(4)]
            for k in range(4):
                basis_ref[k, row, s] = b[k]
            b.append(level_value(4, image, v, b[2]))
            sums = [t + p for t, p in zip(sums, dot_terms(b))]
        return tuple(sums)

    sums = over_rows(Y, 2, last_row, tuple(jnp.zeros((8, Z), F32) for _ in range(DOTS)))
    lane = lax.broadcasted_iota(jnp.int32, (8, Z), 1)
    inner = (lane >= HALO) & (lane < Z - HALO)
    for k in range(DOTS):
        dots_ref[k] = jnp.where(inner, sums[k], 0.0)


def strip_kernel(
    strip_ref, low_ref, high_ref, dots_in_ref, member_ref, courant_ref, diffusion_ref, reaction_ref, quadratic_ref,
    basis_ref, total_ref, wide, b0, b1, b2, b3,
):
    member = member_ref[0]
    low, high = in_grid()
    for r in range(HALO):
        wide[r] = low_ref[r] * low
        wide[HALO + Y + r] = high_ref[r] * high
    for y in range(Y):
        wide[HALO + y] = strip_ref[y]

    lane = lax.broadcasted_iota(jnp.int32, (1, Z), 1)
    place = lane % 32

    def by_species(values):
        out = one_row(values[3])
        for s in (2, 1, 0):
            out = jnp.where(lane < 32 * (s + 1), values[s], out)
        return out

    first = jnp.where(lax.axis_index("gz") > 0, 1.0, 0.0).astype(F32)
    last = jnp.where(lax.axis_index("gz") < lax.axis_size("gz") - 1, 1.0, 0.0).astype(F32)
    inside = jnp.where(place < HALO, first, jnp.where(place >= 27, last, one_row(1.0)))

    courant = [courant_ref[member, d] for d in range(3)]
    plus = [jnp.maximum(c, 0.0) for c in courant]
    minus = [jnp.minimum(c, 0.0) for c in courant]
    kept = 1.0 - (plus[0] - minus[0]) - (plus[1] - minus[1]) - (plus[2] - minus[2])
    linear = [
        by_species([reaction_ref[member, 4 * k + (k - t) % SPECIES] for k in range(SPECIES)]) for t in range(SPECIES)
    ]
    linear[0] = linear[0] + kept
    quad = by_species([quadratic_ref[member, k] for k in range(SPECIES)])

    def source_row(row, _):
        flag = row_flag(row, HALO - 1, low, high)
        v = wide[row + 1]
        turned = [v] + [shift(v, 32 * t) for t in range(1, SPECIES)]
        b = turned[3]
        coupled = v * b / (1.0 + v * v + b * b)
        coupled = jnp.where(lane < 32, coupled, 0.0)
        coupled = coupled + shift(coupled, 32)
        coupled = coupled + shift(coupled, 64)
        below, above = beside_x(v)
        out = plus[0] * below - minus[0] * above
        out = out + (plus[1] * wide[row] - minus[1] * wide[row + 2])
        out = out + (plus[2] * shift(v, 1) - minus[2] * shift(v, -1))
        for t in range(SPECIES):
            out = out + linear[t] * turned[t]
        b0[row] = (out + quad * coupled) * (flag * inside)
        return _

    over_rows(Y + 8, 12, source_row)

    d, most = largest(diffusion_ref, member)
    scale = by_species(d) / one_row(6.0 * most)
    buffers = [b0, b1, b2, b3]

    def image_of(ref, row):
        v = ref[row + 1]
        below, above = beside_x(v)
        beside = (below + above) + (ref[row] + ref[row + 2]) + (shift(v, 1) + shift(v, -1))
        return scale * (6.0 * v - beside), v

    for k in (1, 2, 3):
        before = 4 - k

        def level_row(row, _, k=k, before=before):
            flag = row_flag(row, before, low, high)
            image, v = image_of(buffers[k - 1], row)
            buffers[k][row] = level_value(k, image, v, None) * (flag * inside)
            return _

        over_rows(Y + 2 * before, 11 if k == 1 else 10 if k == 2 else 9, level_row)

    def last_row(row, sums):
        image, v = image_of(b3, row)
        b = [buffers[k][row + 4 - k] for k in range(4)]
        for k in range(4):
            basis_ref[k, row] = b[k]
        b.append(level_value(4, image, v, b[2]))
        return tuple(t + p for t, p in zip(sums, dot_terms(b)))

    sums = over_rows(Y, 8, last_row, tuple(jnp.zeros((8, Z), F32) for _ in range(DOTS)))
    edge = ((place >= HALO) & (place < 2 * HALO)) | ((place >= 22) & (place < 27))
    slot = lax.broadcasted_iota(jnp.int32, (8, SLOTS), 1)
    total = jnp.zeros((8, SLOTS), F32)
    for k in range(DOTS):
        both = jnp.where(edge, sums[k], 0.0) + dots_in_ref[k]
        one = jnp.sum(jnp.sum(both, axis=0, keepdims=True), axis=1, keepdims=True)
        total = jnp.where(slot == k, one, total)
    for i in range(total_ref.shape[0] // 8):
        total_ref[8 * i : 8 * i + 8, :] = total


def least_squares(h, r):
    n = 5
    root = [[None] * n for _ in range(n)]
    for i in range(n):
        rest = h[i][i]
        for k in range(i):
            rest = rest - root[k][i] * root[k][i]
        rest = jnp.maximum(rest, 3e-7 * h[i][i])
        inverse = 1.0 / jnp.sqrt(rest)
        root[i][i] = rest * inverse
        for j in range(i + 1, n):
            t = h[i][j]
            for k in range(i):
                t = t - root[k][i] * root[k][j]
            root[i][j] = t * inverse
    wide = 1.0 + r
    half = 0.5 * r
    columns = []
    for j, weights in enumerate((((0, 1.0), (1, r)), ((1, 1.0), (2, r)), ((2, wide), (3, r)), ((2, half), (3, wide), (4, half)))):
        column = []
        for i in range(j + 2):
            terms = [w * root[i][m] for m, w in weights if i <= m]
            column.append(sum(terms[1:], terms[0]))
        columns.append(column)
    target = [root[0][0]]
    cosines, sines = [], []
    for j in range(4):
        e = columns[j]
        for i in range(j):
            e[i], e[i + 1] = cosines[i] * e[i] + sines[i] * e[i + 1], cosines[i] * e[i + 1] - sines[i] * e[i]
        inverse = 1.0 / jnp.sqrt(e[j] * e[j] + e[j + 1] * e[j + 1])
        cosines.append(e[j] * inverse)
        sines.append(e[j + 1] * inverse)
        e[j] = cosines[j] * e[j] + sines[j] * e[j + 1]
        target.append(-sines[j] * target[j])
        target[j] = cosines[j] * target[j]
    y = [None] * 4
    for j in (3, 2, 1, 0):
        t = target[j]
        for k in range(j + 1, 4):
            t = t - columns[k][j] * y[k]
        y[j] = t / columns[j][j]
    return y


def combine_kernel(sums_ref, member_ref, diffusion_ref, basis_ref, strip_ref, out_ref):
    total = jnp.sum(sums_ref[...], axis=0, keepdims=True)
    p = [total[:, k : k + 1] for k in range(DOTS)]
    h00, h01, h03, h04, h11, h12, h13, h14, h22, h23, h33, h34, h44 = p
    h = [
        [h00, h01, h11, h03, h04],
        [None, h11, h12, h13, h14],
        [None, None, h22, h23, 2.0 * h33 - h22],
        [None, None, None, h33, h34],
        [None, None, None, None, h44],
    ]
    _, most = largest(diffusion_ref, member_ref[0])
    y = [jnp.broadcast_to(c, (X, Z)) for c in least_squares(h, 6.0 * most)]
    lane = lanes()
    for row in range(Y):
        strip = y[0] * strip_ref[0, row]
        for k in (1, 2, 3):
            strip = strip + y[k] * strip_ref[k, row]
        for s in range(SPECIES):
            v = y[0] * basis_ref[0, row, s]
            for k in (1, 2, 3):
                v = v + y[k] * basis_ref[k, row, s]
            v = jnp.where(lane < HALO, shift(strip, -(32 * s + HALO)), v)
            v = jnp.where(lane >= Z - HALO, shift(strip, Z - HALO - (32 * s + 22)), v)
            out_ref[pl.ds(s * X * Y + row, X, stride=Y), :] = v


def call(kernel, outs, spaces, scratch=(), flops=1000):
    return pl.pallas_call(
        kernel,
        out_shape=outs,
        in_specs=[pl.BlockSpec(memory_space=m) for m in spaces],
        out_specs=jax.tree.map(lambda _: pl.BlockSpec(memory_space=VMEM), outs),
        scratch_shapes=list(scratch),
        cost_estimate=pl.CostEstimate(flops=flops, bytes_accessed=1 << 20, transcendentals=0),
        compiler_params=pltpu.CompilerParams(vmem_limit_bytes=24 << 20),
    )


def shards(state, member_set, courant_table, diffusion_table, reaction_table, quadratic_table):
    gy, gz = lax.axis_size("gy"), lax.axis_size("gz")
    up = [(i, (i + 1) % gy) for i in range(gy)]
    down = [(b, a) for a, b in up]
    far, near = [], []
    for i in range(gz - 1):
        (far if i % 2 else near).extend([(i, i + 1), (i + 1, i)])
    flat = state.reshape(SPECIES * X * Y, Z)
    tables = (courant_table, diffusion_table, reaction_table.reshape(-1, SPECIES * SPECIES), quadratic_table)

    edge = struct(HALO, SPECIES, X, Z)
    strip_edge = struct(HALO, X, Z)
    pack = struct(PACKS, X, Z)
    top, bottom, strip, to_far, to_near = call(
        pack_kernel, (edge, edge, struct(Y, X, Z), pack, pack), [VMEM]
    )(flat)
    from_far = lax.ppermute(to_far, "gz", far)
    from_near = lax.ppermute(to_near, "gz", near)
    low = lax.ppermute(bottom, "gy", up)
    high = lax.ppermute(top, "gy", down)
    strip, strip_top, strip_bottom = call(
        unpack_kernel, (struct(Y, X, Z), strip_edge, strip_edge), [VMEM] * 3
    )(strip, from_far, from_near)
    strip_low = lax.ppermute(strip_bottom, "gy", up)
    strip_high = lax.ppermute(strip_top, "gy", down)

    wide = (SPECIES, X, Z)
    basis, dots = call(
        main_kernel,
        (struct(4, Y, *wide), struct(DOTS, 8, Z)),
        [VMEM] * 3 + [SMEM] * 5,
        [VMEM((n, *wide), F32) for n in (ROWS, Y + 8, Y + 6, Y + 4, Y + 2)],
        flops=10_000_000,
    )(flat, low, high, member_set, *tables)
    strip_basis, total = call(
        strip_kernel,
        (struct(4, Y, X, Z), struct(gy * gz, SLOTS)),
        [VMEM] * 4 + [SMEM] * 5,
        [VMEM((n, X, Z), F32) for n in (ROWS, Y + 8, Y + 6, Y + 4, Y + 2)],
    )(strip, strip_low, strip_high, dots, member_set, *tables)
    sums = lax.all_to_all(total, ("gy", "gz"), split_axis=0, concat_axis=0, tiled=True)
    out = call(
        combine_kernel, struct(SPECIES * X * Y, Z), [VMEM, SMEM, SMEM, VMEM, VMEM]
    )(sums, member_set, diffusion_table, basis, strip_basis)
    return out.reshape(state.shape)


def solution(mesh):
    return jax.shard_map(
        shards,
        mesh=mesh,
        in_specs=(P("ens", None, None, "gy", "gz"), P("ens"), P(), P(), P(), P()),
        out_specs=P("ens", None, None, "gy", "gz"),
        check_vma=False,
    )
```

time: 282 us -> 56.1 us (0.20)
  starting transfers between devices: 85.5 us -> 11.6 us
  blocking collectives: 81.5 us -> 25.1 us
  waiting for transfers between devices: 42.7 us -> 1.82 us
  other arithmetic: 30.9 us -> 0 us
  between operations: 23.7 us -> 0.71 us
  Pallas kernels: 0 us -> 11.4 us
  local copies, waits for them, and re-layouts: 13.3 us -> 5.12 us
  matrix products: 3.14 us -> 0 us
    all_to_all x3 -> x1, blocking collectives: 81.5 us -> 25.1 us  [shards(): lax.all_to_all(total, ('gy', 'gz'), split_axis=0, concat_axis=0, tiled=True)]
    all_to_all x2 -> x0, starting transfers between devices: 38.1 us -> none  [copy_for_each(): return lax.all_to_all(copies, axis, split_axis=0, concat_axis=0, tiled=True)]
    ppermute x20 -> x6, starting transfers between devices: 47.4 us -> 11.6 us  [the longest x1 4.31 us: shards(): from_near = lax.ppermute(to_near, 'gz', near)]
    all_to_all x2 -> x0, waiting for transfers between devices: 20.5 us -> none  [copy_for_each(): return lax.all_to_all(copies, axis, split_axis=0, concat_axis=0, tiled=True)]
    ppermute x20 -> x6, waiting for transfers between devices: 22.2 us -> 1.82 us  [the longest x1 1.8 us: shards(): from_near = lax.ppermute(to_near, 'gz', near)]
    reduce_sum x15 -> x0, other arithmetic: 11.5 us -> none  [the longest x4 8.4 us: inner_product(): return jnp.sum(left_side * right_side, axis=(1, 2, 3, 4))]
    pallas_call x0 -> x5, Pallas kernels: none -> 11.4 us  [the longest x1 5.23 us: shards(): call(main_kernel, (struct(4, Y, *wide), struct(DOTS, 8, Z)), [VMEM] * 3 +...]
    concatenate x9 -> x0, other arithmetic: 8.16 us -> none  [the longest x4 3.78 us: extended(): jnp.concatenate([jnp.pad(low, around), x, jnp.pad(high, around)], axis=dim)]
  transfers between devices with their start and end apart: 22 -> 6, of which waited for: 9 -> 1; matrix products, arithmetic and copies ran while one was open for 2% -> 5% of each run, Pallas kernels for 0% -> 10%
where the time goes in v1:
time: 56.1 us; the launch traced here: 55.8 us
  blocking collectives  25.1 us (45%)
  starting transfers between devices  11.6 us (21%)
  Pallas kernels  11.4 us (20%)
  local copies, waits for them, and re-layouts  5.12 us (9%)
  waiting for transfers between devices  1.82 us (3%)
  between operations  0.71 us (1%)
    all_to_all x1, blocking collectives, shards(): lax.all_to_all(total, ('gy', 'gz'), split_axis=0, concat_axis=0, tiled=True)  25.1 us
    pallas_call x1, Pallas kernels, shards(): call(main_kernel, (struct(4, Y, *wide), struct(DOTS, 8, Z)), [VMEM] * 3 +...  5.23 us
    unnamed x7, local copies, waits for them, and re-layouts  4.36 us
    ppermute x1, starting transfers between devices, shards(): from_near = lax.ppermute(to_near, 'gz', near)  4.31 us
    pallas_call x1, Pallas kernels, shards(): call(combine_kernel, struct(SPECIES * X * Y, Z), [VMEM, SMEM, SMEM, VMEM,...  2.88 us
    ppermute x1, starting transfers between devices, shards(): strip_high = lax.ppermute(strip_top, 'gy', down)  2.87 us
    pallas_call x1, Pallas kernels, shards(): call(strip_kernel, (struct(4, Y, X, Z), struct(gy * gz, SLOTS)), [VMEM] *...  2.72 us
    ppermute x1, waiting for transfers between devices, shards(): from_near = lax.ppermute(to_near, 'gz', near)  1.8 us
  transfers between devices with their start and end apart: 6, of which 1 were waited for; matrix products, arithmetic and copies ran while one was open for 5% of the time, Pallas kernels for 10%

profile of v1, /device:TPU:32, one launch (start us, length us, event | category | flops | bytes accessed | tf_op | source)
XLA Modules:
  0.0 55.8 jit_solution(6061849022183930940)
XLA Ops:
  0.0 0.0 copy-start
  0.0 1.0 %copy-done = f32[1,4,16,16,128]{4,3,2,1,0:T(8,128)S(1)} copy-done((f32[1,4,16,16,128]{4,3,2,1,0:T(8,128)S(1)}, f32[1,4,16,16,128]{4,3,2,1,0:T(8,128)}, u32[]{:S(2)}) %copy-start) | copy-done | bytes 524312
  1.0 0.4 shard_map.64
  1.5 1.7 %collective-permute-start.4 = (f32[5,4,16,128]{3,2,1,0:T(8,128)S(1)}, f32[5,4,16,128]{3,2,1,0:T(8,128)S(1)}, u32[]{:S(2)}, u32[]{:S(2)}) collective-permute-start(f32[5,4,16,128]{3,2,1,0:T(8,128)S(1)} %get-tuple-element.23), channel_id=1, source_target_pairs={{0,8},{8,16},{16,24},{24,0},{1,9},{9,17},{17,25},{25,1},{2,10},{10... | collective-permute-start | bytes 491528 | tf_op jit(solution)/shard_map/ppermute | solution.py:429
  3.1 1.7 %collective-permute-start.5 = (f32[5,4,16,128]{3,2,1,0:T(8,128)S(1)}, f32[5,4,16,128]{3,2,1,0:T(8,128)S(1)}, u32[]{:S(2)}, u32[]{:S(2)}) collective-permute-start(f32[5,4,16,128]{3,2,1,0:T(8,128)S(1)} %get-tuple-element.24), channel_id=1, source_target_pairs={{8,0},{16,8},{24,16},{0,24},{9,1},{17,9},{25,17},{1,25},{10,2},{18... | collective-permute-start | bytes 491528 | tf_op jit(solution)/shard_map/ppermute | solution.py:430
  4.8 0.7 %collective-permute-start = (f32[3,16,128]{2,1,0:T(8,128)S(1)}, f32[3,16,128]{2,1,0:T(8,128)S(1)}, u32[]{:S(2)}, u32[]{:S(2)}) collective-permute-start(f32[3,16,128]{2,1,0:T(8,128)S(1)} %get-tuple-element.18), channel_id=1, source_target_pairs={{1,2},{2,1},{3,4},{4,3},{5,6},{6,5},{9,10},{10,9},{11,12},{12,11},... | collective-permute-start | bytes 73736 | tf_op jit(solution)/shard_map/ppermute | solution.py:427
  5.4 4.3 %collective-permute-start.1 = (f32[3,16,128]{2,1,0:T(8,128)S(1)}, f32[3,16,128]{2,1,0:T(8,128)S(1)}, u32[]{:S(2)}, u32[]{:S(2)}) collective-permute-start(f32[3,16,128]{2,1,0:T(8,128)S(1)} %get-tuple-element.19), channel_id=1, source_target_pairs={{0,1},{1,0},{2,3},{3,2},{4,5},{5,4},{6,7},{7,6},{8,9},{9,8},{10,11... | collective-permute-start | bytes 73736 | tf_op jit(solution)/shard_map/ppermute | solution.py:428
  9.7 0.0 collective-permute-done.far_ref
  9.7 1.8 %collective-permute-done.1.near_ref = f32[3,16,128]{2,1,0:T(8,128)S(1)} collective-permute-done((f32[3,16,128]{2,1,0:T(8,128)S(1)}, f32[3,16,128]{2,1,0:T(8,128)S(1)}, u32[]{:S(2)}, u32[]{:S(2)}) %collective-permute-start.1) | collective-permute-done | bytes 24608 | tf_op jit(solution)/shard_map/ppermute | solution.py:428
  11.5 0.1 shard_map.65
  11.7 0.4 collective-permute-start.2
  12.1 2.9 %collective-permute-start.3 = (f32[5,16,128]{2,1,0:T(8,128)S(1)}, f32[5,16,128]{2,1,0:T(8,128)S(1)}, u32[]{:S(2)}, u32[]{:S(2)}) collective-permute-start(f32[5,16,128]{2,1,0:T(8,128)S(1)} %get-tuple-element.22), channel_id=1, source_target_pairs={{8,0},{16,8},{24,16},{0,24},{9,1},{17,9},{25,17},{1,25},{10,2},{18... | collective-permute-start | bytes 122888 | tf_op jit(solution)/shard_map/ppermute | solution.py:435
  15.7 0.8 %copy.25.diffusion_ref = f32[16,4]{1,0:T(8,128)S(1)} copy(f32[16,4]{0,1:T(4,128)} %param.9) | data formatting | bytes 512 | tf_op args[3]
  16.4 0.8 %copy.24.courant_ref = f32[16,3]{1,0:T(8,128)S(1)} copy(f32[16,3]{0,1:T(4,128)} %param.8) | data formatting | bytes 384 | tf_op args[2]
  17.2 0.8 %copy.26.reaction_ref = f32[16,16]{1,0:T(8,128)S(1)} copy(f32[16,16]{0,1:T(8,128)} %bitcast.11) | data formatting | bytes 2048 | tf_op jit(solution)/shard_map/reshape | solution.py:419
  17.9 0.8 %copy.27.quadratic_ref = f32[16,4]{1,0:T(8,128)S(1)} copy(f32[16,4]{0,1:T(4,128)} %param.11) | data formatting | bytes 512 | tf_op args[5]
  18.7 0.0 collective-permute-done.4.low_ref
  18.7 0.0 collective-permute-done.5.high_ref
  18.7 0.0 copy-start.1
  18.7 1.0 %copy-done.1 = f32[1,4,16,16,128]{4,3,2,1,0:T(8,128)S(1)} copy-done((f32[1,4,16,16,128]{4,3,2,1,0:T(8,128)S(1)}, f32[1,4,16,16,128]{4,3,2,1,0:T(8,128)}, u32[]{:S(2)}) %copy-start.1) | copy-done | bytes 524312
  19.7 5.2 %shard_map.66 = (f32[4,16,4,16,128]{4,3,2,1,0:T(8,128)S(1)}, f32[13,8,128]{2,1,0:T(8,128)S(1)}) custom-call(f32[1024,128]{1,0:T(8,128)S(1)} %bitcast.8, f32[5,4,16,128]{3,2,1,0:T(8,128)S(1)} %collective-permute-done.4.low_ref, f32[5,4,16,128]{3,2,1,0:T(8,128)S(1)} %collective-permute-done.5.high_ref, s32[1]{0:T(128)S(6)} %copy.34.member_ref, ...), custom_call_target="tpu_custom_call" | custom-call | flops 10000000 | bytes 1048576 | tf_op jit(solution)/shard_map/pallas_call | solution.py:438
  25.0 0.0 collective-permute-done.2.low_ref
  25.0 0.0 collective-permute-done.3.high_ref
  25.0 2.7 %shard_map.67 = (f32[4,16,16,128]{3,2,1,0:T(8,128)S(1)}, f32[32,16]{1,0:T(8,128)S(1)}) custom-call(f32[16,16,128]{2,1,0:T(8,128)S(1)} %get-tuple-element.20.strip_ref, f32[5,16,128]{2,1,0:T(8,128)S(1)} %collective-permute-done.2.low_ref, f32[5,16,128]{2,1,0:T(8,128)S(1)} %collective-permute-done.3.high_ref, f32[13,8,128]{2,1,0:T(8,128)S(1)} %get-tuple-element.25.dots_in_ref, ...), custom_call_target="tpu_custom_call" | custom-call | flops 1000 | bytes 1048576 | tf_op jit(solution)/shard_map/pallas_call | solution.py:445
  27.7 25.1 %all_to_all.11 = f32[32,1,16]{2,1,0:T(1,128)S(1)} all-to-all(f32[32,1,16]{2,1,0:T(1,128)S(1)} %bitcast.10), channel_id=1, replica_groups=mesh['ens'=8,'gy'=4,'gz'=8] {'gy','gz'}, dimensions={0} | all-to-all | bytes 4096 | tf_op jit(solution)/shard_map/all_to_all | solution.py:451
  52.9 2.9 %shard_map.68 = f32[1024,128]{1,0:T(8,128)} custom-call(f32[32,16]{1,0:T(8,128)S(1)} %bitcast.9, s32[1]{0:T(128)S(6)} %copy.34.member_ref, f32[16,4]{1,0:T(8,128)S(1)} %copy.25.diffusion_ref, f32[4,16,4,16,128]{4,3,2,1,0:T(8,128)S(1)} %get-tuple-element.27.basis_ref, f32[4,16,16,128]{3,2,1,0:T(8,128)S(1)} %get-tuple-element.28.strip_ref), custom_call_target="tpu_custom_call" | custom-call | flops 1000 | bytes 1048576 | tf_op jit(solution)/shard_map/pallas_call | solution.py:452
Async XLA Ops:
  0.0 1.0 %copy-start = (f32[1,4,16,16,128]{4,3,2,1,0:T(8,128)S(1)}, f32[1,4,16,16,128]{4,3,2,1,0:T(8,128)}, u32[]{:S(2)}) copy-start(f32[1,4,16,16,128]{4,3,2,1,0:T(8,128)} %param.6) | copy-start | bytes 1572868
  1.5 17.2 %collective-permute-start.4 = (f32[5,4,16,128]{3,2,1,0:T(8,128)S(1)}, f32[5,4,16,128]{3,2,1,0:T(8,128)S(1)}, u32[]{:S(2)}, u32[]{:S(2)}) collective-permute-start(f32[5,4,16,128]{3,2,1,0:T(8,128)S(1)} %get-tuple-element.23), channel_id=1, source_target_pairs={{0,8},{8,16},{16,24},{24,0},{1,9},{9,17},{17,25},{25,1},{2,10},{10... | collective-permute-start | bytes 491528 | tf_op jit(solution)/shard_map/ppermute | solution.py:429
  3.1 15.6 %collective-permute-start.5 = (f32[5,4,16,128]{3,2,1,0:T(8,128)S(1)}, f32[5,4,16,128]{3,2,1,0:T(8,128)S(1)}, u32[]{:S(2)}, u32[]{:S(2)}) collective-permute-start(f32[5,4,16,128]{3,2,1,0:T(8,128)S(1)} %get-tuple-element.24), channel_id=1, source_target_pairs={{8,0},{16,8},{24,16},{0,24},{9,1},{17,9},{25,17},{1,25},{10,2},{18... | collective-permute-start | bytes 491528 | tf_op jit(solution)/shard_map/ppermute | solution.py:430
  4.8 5.0 %collective-permute-start = (f32[3,16,128]{2,1,0:T(8,128)S(1)}, f32[3,16,128]{2,1,0:T(8,128)S(1)}, u32[]{:S(2)}, u32[]{:S(2)}) collective-permute-start(f32[3,16,128]{2,1,0:T(8,128)S(1)} %get-tuple-element.18), channel_id=1, source_target_pairs={{1,2},{2,1},{3,4},{4,3},{5,6},{6,5},{9,10},{10,9},{11,12},{12,11},... | collective-permute-start | bytes 73736 | tf_op jit(solution)/shard_map/ppermute | solution.py:427
  5.4 6.1 %collective-permute-start.1 = (f32[3,16,128]{2,1,0:T(8,128)S(1)}, f32[3,16,128]{2,1,0:T(8,128)S(1)}, u32[]{:S(2)}, u32[]{:S(2)}) collective-permute-start(f32[3,16,128]{2,1,0:T(8,128)S(1)} %get-tuple-element.19), channel_id=1, source_target_pairs={{0,1},{1,0},{2,3},{3,2},{4,5},{5,4},{6,7},{7,6},{8,9},{9,8},{10,11... | collective-permute-start | bytes 73736 | tf_op jit(solution)/shard_map/ppermute | solution.py:428
  11.7 13.3 %collective-permute-start.2 = (f32[5,16,128]{2,1,0:T(8,128)S(1)}, f32[5,16,128]{2,1,0:T(8,128)S(1)}, u32[]{:S(2)}, u32[]{:S(2)}) collective-permute-start(f32[5,16,128]{2,1,0:T(8,128)S(1)} %get-tuple-element.21), channel_id=1, source_target_pairs={{0,8},{8,16},{16,24},{24,0},{1,9},{9,17},{17,25},{25,1},{2,10},{10... | collective-permute-start | bytes 122888 | tf_op jit(solution)/shard_map/ppermute | solution.py:434
  12.1 12.9 %collective-permute-start.3 = (f32[5,16,128]{2,1,0:T(8,128)S(1)}, f32[5,16,128]{2,1,0:T(8,128)S(1)}, u32[]{:S(2)}, u32[]{:S(2)}) collective-permute-start(f32[5,16,128]{2,1,0:T(8,128)S(1)} %get-tuple-element.22), channel_id=1, source_target_pairs={{8,0},{16,8},{24,16},{0,24},{9,1},{17,9},{25,17},{1,25},{10,2},{18... | collective-permute-start | bytes 122888 | tf_op jit(solution)/shard_map/ppermute | solution.py:435
  18.7 1.0 %copy-start.1 = (f32[1,4,16,16,128]{4,3,2,1,0:T(8,128)S(1)}, f32[1,4,16,16,128]{4,3,2,1,0:T(8,128)}, u32[]{:S(2)}) copy-start(f32[1,4,16,16,128]{4,3,2,1,0:T(8,128)} %param.6) | copy-start | bytes 1572868

commit v2 on v1

--- a/solution.py
+++ b/solution.py
@@ -1,11 +1,10 @@
-import functools
-
 import jax
 import jax.numpy as jnp
 from jax import lax
 from jax.experimental import pallas as pl
 from jax.experimental.pallas import tpu as pltpu
 from jax.sharding import PartitionSpec as P
+
 
 SPECIES = 4
 X = 16
@@ -20,7 +19,6 @@
 
 F32 = jnp.float32
 VMEM = pltpu.VMEM
-SMEM = pltpu.SMEM
 
 
 def struct(*shape):
@@ -36,11 +34,12 @@
     return pltpu.roll(v, amount, 1) if amount else v
 
 
-def own(state_ref, s, y):
-    return state_ref[pl.ds(s * X * Y + y, X, stride=Y), :]
-
-
 def over_rows(count, at_once, body, carry=None):
+    if at_once >= count:
+        for row in range(count):
+            carry = body(row, carry)
+        return carry
+
     def step(i, c):
         for k in range(at_once):
             c = body(i * at_once + k, c)
@@ -53,23 +52,28 @@
     return carry
 
 
-def pack_kernel(state_ref, top_ref, bottom_ref, strip_ref, far_ref, near_ref):
+def pack_kernel(state_ref, own_ref, top_ref, bottom_ref, strip_ref, far_ref, near_ref, held, sems):
     lane = lanes()
     odd = lax.axis_index("gz") % 2 == 1
     place = lane % 32
-    for y in range(Y):
-        total = jnp.zeros((X, Z), F32)
-        for s in range(SPECIES):
-            v = own(state_ref, s, y)
+    copies = [pltpu.make_async_copy(state_ref.at[s], held.at[s], sems.at[s]) for s in range(SPECIES)]
+    for copy in copies:
+        copy.start()
+    for s in range(SPECIES):
+        copies[s].wait()
+        for y in range(Y):
+            v = held[s, pl.ds(y, X, stride=Y), :]
+            own_ref[y, s] = v
             if y < HALO:
                 top_ref[y, s] = v
             if y >= Y - HALO:
                 bottom_ref[y - (Y - HALO), s] = v
+            total = strip_ref[y] if s else jnp.zeros((X, Z), F32)
             low = shift(v, 32 * s + HALO)
             high = shift(v, 32 * s + 16 - (Z - 11))
             total = jnp.where((lane >= 32 * s + HALO) & (lane < 32 * s + 16), low, total)
             total = jnp.where((lane >= 32 * s + 16) & (lane < 32 * s + 27), high, total)
-        strip_ref[y] = total
+            strip_ref[y] = total
     for g in range(PACKS):
         lows = jnp.zeros((X, Z), F32)
         highs = jnp.zeros((X, Z), F32)
@@ -117,17 +121,66 @@
 
 
 def row_flag(row, before, low, high):
+    if isinstance(row, int):
+        return low if row < before else high if row >= before + Y else 1.0
     flag = jnp.where(row < before, low, 1.0)
     return jnp.where(row >= before + Y, high, flag)
 
 
-def one_row(value):
-    return jnp.full((1, Z), value, F32)
-
-
-def largest(diffusion_ref, member):
-    d = [diffusion_ref[member, s] for s in range(SPECIES)]
-    return d, jnp.maximum(jnp.maximum(d[0], d[1]), jnp.maximum(d[2], d[3]))
+PLUS, MINUS, LINEAR, QUAD, SCALE, TURNED, STRIP_QUAD, STRIP_SCALE, RANGE = 0, 3, 6, 22, 26, 30, 34, 35, 36
+COEFFICIENTS = 40
+
+
+def coefficient_kernel(member_ref, courant_ref, diffusion_ref, reaction_ref, quadratic_ref, out_ref):
+    sets = courant_ref.shape[-1]
+    hot = lax.broadcasted_iota(jnp.int32, (1, sets), 1) == member_ref[...]
+
+    def picked(table):
+        return jnp.sum(jnp.where(hot, table, 0.0), axis=1, keepdims=True)
+
+    def put(row, value):
+        out_ref[row : row + 1, :] = jnp.broadcast_to(value, (1, Z))
+
+    lane = lax.broadcasted_iota(jnp.int32, (1, Z), 1)
+
+    def by_species(values):
+        out = jnp.broadcast_to(values[3], (1, Z))
+        for s in (2, 1, 0):
+            out = jnp.where(lane < 32 * (s + 1), values[s], out)
+        return out
+
+    courant = picked(courant_ref[...])
+    plus, minus = jnp.maximum(courant, 0.0), jnp.minimum(courant, 0.0)
+    kept = jnp.ones((1, 1), F32)
+    for d in range(3):
+        put(PLUS + d, plus[d : d + 1])
+        put(MINUS + d, minus[d : d + 1])
+        kept = kept - (plus[d : d + 1] - minus[d : d + 1])
+    linear = []
+    for k in range(SPECIES):
+        rates = picked(reaction_ref[k])
+        linear.append([rates[l : l + 1] for l in range(SPECIES)])
+        linear[k][k] = linear[k][k] + kept
+        for l in range(SPECIES):
+            put(LINEAR + SPECIES * k + l, linear[k][l])
+    for t in range(SPECIES):
+        put(TURNED + t, by_species([linear[k][(k - t) % SPECIES] for k in range(SPECIES)]))
+    rates = picked(quadratic_ref[...])
+    quad = [rates[k : k + 1] for k in range(SPECIES)]
+    d = picked(diffusion_ref[...])
+    d = [d[k : k + 1] for k in range(SPECIES)]
+    reach = 6.0 * jnp.maximum(jnp.maximum(d[0], d[1]), jnp.maximum(d[2], d[3]))
+    scale = [v / reach for v in d]
+    for k in range(SPECIES):
+        put(QUAD + k, quad[k])
+        put(SCALE + k, scale[k])
+    put(STRIP_QUAD, by_species(quad))
+    put(STRIP_SCALE, by_species(scale))
+    put(RANGE, reach)
+
+
+def spread(table_ref, row):
+    return jnp.broadcast_to(table_ref[row : row + 1, :], (X, Z))
 
 
 def dot_terms(b):
@@ -147,11 +200,7 @@
     return 2.0 * (image - v) - before
 
 
-def main_kernel(
-    state_ref, low_ref, high_ref, member_ref, courant_ref, diffusion_ref, reaction_ref, quadratic_ref,
-    basis_ref, dots_ref, wide, b0, b1, b2, b3,
-):
-    member = member_ref[0]
+def main_kernel(own_ref, low_ref, high_ref, table_ref, basis_ref, dots_ref, wide, b0, b1, b2, b3):
     low, high = in_grid()
     for r in range(HALO):
         for s in range(SPECIES):
@@ -159,16 +208,12 @@
             wide[HALO + Y + r, s] = high_ref[r, s] * high
     for y in range(Y):
         for s in range(SPECIES):
-            wide[HALO + y, s] = own(state_ref, s, y)
-
-    courant = [courant_ref[member, d] for d in range(3)]
-    plus = [jnp.maximum(c, 0.0) for c in courant]
-    minus = [jnp.minimum(c, 0.0) for c in courant]
-    kept = 1.0 - (plus[0] - minus[0]) - (plus[1] - minus[1]) - (plus[2] - minus[2])
-    linear = [[reaction_ref[member, 4 * k + l] for l in range(SPECIES)] for k in range(SPECIES)]
-    for k in range(SPECIES):
-        linear[k][k] = linear[k][k] + kept
-    quad = [quadratic_ref[member, k] for k in range(SPECIES)]
+            wide[HALO + y, s] = own_ref[y, s]
+
+    plus = [spread(table_ref, PLUS + d) for d in range(3)]
+    minus = [spread(table_ref, MINUS + d) for d in range(3)]
+    linear = [[spread(table_ref, LINEAR + SPECIES * k + l) for l in range(SPECIES)] for k in range(SPECIES)]
+    quad = [spread(table_ref, QUAD + k) for k in range(SPECIES)]
 
     def source_row(row, _):
         flag = row_flag(row, HALO - 1, low, high)
@@ -187,9 +232,7 @@
 
     over_rows(Y + 8, 4, source_row)
 
-    d, most = largest(diffusion_ref, member)
-    scale = [one_row(d[s]) / one_row(6.0 * most) for s in range(SPECIES)]
-
+    scale = [spread(table_ref, SCALE + s) for s in range(SPECIES)]
     buffers = [b0, b1, b2, b3]
 
     def image_of(ref, row, s):
@@ -229,10 +272,8 @@
 
 
 def strip_kernel(
-    strip_ref, low_ref, high_ref, dots_in_ref, member_ref, courant_ref, diffusion_ref, reaction_ref, quadratic_ref,
-    basis_ref, total_ref, wide, b0, b1, b2, b3,
+    strip_ref, low_ref, high_ref, dots_in_ref, table_ref, basis_ref, total_ref, wide, b0, b1, b2, b3
 ):
-    member = member_ref[0]
     low, high = in_grid()
     for r in range(HALO):
         wide[r] = low_ref[r] * low
@@ -240,28 +281,15 @@
     for y in range(Y):
         wide[HALO + y] = strip_ref[y]
 
-    lane = lax.broadcasted_iota(jnp.int32, (1, Z), 1)
+    lane = lanes()
     place = lane % 32
-
-    def by_species(values):
-        out = one_row(values[3])
-        for s in (2, 1, 0):
-            out = jnp.where(lane < 32 * (s + 1), values[s], out)
-        return out
-
     first = jnp.where(lax.axis_index("gz") > 0, 1.0, 0.0).astype(F32)
     last = jnp.where(lax.axis_index("gz") < lax.axis_size("gz") - 1, 1.0, 0.0).astype(F32)
-    inside = jnp.where(place < HALO, first, jnp.where(place >= 27, last, one_row(1.0)))
-
-    courant = [courant_ref[member, d] for d in range(3)]
-    plus = [jnp.maximum(c, 0.0) for c in courant]
-    minus = [jnp.minimum(c, 0.0) for c in courant]
-    kept = 1.0 - (plus[0] - minus[0]) - (plus[1] - minus[1]) - (plus[2] - minus[2])
-    linear = [
-        by_species([reaction_ref[member, 4 * k + (k - t) % SPECIES] for k in range(SPECIES)]) for t in range(SPECIES)
-    ]
-    linear[0] = linear[0] + kept
-    quad = by_species([quadratic_ref[member, k] for k in range(SPECIES)])
+    inside = jnp.where(place < HALO, first, jnp.where(place >= 27, last, 1.0))
+    plus = [spread(table_ref, PLUS + d) for d in range(3)]
+    minus = [spread(table_ref, MINUS + d) for d in range(3)]
+    linear = [spread(table_ref, TURNED + t) for t in range(SPECIES)]
+    quad = spread(table_ref, STRIP_QUAD)
 
     def source_row(row, _):
         flag = row_flag(row, HALO - 1, low, high)
@@ -281,10 +309,9 @@
         b0[row] = (out + quad * coupled) * (flag * inside)
         return _
 
-    over_rows(Y + 8, 12, source_row)
-
-    d, most = largest(diffusion_ref, member)
-    scale = by_species(d) / one_row(6.0 * most)
+    over_rows(Y + 8, Y + 8, source_row)
+
+    scale = spread(table_ref, STRIP_SCALE)
     buffers = [b0, b1, b2, b3]
 
     def image_of(ref, row):
@@ -302,7 +329,7 @@
             buffers[k][row] = level_value(k, image, v, None) * (flag * inside)
             return _
 
-        over_rows(Y + 2 * before, 11 if k == 1 else 10 if k == 2 else 9, level_row)
+        over_rows(Y + 2 * before, Y + 2 * before, level_row)
 
     def last_row(row, sums):
         image, v = image_of(b3, row)
@@ -312,10 +339,11 @@
         b.append(level_value(4, image, v, b[2]))
         return tuple(t + p for t, p in zip(sums, dot_terms(b)))
 
-    sums = over_rows(Y, 8, last_row, tuple(jnp.zeros((8, Z), F32) for _ in range(DOTS)))
+    sums = over_rows(Y, Y, last_row, tuple(jnp.zeros((8, Z), F32) for _ in range(DOTS)))
+    place = place[:8]
     edge = ((place >= HALO) & (place < 2 * HALO)) | ((place >= 22) & (place < 27))
     slot = lax.broadcasted_iota(jnp.int32, (8, SLOTS), 1)
-    total = jnp.zeros((8, SLOTS), F32)
+    total = jnp.broadcast_to(table_ref[RANGE : RANGE + 1, :SLOTS], (8, SLOTS))
     for k in range(DOTS):
         both = jnp.where(edge, sums[k], 0.0) + dots_in_ref[k]
         one = jnp.sum(jnp.sum(both, axis=0, keepdims=True), axis=1, keepdims=True)
@@ -369,10 +397,9 @@
     return y
 
 
-def combine_kernel(sums_ref, member_ref, diffusion_ref, basis_ref, strip_ref, out_ref):
+def combine_kernel(sums_ref, basis_ref, strip_ref, out_ref, held, strips, sems):
     total = jnp.sum(sums_ref[...], axis=0, keepdims=True)
-    p = [total[:, k : k + 1] for k in range(DOTS)]
-    h00, h01, h03, h04, h11, h12, h13, h14, h22, h23, h33, h34, h44 = p
+    h00, h01, h03, h04, h11, h12, h13, h14, h22, h23, h33, h34, h44 = (total[:, k : k + 1] for k in range(DOTS))
     h = [
         [h00, h01, h11, h03, h04],
         [None, h11, h12, h13, h14],
@@ -380,28 +407,34 @@
         [None, None, None, h33, h34],
         [None, None, None, None, h44],
     ]
-    _, most = largest(diffusion_ref, member_ref[0])
-    y = [jnp.broadcast_to(c, (X, Z)) for c in least_squares(h, 6.0 * most)]
+    y = [jnp.broadcast_to(c, (X, Z)) for c in least_squares(h, sums_ref[0:1, DOTS : DOTS + 1])]
     lane = lanes()
     for row in range(Y):
         strip = y[0] * strip_ref[0, row]
         for k in (1, 2, 3):
             strip = strip + y[k] * strip_ref[k, row]
-        for s in range(SPECIES):
+        strips[row] = strip
+    copies = [pltpu.make_async_copy(held.at[s], out_ref.at[s], sems.at[s]) for s in range(SPECIES)]
+    for s in range(SPECIES):
+        for row in range(Y):
             v = y[0] * basis_ref[0, row, s]
             for k in (1, 2, 3):
                 v = v + y[k] * basis_ref[k, row, s]
+            strip = strips[row]
             v = jnp.where(lane < HALO, shift(strip, -(32 * s + HALO)), v)
             v = jnp.where(lane >= Z - HALO, shift(strip, Z - HALO - (32 * s + 22)), v)
-            out_ref[pl.ds(s * X * Y + row, X, stride=Y), :] = v
-
-
-def call(kernel, outs, spaces, scratch=(), flops=1000):
+            held[s, pl.ds(row, X, stride=Y), :] = v
+        copies[s].start()
+    for copy in copies:
+        copy.wait()
+
+
+def call(kernel, outs, spaces, scratch=(), flops=1000, out_space=VMEM):
     return pl.pallas_call(
         kernel,
         out_shape=outs,
         in_specs=[pl.BlockSpec(memory_space=m) for m in spaces],
-        out_specs=jax.tree.map(lambda _: pl.BlockSpec(memory_space=VMEM), outs),
+        out_specs=jax.tree.map(lambda _: pl.BlockSpec(memory_space=out_space), outs),
         scratch_shapes=list(scratch),
         cost_estimate=pl.CostEstimate(flops=flops, bytes_accessed=1 << 20, transcendentals=0),
         compiler_params=pltpu.CompilerParams(vmem_limit_bytes=24 << 20),
@@ -415,43 +448,51 @@
     far, near = [], []
     for i in range(gz - 1):
         (far if i % 2 else near).extend([(i, i + 1), (i + 1, i)])
-    flat = state.reshape(SPECIES * X * Y, Z)
-    tables = (courant_table, diffusion_table, reaction_table.reshape(-1, SPECIES * SPECIES), quadratic_table)
+    flat = state.reshape(SPECIES, X * Y, Z)
 
     edge = struct(HALO, SPECIES, X, Z)
     strip_edge = struct(HALO, X, Z)
     pack = struct(PACKS, X, Z)
-    top, bottom, strip, to_far, to_near = call(
-        pack_kernel, (edge, edge, struct(Y, X, Z), pack, pack), [VMEM]
+    own, top, bottom, strip, to_far, to_near = call(
+        pack_kernel,
+        (struct(Y, SPECIES, X, Z), edge, edge, struct(Y, X, Z), pack, pack),
+        [pltpu.HBM],
+        [VMEM((SPECIES, X * Y, Z), F32), pltpu.SemaphoreType.DMA((SPECIES,))],
     )(flat)
     from_far = lax.ppermute(to_far, "gz", far)
     from_near = lax.ppermute(to_near, "gz", near)
     low = lax.ppermute(bottom, "gy", up)
     high = lax.ppermute(top, "gy", down)
+    table = call(coefficient_kernel, struct(COEFFICIENTS, Z), [VMEM] * 5)(
+        member_set.reshape(1, 1), courant_table.T, diffusion_table.T, reaction_table.transpose(1, 2, 0), quadratic_table.T
+    )
+    wide = (SPECIES, X, Z)
+    basis, dots = call(
+        main_kernel,
+        (struct(4, Y, *wide), struct(DOTS, 8, Z)),
+        [VMEM] * 4,
+        [VMEM((n, *wide), F32) for n in (ROWS, Y + 8, Y + 6, Y + 4, Y + 2)],
+        flops=10_000_000,
+    )(own, low, high, table)
     strip, strip_top, strip_bottom = call(
         unpack_kernel, (struct(Y, X, Z), strip_edge, strip_edge), [VMEM] * 3
     )(strip, from_far, from_near)
     strip_low = lax.ppermute(strip_bottom, "gy", up)
     strip_high = lax.ppermute(strip_top, "gy", down)
-
-    wide = (SPECIES, X, Z)
-    basis, dots = call(
-        main_kernel,
-        (struct(4, Y, *wide), struct(DOTS, 8, Z)),
-        [VMEM] * 3 + [SMEM] * 5,
-        [VMEM((n, *wide), F32) for n in (ROWS, Y + 8, Y + 6, Y + 4, Y + 2)],
-        flops=10_000_000,
-    )(flat, low, high, member_set, *tables)
     strip_basis, total = call(
         strip_kernel,
         (struct(4, Y, X, Z), struct(gy * gz, SLOTS)),
-        [VMEM] * 4 + [SMEM] * 5,
+        [VMEM] * 5,
         [VMEM((n, X, Z), F32) for n in (ROWS, Y + 8, Y + 6, Y + 4, Y + 2)],
-    )(strip, strip_low, strip_high, dots, member_set, *tables)
+    )(strip, strip_low, strip_high, dots, table)
     sums = lax.all_to_all(total, ("gy", "gz"), split_axis=0, concat_axis=0, tiled=True)
     out = call(
-        combine_kernel, struct(SPECIES * X * Y, Z), [VMEM, SMEM, SMEM, VMEM, VMEM]
-    )(sums, member_set, diffusion_table, basis, strip_basis)
+        combine_kernel,
+        struct(SPECIES, X * Y, Z),
+        [VMEM] * 3,
+        [VMEM((SPECIES, X * Y, Z), F32), VMEM((Y, X, Z), F32), pltpu.SemaphoreType.DMA((SPECIES,))],
+        out_space=pltpu.HBM,
+    )(sums, basis, strip_basis)
     return out.reshape(state.shape)
 
 

time: 56.1 us -> 54.4 us (0.970)
  local copies, waits for them, and re-layouts: 5.12 us -> 3.78 us
    pallas_call x3 -> x4, Pallas kernels: 8.52 us -> 7.74 us  [the longest x1 4.06 us: shards(): call(main_kernel, (struct(4, Y, *wide), struct(DOTS, 8, Z)), [VMEM] * 4,...]
    reshape x1 -> x0, local copies, waits for them, and re-layouts: 0.77 us -> none  [shards(): reaction_table.reshape(-1, SPECIES * SPECIES)]
    unnamed x7 -> x10, local copies, waits for them, and re-layouts: 4.36 us -> 3.78 us
  transfers between devices with their start and end apart: 6 -> 6, of which waited for: 1 -> 1; matrix products, arithmetic and copies ran while one was open for 5% -> 0% of each run, Pallas kernels for 10% -> 8%
where the time goes in v2:
time: 54.4 us; the launch traced here: 54.1 us
  blocking collectives  25.1 us (46%)
  starting transfers between devices  11.6 us (21%)
  Pallas kernels  11 us (20%)
  local copies, waits for them, and re-layouts  3.78 us (7%)
  waiting for transfers between devices  1.82 us (3%)
  between operations  0.73 us (1%)
    all_to_all x1, blocking collectives, shards(): lax.all_to_all(total, ('gy', 'gz'), split_axis=0, concat_axis=0, tiled=True)  25.1 us
    ppermute x1, starting transfers between devices, shards(): from_near = lax.ppermute(to_near, 'gz', near)  4.31 us
    pallas_call x1, Pallas kernels, shards(): call(main_kernel, (struct(4, Y, *wide), struct(DOTS, 8, Z)), [VMEM] * 4,...  4.06 us
    unnamed x10, local copies, waits for them, and re-layouts  3.78 us
    pallas_call x1, Pallas kernels, shards(): call(strip_kernel, (struct(4, Y, X, Z), struct(gy * gz, SLOTS)), [VMEM] *...  3.16 us
    ppermute x1, starting transfers between devices, shards(): strip_high = lax.ppermute(strip_top, 'gy', down)  2.87 us
    pallas_call x1, Pallas kernels, shards(): call(combine_kernel, struct(SPECIES, X * Y, Z), [VMEM] * 3, [VMEM((SPECIE...  2.1 us
    ppermute x1, waiting for transfers between devices, shards(): from_near = lax.ppermute(to_near, 'gz', near)  1.8 us
  transfers between devices with their start and end apart: 6, of which 1 were waited for; matrix products, arithmetic and copies ran while one was open for 0% of the time, Pallas kernels for 8%

profile of v2, /device:TPU:32, one launch (start us, length us, event | category | flops | bytes accessed | tf_op | source)
XLA Modules:
  0.0 54.1 jit_solution(15520194943441942509)
XLA Ops:
  0.0 0.0 copy-start
  0.0 1.0 %copy-done = f32[1,4,16,16,128]{4,3,2,1,0:T(8,128)S(1)} copy-done((f32[1,4,16,16,128]{4,3,2,1,0:T(8,128)S(1)}, f32[1,4,16,16,128]{4,3,2,1,0:T(8,128)}, u32[]{:S(2)}) %copy-start) | copy-done | bytes 524312
  1.0 1.3 %shard_map.64 = (f32[16,4,16,128]{3,2,1,0:T(8,128)S(1)}, f32[5,4,16,128]{3,2,1,0:T(8,128)S(1)}, f32[5,4,16,128]{3,2,1,0:T(8,128)S(1)}, f32[16,16,128]{2,1,0:T(8,...) custom-call(f32[4,256,128]{2,1,0:T(8,128)S(1)} %bitcast.12), custom_call_target="tpu_custom_call" | custom-call | flops 1000 | bytes 1048576 | tf_op jit(solution)/shard_map/pallas_call | solution.py:456
  2.4 1.7 %collective-permute-start.4 = (f32[5,4,16,128]{3,2,1,0:T(8,128)S(1)}, f32[5,4,16,128]{3,2,1,0:T(8,128)S(1)}, u32[]{:S(2)}, u32[]{:S(2)}) collective-permute-start(f32[5,4,16,128]{3,2,1,0:T(8,128)S(1)} %get-tuple-element.25), channel_id=1, source_target_pairs={{0,8},{8,16},{16,24},{24,0},{1,9},{9,17},{17,25},{25,1},{2,10},{10... | collective-permute-start | bytes 491528 | tf_op jit(solution)/shard_map/ppermute | solution.py:464
  4.0 1.7 %collective-permute-start.5 = (f32[5,4,16,128]{3,2,1,0:T(8,128)S(1)}, f32[5,4,16,128]{3,2,1,0:T(8,128)S(1)}, u32[]{:S(2)}, u32[]{:S(2)}) collective-permute-start(f32[5,4,16,128]{3,2,1,0:T(8,128)S(1)} %get-tuple-element.26), channel_id=1, source_target_pairs={{8,0},{16,8},{24,16},{0,24},{9,1},{17,9},{25,17},{1,25},{10,2},{18... | collective-permute-start | bytes 491528 | tf_op jit(solution)/shard_map/ppermute | solution.py:465
  5.7 0.7 %collective-permute-start = (f32[3,16,128]{2,1,0:T(8,128)S(1)}, f32[3,16,128]{2,1,0:T(8,128)S(1)}, u32[]{:S(2)}, u32[]{:S(2)}) collective-permute-start(f32[3,16,128]{2,1,0:T(8,128)S(1)} %get-tuple-element.19), channel_id=1, source_target_pairs={{1,2},{2,1},{3,4},{4,3},{5,6},{6,5},{9,10},{10,9},{11,12},{12,11},... | collective-permute-start | bytes 73736 | tf_op jit(solution)/shard_map/ppermute | solution.py:462
  6.3 4.3 %collective-permute-start.1 = (f32[3,16,128]{2,1,0:T(8,128)S(1)}, f32[3,16,128]{2,1,0:T(8,128)S(1)}, u32[]{:S(2)}, u32[]{:S(2)}) collective-permute-start(f32[3,16,128]{2,1,0:T(8,128)S(1)} %get-tuple-element.20), channel_id=1, source_target_pairs={{0,1},{1,0},{2,3},{3,2},{4,5},{5,4},{6,7},{7,6},{8,9},{9,8},{10,11... | collective-permute-start | bytes 73736 | tf_op jit(solution)/shard_map/ppermute | solution.py:463
  10.7 0.0 collective-permute-done.far_ref
  10.7 1.8 %collective-permute-done.1.near_ref = f32[3,16,128]{2,1,0:T(8,128)S(1)} collective-permute-done((f32[3,16,128]{2,1,0:T(8,128)S(1)}, f32[3,16,128]{2,1,0:T(8,128)S(1)}, u32[]{:S(2)}, u32[]{:S(2)}) %collective-permute-start.1) | collective-permute-done | bytes 24608 | tf_op jit(solution)/shard_map/ppermute | solution.py:463
  12.5 0.1 shard_map.65
  12.6 0.4 collective-permute-start.2
  13.1 2.9 %collective-permute-start.3 = (f32[5,16,128]{2,1,0:T(8,128)S(1)}, f32[5,16,128]{2,1,0:T(8,128)S(1)}, u32[]{:S(2)}, u32[]{:S(2)}) collective-permute-start(f32[5,16,128]{2,1,0:T(8,128)S(1)} %get-tuple-element.23), channel_id=1, source_target_pairs={{8,0},{16,8},{24,16},{0,24},{9,1},{17,9},{25,17},{1,25},{10,2},{18... | collective-permute-start | bytes 122888 | tf_op jit(solution)/shard_map/ppermute | solution.py:481
  16.6 0.0 copy-start.1
  16.6 0.7 %copy-done.1 = f32[16,4,4]{0,2,1:T(4,128)S(1)} copy-done((f32[16,4,4]{0,2,1:T(4,128)S(1)}, f32[16,4,4]{0,2,1:T(4,128)}, u32[]{:S(2)}) %copy-start.1) | copy-done | bytes 1048
  17.3 0.0 copy-start.2
  17.3 0.7 %copy-done.2 = f32[16,3]{0,1:T(4,128)S(1)} copy-done((f32[16,3]{0,1:T(4,128)S(1)}, f32[16,3]{0,1:T(4,128)}, u32[]{:S(2)}) %copy-start.2) | copy-done | bytes 216
  18.0 0.0 copy-start.3
  18.0 0.7 %copy-done.3 = f32[16,4]{0,1:T(4,128)S(1)} copy-done((f32[16,4]{0,1:T(4,128)S(1)}, f32[16,4]{0,1:T(4,128)}, u32[]{:S(2)}) %copy-start.3) | copy-done | bytes 280
  18.6 0.0 copy-start.4
  18.6 0.7 %copy-done.4 = f32[16,4]{0,1:T(4,128)S(1)} copy-done((f32[16,4]{0,1:T(4,128)S(1)}, f32[16,4]{0,1:T(4,128)}, u32[]{:S(2)}) %copy-start.4) | copy-done | bytes 280
  19.3 0.3 shard_map.66.table_ref
  19.6 0.0 collective-permute-done.4.low_ref
  19.6 0.0 collective-permute-done.5.high_ref
  19.6 4.1 %shard_map.67 = (f32[4,16,4,16,128]{4,3,2,1,0:T(8,128)S(1)}, f32[13,8,128]{2,1,0:T(8,128)S(1)}) custom-call(f32[16,4,16,128]{3,2,1,0:T(8,128)S(1)} %get-tuple-element.24.own_ref, f32[5,4,16,128]{3,2,1,0:T(8,128)S(1)} %collective-permute-done.4.low_ref, f32[5,4,16,128]{3,2,1,0:T(8,128)S(1)} %collective-permute-done.5.high_ref, f32[40,128]{1,0:T(8,128)S(1)} %shard_map.66.table_ref), custom_call_target="tpu_custom_call" | custom-call | flops 10000000 | bytes 1048576 | tf_op jit(solution)/shard_map/pallas_call | solution.py:470
  23.7 0.0 collective-permute-done.2.low_ref
  23.7 0.0 collective-permute-done.3.high_ref
  23.7 3.2 %shard_map.68 = (f32[4,16,16,128]{3,2,1,0:T(8,128)S(1)}, f32[32,16]{1,0:T(8,128)S(1)}) custom-call(f32[16,16,128]{2,1,0:T(8,128)S(1)} %get-tuple-element.21.strip_ref, f32[5,16,128]{2,1,0:T(8,128)S(1)} %collective-permute-done.2.low_ref, f32[5,16,128]{2,1,0:T(8,128)S(1)} %collective-permute-done.3.high_ref, f32[13,8,128]{2,1,0:T(8,128)S(1)} %get-tuple-element.27.dots_in_ref, ...), custom_call_target="tpu_custom_call" | custom-call | flops 1000 | bytes 1048576 | tf_op jit(solution)/shard_map/pallas_call | solution.py:482
  26.8 25.1 %all_to_all.11 = f32[32,1,16]{2,1,0:T(1,128)S(1)} all-to-all(f32[32,1,16]{2,1,0:T(1,128)S(1)} %bitcast.14), channel_id=1, replica_groups=mesh['ens'=8,'gy'=4,'gz'=8] {'gy','gz'}, dimensions={0} | all-to-all | bytes 4096 | tf_op jit(solution)/shard_map/all_to_all | solution.py:488
  52.0 2.1 %shard_map.69 = f32[4,256,128]{2,1,0:T(8,128)} custom-call(f32[32,16]{1,0:T(8,128)S(1)} %bitcast.13, f32[4,16,4,16,128]{4,3,2,1,0:T(8,128)S(1)} %get-tuple-element.29.basis_ref, f32[4,16,16,128]{3,2,1,0:T(8,128)S(1)} %get-tuple-element.30.strip_ref), custom_call_target="tpu_custom_call" | custom-call | flops 1000 | bytes 1048576 | tf_op jit(solution)/shard_map/pallas_call | solution.py:489
Async XLA Ops:
  0.0 1.0 %copy-start = (f32[1,4,16,16,128]{4,3,2,1,0:T(8,128)S(1)}, f32[1,4,16,16,128]{4,3,2,1,0:T(8,128)}, u32[]{:S(2)}) copy-start(f32[1,4,16,16,128]{4,3,2,1,0:T(8,128)} %param.6) | copy-start | bytes 1572868
  2.4 17.2 %collective-permute-start.4 = (f32[5,4,16,128]{3,2,1,0:T(8,128)S(1)}, f32[5,4,16,128]{3,2,1,0:T(8,128)S(1)}, u32[]{:S(2)}, u32[]{:S(2)}) collective-permute-start(f32[5,4,16,128]{3,2,1,0:T(8,128)S(1)} %get-tuple-element.25), channel_id=1, source_target_pairs={{0,8},{8,16},{16,24},{24,0},{1,9},{9,17},{17,25},{25,1},{2,10},{10... | collective-permute-start | bytes 491528 | tf_op jit(solution)/shard_map/ppermute | solution.py:464
  4.0 15.6 %collective-permute-start.5 = (f32[5,4,16,128]{3,2,1,0:T(8,128)S(1)}, f32[5,4,16,128]{3,2,1,0:T(8,128)S(1)}, u32[]{:S(2)}, u32[]{:S(2)}) collective-permute-start(f32[5,4,16,128]{3,2,1,0:T(8,128)S(1)} %get-tuple-element.26), channel_id=1, source_target_pairs={{8,0},{16,8},{24,16},{0,24},{9,1},{17,9},{25,17},{1,25},{10,2},{18... | collective-permute-start | bytes 491528 | tf_op jit(solution)/shard_map/ppermute | solution.py:465
  5.7 5.0 %collective-permute-start = (f32[3,16,128]{2,1,0:T(8,128)S(1)}, f32[3,16,128]{2,1,0:T(8,128)S(1)}, u32[]{:S(2)}, u32[]{:S(2)}) collective-permute-start(f32[3,16,128]{2,1,0:T(8,128)S(1)} %get-tuple-element.19), channel_id=1, source_target_pairs={{1,2},{2,1},{3,4},{4,3},{5,6},{6,5},{9,10},{10,9},{11,12},{12,11},... | collective-permute-start | bytes 73736 | tf_op jit(solution)/shard_map/ppermute | solution.py:462
  6.3 6.1 %collective-permute-start.1 = (f32[3,16,128]{2,1,0:T(8,128)S(1)}, f32[3,16,128]{2,1,0:T(8,128)S(1)}, u32[]{:S(2)}, u32[]{:S(2)}) collective-permute-start(f32[3,16,128]{2,1,0:T(8,128)S(1)} %get-tuple-element.20), channel_id=1, source_target_pairs={{0,1},{1,0},{2,3},{3,2},{4,5},{5,4},{6,7},{7,6},{8,9},{9,8},{10,11... | collective-permute-start | bytes 73736 | tf_op jit(solution)/shard_map/ppermute | solution.py:463
  12.6 11.1 %collective-permute-start.2 = (f32[5,16,128]{2,1,0:T(8,128)S(1)}, f32[5,16,128]{2,1,0:T(8,128)S(1)}, u32[]{:S(2)}, u32[]{:S(2)}) collective-permute-start(f32[5,16,128]{2,1,0:T(8,128)S(1)} %get-tuple-element.22), channel_id=1, source_target_pairs={{0,8},{8,16},{16,24},{24,0},{1,9},{9,17},{17,25},{25,1},{2,10},{10... | collective-permute-start | bytes 122888 | tf_op jit(solution)/shard_map/ppermute | solution.py:480
  13.1 10.6 %collective-permute-start.3 = (f32[5,16,128]{2,1,0:T(8,128)S(1)}, f32[5,16,128]{2,1,0:T(8,128)S(1)}, u32[]{:S(2)}, u32[]{:S(2)}) collective-permute-start(f32[5,16,128]{2,1,0:T(8,128)S(1)} %get-tuple-element.23), channel_id=1, source_target_pairs={{8,0},{16,8},{24,16},{0,24},{9,1},{17,9},{25,17},{1,25},{10,2},{18... | collective-permute-start | bytes 122888 | tf_op jit(solution)/shard_map/ppermute | solution.py:481
  16.6 0.7 %copy-start.1 = (f32[16,4,4]{0,2,1:T(4,128)S(1)}, f32[16,4,4]{0,2,1:T(4,128)}, u32[]{:S(2)}) copy-start(f32[16,4,4]{0,2,1:T(4,128)} %param.10) | copy-start | bytes 3076
  17.3 0.7 %copy-start.2 = (f32[16,3]{0,1:T(4,128)S(1)}, f32[16,3]{0,1:T(4,128)}, u32[]{:S(2)}) copy-start(f32[16,3]{0,1:T(4,128)} %param.8) | copy-start | bytes 580
  18.0 0.7 %copy-start.3 = (f32[16,4]{0,1:T(4,128)S(1)}, f32[16,4]{0,1:T(4,128)}, u32[]{:S(2)}) copy-start(f32[16,4]{0,1:T(4,128)} %param.9) | copy-start | bytes 772
  18.6 0.7 %copy-start.4 = (f32[16,4]{0,1:T(4,128)S(1)}, f32[16,4]{0,1:T(4,128)}, u32[]{:S(2)}) copy-start(f32[16,4]{0,1:T(4,128)} %param.11) | copy-start | bytes 772

commit v3 on v2

--- a/solution.py
+++ b/solution.py
@@ -16,9 +16,12 @@
 ROWS = Y + 2 * HALO
 DOTS = 13
 SLOTS = 16
+MAIN_SOURCE, MAIN_LEVEL, MAIN_DOT = 8, (11, 10, 9, 8), 4
+STRIP_SOURCE, STRIP_LEVEL, STRIP_DOT = 12, (11, 10, 9, 8), 4
 
 F32 = jnp.float32
 VMEM = pltpu.VMEM
+SMEM = pltpu.SMEM
 
 
 def struct(*shape):
@@ -50,41 +53,6 @@
     for row in range(whole * at_once, count):
         carry = body(row, carry)
     return carry
-
-
-def pack_kernel(state_ref, own_ref, top_ref, bottom_ref, strip_ref, far_ref, near_ref, held, sems):
-    lane = lanes()
-    odd = lax.axis_index("gz") % 2 == 1
-    place = lane % 32
-    copies = [pltpu.make_async_copy(state_ref.at[s], held.at[s], sems.at[s]) for s in range(SPECIES)]
-    for copy in copies:
-        copy.start()
-    for s in range(SPECIES):
-        copies[s].wait()
-        for y in range(Y):
-            v = held[s, pl.ds(y, X, stride=Y), :]
-            own_ref[y, s] = v
-            if y < HALO:
-                top_ref[y, s] = v
-            if y >= Y - HALO:
-                bottom_ref[y - (Y - HALO), s] = v
-            total = strip_ref[y] if s else jnp.zeros((X, Z), F32)
-            low = shift(v, 32 * s + HALO)
-            high = shift(v, 32 * s + 16 - (Z - 11))
-            total = jnp.where((lane >= 32 * s + HALO) & (lane < 32 * s + 16), low, total)
-            total = jnp.where((lane >= 32 * s + 16) & (lane < 32 * s + 27), high, total)
-            strip_ref[y] = total
-    for g in range(PACKS):
-        lows = jnp.zeros((X, Z), F32)
-        highs = jnp.zeros((X, Z), F32)
-        for i in range(GROUP):
-            if g * GROUP + i < Y:
-                v = strip_ref[g * GROUP + i]
-                here = (place >= i * HALO) & (place < (i + 1) * HALO)
-                lows = jnp.where(here, shift(v, i * HALO - HALO), lows)
-                highs = jnp.where(here, shift(v, i * HALO - 22), highs)
-        far_ref[g] = jnp.where(odd, highs, lows)
-        near_ref[g] = jnp.where(odd, lows, highs)
 
 
 def unpack_kernel(strip_ref, far_ref, near_ref, full_ref, top_ref, bottom_ref):
@@ -131,9 +99,7 @@
 COEFFICIENTS = 40
 
 
-def coefficient_kernel(member_ref, courant_ref, diffusion_ref, reaction_ref, quadratic_ref, out_ref):
-    sets = courant_ref.shape[-1]
-    hot = lax.broadcasted_iota(jnp.int32, (1, sets), 1) == member_ref[...]
+def coefficients(hot, courant_ref, diffusion_ref, reaction_ref, quadratic_ref, out_ref):
 
     def picked(table):
         return jnp.sum(jnp.where(hot, table, 0.0), axis=1, keepdims=True)
@@ -179,6 +145,54 @@
     put(RANGE, reach)
 
 
+def pack_kernel(
+    state_ref, member_ref, courant_ref, diffusion_ref, reaction_ref, quadratic_ref,
+    own_ref, top_ref, bottom_ref, strip_ref, far_ref, near_ref, table_ref,
+    state, courant, diffusion, reaction, quadratic, state_sems, sems,
+):
+    blocks = [pltpu.make_async_copy(state_ref.at[s], state.at[s], state_sems.at[s]) for s in range(SPECIES)]
+    tables = (
+        (courant_ref, courant), (diffusion_ref, diffusion), (reaction_ref, reaction),
+        (quadratic_ref, quadratic),
+    )
+    copies = [pltpu.make_async_copy(a, b, sems.at[i]) for i, (a, b) in enumerate(tables)]
+    for copy in blocks + copies:
+        copy.start()
+    lane = lanes()
+    odd = lax.axis_index("gz") % 2 == 1
+    place = lane % 32
+    for s in range(SPECIES):
+        blocks[s].wait()
+        for y in range(Y):
+            v = state[s, pl.ds(y, X, stride=Y), :]
+            own_ref[y, s] = v
+            if y < HALO:
+                top_ref[y, s] = v
+            if y >= Y - HALO:
+                bottom_ref[y - (Y - HALO), s] = v
+            total = strip_ref[y] if s else jnp.zeros((X, Z), F32)
+            low = shift(v, 32 * s + HALO)
+            high = shift(v, 32 * s + 16 - (Z - 11))
+            total = jnp.where((lane >= 32 * s + HALO) & (lane < 32 * s + 16), low, total)
+            total = jnp.where((lane >= 32 * s + 16) & (lane < 32 * s + 27), high, total)
+            strip_ref[y] = total
+    for g in range(PACKS):
+        lows = jnp.zeros((X, Z), F32)
+        highs = jnp.zeros((X, Z), F32)
+        for i in range(GROUP):
+            if g * GROUP + i < Y:
+                v = strip_ref[g * GROUP + i]
+                here = (place >= i * HALO) & (place < (i + 1) * HALO)
+                lows = jnp.where(here, shift(v, i * HALO - HALO), lows)
+                highs = jnp.where(here, shift(v, i * HALO - 22), highs)
+        far_ref[g] = jnp.where(odd, highs, lows)
+        near_ref[g] = jnp.where(odd, lows, highs)
+    for copy in copies:
+        copy.wait()
+    hot = lax.broadcasted_iota(jnp.int32, (1, courant.shape[-1]), 1) == member_ref[0]
+    coefficients(hot, courant, diffusion, reaction, quadratic, table_ref)
+
+
 def spread(table_ref, row):
     return jnp.broadcast_to(table_ref[row : row + 1, :], (X, Z))
 
@@ -200,7 +214,7 @@
     return 2.0 * (image - v) - before
 
 
-def main_kernel(own_ref, low_ref, high_ref, table_ref, basis_ref, dots_ref, wide, b0, b1, b2, b3):
+def main_kernel(own_ref, low_ref, high_ref, table_ref, basis_ref, dots_ref, wide, b0, b1, b2, b3, b4):
     low, high = in_grid()
     for r in range(HALO):
         for s in range(SPECIES):
@@ -230,10 +244,10 @@
             b0[row, k] = (out + quad[k] * coupled) * flag
         return _
 
-    over_rows(Y + 8, 4, source_row)
+    over_rows(Y + 8, MAIN_SOURCE, source_row)
 
     scale = [spread(table_ref, SCALE + s) for s in range(SPECIES)]
-    buffers = [b0, b1, b2, b3]
+    buffers = [b0, b1, b2, b3, b4]
 
     def image_of(ref, row, s):
         v = ref[row + 1, s]
@@ -241,30 +255,29 @@
         beside = (below + above) + (ref[row, s] + ref[row + 2, s]) + (shift(v, 1) + shift(v, -1))
         return scale[s] * (6.0 * v - beside), v
 
-    for k in (1, 2, 3):
+    for k in (1, 2, 3, 4):
         before = 4 - k
 
         def level_row(row, _, k=k, before=before):
             flag = row_flag(row, before, low, high)
             for s in range(SPECIES):
                 image, v = image_of(buffers[k - 1], row, s)
-                buffers[k][row, s] = level_value(k, image, v, None) * flag
+                value = level_value(k, image, v, buffers[2][row + 2, s] if k == 4 else None)
+                buffers[k][row, s] = value * flag if before else value
             return _
 
-        over_rows(Y + 2 * before, 4, level_row)
-
-    def last_row(row, sums):
+        over_rows(Y + 2 * before, MAIN_LEVEL[k - 1], level_row)
+
+    def dot_row(row, sums):
         sums = list(sums)
         for s in range(SPECIES):
-            image, v = image_of(b3, row, s)
-            b = [buffers[k][row + 4 - k, s] for k in range(4)]
+            b = [buffers[k][row + 4 - k, s] for k in range(5)]
             for k in range(4):
                 basis_ref[k, row, s] = b[k]
-            b.append(level_value(4, image, v, b[2]))
             sums = [t + p for t, p in zip(sums, dot_terms(b))]
         return tuple(sums)
 
-    sums = over_rows(Y, 2, last_row, tuple(jnp.zeros((8, Z), F32) for _ in range(DOTS)))
+    sums = over_rows(Y, MAIN_DOT, dot_row, tuple(jnp.zeros((8, Z), F32) for _ in range(DOTS)))
     lane = lax.broadcasted_iota(jnp.int32, (8, Z), 1)
     inner = (lane >= HALO) & (lane < Z - HALO)
     for k in range(DOTS):
@@ -272,7 +285,7 @@
 
 
 def strip_kernel(
-    strip_ref, low_ref, high_ref, dots_in_ref, table_ref, basis_ref, total_ref, wide, b0, b1, b2, b3
+    strip_ref, low_ref, high_ref, dots_in_ref, table_ref, basis_ref, total_ref, wide, b0, b1, b2, b3, b4
 ):
     low, high = in_grid()
     for r in range(HALO):
@@ -283,6 +296,7 @@
 
     lane = lanes()
     place = lane % 32
+    species = lane // 32
     first = jnp.where(lax.axis_index("gz") > 0, 1.0, 0.0).astype(F32)
     last = jnp.where(lax.axis_index("gz") < lax.axis_size("gz") - 1, 1.0, 0.0).astype(F32)
     inside = jnp.where(place < HALO, first, jnp.where(place >= 27, last, 1.0))
@@ -295,11 +309,11 @@
         flag = row_flag(row, HALO - 1, low, high)
         v = wide[row + 1]
         turned = [v] + [shift(v, 32 * t) for t in range(1, SPECIES)]
-        b = turned[3]
-        coupled = v * b / (1.0 + v * v + b * b)
-        coupled = jnp.where(lane < 32, coupled, 0.0)
-        coupled = coupled + shift(coupled, 32)
-        coupled = coupled + shift(coupled, 64)
+        a, b = turned[3], turned[2]
+        for t in (2, 1, 0):
+            a = jnp.where(species == t, turned[t], a)
+            b = jnp.where(species == (t + 1) % SPECIES, turned[t], b) if t != 2 else jnp.where(species == 0, turned[3], b)
+        coupled = a * b / (1.0 + a * a + b * b)
         below, above = beside_x(v)
         out = plus[0] * below - minus[0] * above
         out = out + (plus[1] * wide[row] - minus[1] * wide[row + 2])
@@ -309,10 +323,10 @@
         b0[row] = (out + quad * coupled) * (flag * inside)
         return _
 
-    over_rows(Y + 8, Y + 8, source_row)
+    over_rows(Y + 8, STRIP_SOURCE, source_row)
 
     scale = spread(table_ref, STRIP_SCALE)
-    buffers = [b0, b1, b2, b3]
+    buffers = [b0, b1, b2, b3, b4]
 
     def image_of(ref, row):
         v = ref[row + 1]
@@ -320,26 +334,25 @@
         beside = (below + above) + (ref[row] + ref[row + 2]) + (shift(v, 1) + shift(v, -1))
         return scale * (6.0 * v - beside), v
 
-    for k in (1, 2, 3):
+    for k in (1, 2, 3, 4):
         before = 4 - k
 
         def level_row(row, _, k=k, before=before):
             flag = row_flag(row, before, low, high)
             image, v = image_of(buffers[k - 1], row)
-            buffers[k][row] = level_value(k, image, v, None) * (flag * inside)
+            value = level_value(k, image, v, buffers[2][row + 2] if k == 4 else None)
+            buffers[k][row] = value * (flag * inside) if before else value
             return _
 
-        over_rows(Y + 2 * before, Y + 2 * before, level_row)
-
-    def last_row(row, sums):
-        image, v = image_of(b3, row)
-        b = [buffers[k][row + 4 - k] for k in range(4)]
+        over_rows(Y + 2 * before, STRIP_LEVEL[k - 1], level_row)
+
+    def dot_row(row, sums):
+        b = [buffers[k][row + 4 - k] for k in range(5)]
         for k in range(4):
             basis_ref[k, row] = b[k]
-        b.append(level_value(4, image, v, b[2]))
         return tuple(t + p for t, p in zip(sums, dot_terms(b)))
 
-    sums = over_rows(Y, Y, last_row, tuple(jnp.zeros((8, Z), F32) for _ in range(DOTS)))
+    sums = over_rows(Y, STRIP_DOT, dot_row, tuple(jnp.zeros((8, Z), F32) for _ in range(DOTS)))
     place = place[:8]
     edge = ((place >= HALO) & (place < 2 * HALO)) | ((place >= 22) & (place < 27))
     slot = lax.broadcasted_iota(jnp.int32, (8, SLOTS), 1)
@@ -360,7 +373,7 @@
         for k in range(i):
             rest = rest - root[k][i] * root[k][i]
         rest = jnp.maximum(rest, 3e-7 * h[i][i])
-        inverse = 1.0 / jnp.sqrt(rest)
+        inverse = lax.rsqrt(rest)
         root[i][i] = rest * inverse
         for j in range(i + 1, n):
             t = h[i][j]
@@ -382,7 +395,7 @@
         e = columns[j]
         for i in range(j):
             e[i], e[i + 1] = cosines[i] * e[i] + sines[i] * e[i + 1], cosines[i] * e[i + 1] - sines[i] * e[i]
-        inverse = 1.0 / jnp.sqrt(e[j] * e[j] + e[j + 1] * e[j + 1])
+        inverse = lax.rsqrt(e[j] * e[j] + e[j + 1] * e[j + 1])
         cosines.append(e[j] * inverse)
         sines.append(e[j + 1] * inverse)
         e[j] = cosines[j] * e[j] + sines[j] * e[j + 1]
@@ -453,25 +466,27 @@
     edge = struct(HALO, SPECIES, X, Z)
     strip_edge = struct(HALO, X, Z)
     pack = struct(PACKS, X, Z)
-    own, top, bottom, strip, to_far, to_near = call(
+    inputs = (
+        flat, member_set, courant_table.T, diffusion_table.T, reaction_table.transpose(1, 2, 0), quadratic_table.T,
+    )
+    own, top, bottom, strip, to_far, to_near, table = call(
         pack_kernel,
-        (struct(Y, SPECIES, X, Z), edge, edge, struct(Y, X, Z), pack, pack),
-        [pltpu.HBM],
-        [VMEM((SPECIES, X * Y, Z), F32), pltpu.SemaphoreType.DMA((SPECIES,))],
-    )(flat)
+        (struct(Y, SPECIES, X, Z), edge, edge, struct(Y, X, Z), pack, pack, struct(COEFFICIENTS, Z)),
+        [pltpu.HBM, SMEM] + [pltpu.HBM] * 4,
+        [VMEM(flat.shape, F32)]
+        + [VMEM(t.shape, F32) for t in inputs[2:]]
+        + [pltpu.SemaphoreType.DMA((SPECIES,)), pltpu.SemaphoreType.DMA((len(inputs) - 2,))],
+    )(*(t if t is member_set else pltpu.with_memory_space_constraint(t, pltpu.HBM) for t in inputs))
     from_far = lax.ppermute(to_far, "gz", far)
     from_near = lax.ppermute(to_near, "gz", near)
     low = lax.ppermute(bottom, "gy", up)
     high = lax.ppermute(top, "gy", down)
-    table = call(coefficient_kernel, struct(COEFFICIENTS, Z), [VMEM] * 5)(
-        member_set.reshape(1, 1), courant_table.T, diffusion_table.T, reaction_table.transpose(1, 2, 0), quadratic_table.T
-    )
     wide = (SPECIES, X, Z)
     basis, dots = call(
         main_kernel,
         (struct(4, Y, *wide), struct(DOTS, 8, Z)),
         [VMEM] * 4,
-        [VMEM((n, *wide), F32) for n in (ROWS, Y + 8, Y + 6, Y + 4, Y + 2)],
+        [VMEM((n, *wide), F32) for n in (ROWS, Y + 8, Y + 6, Y + 4, Y + 2, Y)],
         flops=10_000_000,
     )(own, low, high, table)
     strip, strip_top, strip_bottom = call(
@@ -483,7 +498,7 @@
         strip_kernel,
         (struct(4, Y, X, Z), struct(gy * gz, SLOTS)),
         [VMEM] * 5,
-        [VMEM((n, X, Z), F32) for n in (ROWS, Y + 8, Y + 6, Y + 4, Y + 2)],
+        [VMEM((n, X, Z), F32) for n in (ROWS, Y + 8, Y + 6, Y + 4, Y + 2, Y)],
     )(strip, strip_low, strip_high, dots, table)
     sums = lax.all_to_all(total, ("gy", "gz"), split_axis=0, concat_axis=0, tiled=True)
     out = call(

time: 54.4 us -> 49.4 us (0.908)
  local copies, waits for them, and re-layouts: 3.78 us -> 0 us
  Pallas kernels: 11 us -> 8.82 us
  blocking collectives: 25.1 us -> 26.3 us
    unnamed x10 -> x0, local copies, waits for them, and re-layouts: 3.78 us -> none
    pallas_call x1, Pallas kernels: 3.16 us -> 1.56 us  [shards(): call(strip_kernel, (struct(4, Y, X, Z), struct(gy * gz, SLOTS)), [VMEM] *...]
    all_to_all x1, blocking collectives: 25.1 us -> 26.3 us  [shards(): lax.all_to_all(total, ('gy', 'gz'), split_axis=0, concat_axis=0, tiled=True)]
    pallas_call x1, Pallas kernels: 4.06 us -> 3.24 us  [shards(): call(main_kernel, (struct(4, Y, *wide), struct(DOTS, 8, Z)), [VMEM] * 4,...]
  transfers between devices with their start and end apart: 6 -> 6, of which waited for: 1 -> 1; matrix products, arithmetic and copies ran while one was open for 0% -> 0% of each run, Pallas kernels for 8% -> 7%
where the time goes in v3:
time: 49.4 us; the launch traced here: 49.2 us
  blocking collectives  26.3 us (53%)
  starting transfers between devices  11.6 us (23%)
  Pallas kernels  8.82 us (18%)
  waiting for transfers between devices  1.82 us (4%)
  between operations  0.71 us (1%)
    all_to_all x1, blocking collectives, shards(): lax.all_to_all(total, ('gy', 'gz'), split_axis=0, concat_axis=0, tiled=True)  26.3 us
    ppermute x1, starting transfers between devices, shards(): from_near = lax.ppermute(to_near, 'gz', near)  4.31 us
    pallas_call x1, Pallas kernels, shards(): call(main_kernel, (struct(4, Y, *wide), struct(DOTS, 8, Z)), [VMEM] * 4,...  3.24 us
    ppermute x1, starting transfers between devices, shards(): strip_high = lax.ppermute(strip_top, 'gy', down)  2.87 us
    pallas_call x1, Pallas kernels, shards(): call(combine_kernel, struct(SPECIES, X * Y, Z), [VMEM] * 3, [VMEM((SPECIE...  2.05 us
    pallas_call x1, Pallas kernels, shards(): call(pack_kernel, (struct(Y, SPECIES, X, Z), edge, edge, struct(Y, X, Z),...  1.83 us
    ppermute x1, waiting for transfers between devices, shards(): from_near = lax.ppermute(to_near, 'gz', near)  1.8 us
    ppermute x1, starting transfers between devices, shards(): high = lax.ppermute(top, 'gy', down)  1.66 us
  transfers between devices with their start and end apart: 6, of which 1 were waited for; matrix products, arithmetic and copies ran while one was open for 0% of the time, Pallas kernels for 7%

profile of v3, /device:TPU:32, one launch (start us, length us, event | category | flops | bytes accessed | tf_op | source)
XLA Modules:
  0.0 49.2 jit_solution(4527523278783908203)
XLA Ops:
  0.7 1.8 %shard_map.64 = (f32[16,4,16,128]{3,2,1,0:T(8,128)S(1)}, f32[5,4,16,128]{3,2,1,0:T(8,128)S(1)}, f32[5,4,16,128]{3,2,1,0:T(8,128)S(1)}, f32[16,16,128]{2,1,0:T(8,...) custom-call(f32[4,256,128]{2,1,0:T(8,128)} %bitcast.12, ...), custom_call_target="tpu_custom_call" | custom-call | flops 1000 | bytes 1048576 | tf_op jit(solution)/shard_map/pallas_call | solution.py:472
  2.5 1.7 %collective-permute-start.4 = (f32[5,4,16,128]{3,2,1,0:T(8,128)S(1)}, f32[5,4,16,128]{3,2,1,0:T(8,128)S(1)}, u32[]{:S(2)}, u32[]{:S(2)}) collective-permute-start(f32[5,4,16,128]{3,2,1,0:T(8,128)S(1)} %get-tuple-element.26), channel_id=1, source_target_pairs={{0,8},{8,16},{16,24},{24,0},{1,9},{9,17},{17,25},{25,1},{2,10},{10... | collective-permute-start | bytes 491528 | tf_op jit(solution)/shard_map/ppermute | solution.py:482
  4.1 1.7 %collective-permute-start.5 = (f32[5,4,16,128]{3,2,1,0:T(8,128)S(1)}, f32[5,4,16,128]{3,2,1,0:T(8,128)S(1)}, u32[]{:S(2)}, u32[]{:S(2)}) collective-permute-start(f32[5,4,16,128]{3,2,1,0:T(8,128)S(1)} %get-tuple-element.27), channel_id=1, source_target_pairs={{8,0},{16,8},{24,16},{0,24},{9,1},{17,9},{25,17},{1,25},{10,2},{18... | collective-permute-start | bytes 491528 | tf_op jit(solution)/shard_map/ppermute | solution.py:483
  5.8 0.7 %collective-permute-start = (f32[3,16,128]{2,1,0:T(8,128)S(1)}, f32[3,16,128]{2,1,0:T(8,128)S(1)}, u32[]{:S(2)}, u32[]{:S(2)}) collective-permute-start(f32[3,16,128]{2,1,0:T(8,128)S(1)} %get-tuple-element.20), channel_id=1, source_target_pairs={{1,2},{2,1},{3,4},{4,3},{5,6},{6,5},{9,10},{10,9},{11,12},{12,11},... | collective-permute-start | bytes 73736 | tf_op jit(solution)/shard_map/ppermute | solution.py:480
  6.5 4.3 %collective-permute-start.1 = (f32[3,16,128]{2,1,0:T(8,128)S(1)}, f32[3,16,128]{2,1,0:T(8,128)S(1)}, u32[]{:S(2)}, u32[]{:S(2)}) collective-permute-start(f32[3,16,128]{2,1,0:T(8,128)S(1)} %get-tuple-element.21), channel_id=1, source_target_pairs={{0,1},{1,0},{2,3},{3,2},{4,5},{5,4},{6,7},{7,6},{8,9},{9,8},{10,11... | collective-permute-start | bytes 73736 | tf_op jit(solution)/shard_map/ppermute | solution.py:481
  10.8 0.0 collective-permute-done.far_ref
  10.8 1.8 %collective-permute-done.1.near_ref = f32[3,16,128]{2,1,0:T(8,128)S(1)} collective-permute-done((f32[3,16,128]{2,1,0:T(8,128)S(1)}, f32[3,16,128]{2,1,0:T(8,128)S(1)}, u32[]{:S(2)}, u32[]{:S(2)}) %collective-permute-start.1) | collective-permute-done | bytes 24608 | tf_op jit(solution)/shard_map/ppermute | solution.py:481
  12.6 0.1 shard_map.65
  12.7 0.4 collective-permute-start.2
  13.2 2.9 %collective-permute-start.3 = (f32[5,16,128]{2,1,0:T(8,128)S(1)}, f32[5,16,128]{2,1,0:T(8,128)S(1)}, u32[]{:S(2)}, u32[]{:S(2)}) collective-permute-start(f32[5,16,128]{2,1,0:T(8,128)S(1)} %get-tuple-element.24), channel_id=1, source_target_pairs={{8,0},{16,8},{24,16},{0,24},{9,1},{17,9},{25,17},{1,25},{10,2},{18... | collective-permute-start | bytes 122888 | tf_op jit(solution)/shard_map/ppermute | solution.py:496
  16.0 0.0 collective-permute-done.4.low_ref
  16.0 0.0 collective-permute-done.5.high_ref
  16.0 3.2 %shard_map.66 = (f32[4,16,4,16,128]{4,3,2,1,0:T(8,128)S(1)}, f32[13,8,128]{2,1,0:T(8,128)S(1)}) custom-call(f32[16,4,16,128]{3,2,1,0:T(8,128)S(1)} %get-tuple-element.25.own_ref, f32[5,4,16,128]{3,2,1,0:T(8,128)S(1)} %collective-permute-done.4.low_ref, f32[5,4,16,128]{3,2,1,0:T(8,128)S(1)} %collective-permute-done.5.high_ref, ...), custom_call_target="tpu_custom_call" | custom-call | flops 10000000 | bytes 1048576 | tf_op jit(solution)/shard_map/pallas_call | solution.py:485
  19.3 0.0 collective-permute-done.2.low_ref
  19.3 0.0 collective-permute-done.3.high_ref
  19.3 1.6 %shard_map.67 = (f32[4,16,16,128]{3,2,1,0:T(8,128)S(1)}, f32[32,16]{1,0:T(8,128)S(1)}) custom-call(f32[16,16,128]{2,1,0:T(8,128)S(1)} %get-tuple-element.22.strip_ref, f32[5,16,128]{2,1,0:T(8,128)S(1)} %collective-permute-done.2.low_ref, f32[5,16,128]{2,1,0:T(8,128)S(1)} %collective-permute-done.3.high_ref, f32[13,8,128]{2,1,0:T(8,128)S(1)} %get-tuple-element.29.dots_in_ref, ...), custom_call_target="tpu_custom_call" | custom-call | flops 1000 | bytes 1048576 | tf_op jit(solution)/shard_map/pallas_call | solution.py:497
  20.9 26.3 %all_to_all.11 = f32[32,1,16]{2,1,0:T(1,128)S(1)} all-to-all(f32[32,1,16]{2,1,0:T(1,128)S(1)} %bitcast.11), channel_id=1, replica_groups=mesh['ens'=8,'gy'=4,'gz'=8] {'gy','gz'}, dimensions={0} | all-to-all | bytes 4096 | tf_op jit(solution)/shard_map/all_to_all | solution.py:503
  47.2 2.1 %shard_map.68 = f32[4,256,128]{2,1,0:T(8,128)} custom-call(f32[32,16]{1,0:T(8,128)S(1)} %bitcast.10, f32[4,16,4,16,128]{4,3,2,1,0:T(8,128)S(1)} %get-tuple-element.31.basis_ref, f32[4,16,16,128]{3,2,1,0:T(8,128)S(1)} %get-tuple-element.32.strip_ref), custom_call_target="tpu_custom_call" | custom-call | flops 1000 | bytes 1048576 | tf_op jit(solution)/shard_map/pallas_call | solution.py:504
Async XLA Ops:
  2.5 13.6 %collective-permute-start.4 = (f32[5,4,16,128]{3,2,1,0:T(8,128)S(1)}, f32[5,4,16,128]{3,2,1,0:T(8,128)S(1)}, u32[]{:S(2)}, u32[]{:S(2)}) collective-permute-start(f32[5,4,16,128]{3,2,1,0:T(8,128)S(1)} %get-tuple-element.26), channel_id=1, source_target_pairs={{0,8},{8,16},{16,24},{24,0},{1,9},{9,17},{17,25},{25,1},{2,10},{10... | collective-permute-start | bytes 491528 | tf_op jit(solution)/shard_map/ppermute | solution.py:482
  4.1 11.9 %collective-permute-start.5 = (f32[5,4,16,128]{3,2,1,0:T(8,128)S(1)}, f32[5,4,16,128]{3,2,1,0:T(8,128)S(1)}, u32[]{:S(2)}, u32[]{:S(2)}) collective-permute-start(f32[5,4,16,128]{3,2,1,0:T(8,128)S(1)} %get-tuple-element.27), channel_id=1, source_target_pairs={{8,0},{16,8},{24,16},{0,24},{9,1},{17,9},{25,17},{1,25},{10,2},{18... | collective-permute-start | bytes 491528 | tf_op jit(solution)/shard_map/ppermute | solution.py:483
  5.8 5.0 %collective-permute-start = (f32[3,16,128]{2,1,0:T(8,128)S(1)}, f32[3,16,128]{2,1,0:T(8,128)S(1)}, u32[]{:S(2)}, u32[]{:S(2)}) collective-permute-start(f32[3,16,128]{2,1,0:T(8,128)S(1)} %get-tuple-element.20), channel_id=1, source_target_pairs={{1,2},{2,1},{3,4},{4,3},{5,6},{6,5},{9,10},{10,9},{11,12},{12,11},... | collective-permute-start | bytes 73736 | tf_op jit(solution)/shard_map/ppermute | solution.py:480
  6.5 6.1 %collective-permute-start.1 = (f32[3,16,128]{2,1,0:T(8,128)S(1)}, f32[3,16,128]{2,1,0:T(8,128)S(1)}, u32[]{:S(2)}, u32[]{:S(2)}) collective-permute-start(f32[3,16,128]{2,1,0:T(8,128)S(1)} %get-tuple-element.21), channel_id=1, source_target_pairs={{0,1},{1,0},{2,3},{3,2},{4,5},{5,4},{6,7},{7,6},{8,9},{9,8},{10,11... | collective-permute-start | bytes 73736 | tf_op jit(solution)/shard_map/ppermute | solution.py:481
  12.7 6.6 %collective-permute-start.2 = (f32[5,16,128]{2,1,0:T(8,128)S(1)}, f32[5,16,128]{2,1,0:T(8,128)S(1)}, u32[]{:S(2)}, u32[]{:S(2)}) collective-permute-start(f32[5,16,128]{2,1,0:T(8,128)S(1)} %get-tuple-element.23), channel_id=1, source_target_pairs={{0,8},{8,16},{16,24},{24,0},{1,9},{9,17},{17,25},{25,1},{2,10},{10... | collective-permute-start | bytes 122888 | tf_op jit(solution)/shard_map/ppermute | solution.py:495
  13.2 6.1 %collective-permute-start.3 = (f32[5,16,128]{2,1,0:T(8,128)S(1)}, f32[5,16,128]{2,1,0:T(8,128)S(1)}, u32[]{:S(2)}, u32[]{:S(2)}) collective-permute-start(f32[5,16,128]{2,1,0:T(8,128)S(1)} %get-tuple-element.24), channel_id=1, source_target_pairs={{8,0},{16,8},{24,16},{0,24},{9,1},{17,9},{25,17},{1,25},{10,2},{18... | collective-permute-start | bytes 122888 | tf_op jit(solution)/shard_map/ppermute | solution.py:496

commit v4 on v3

--- a/solution.py
+++ b/solution.py
@@ -28,6 +28,17 @@
     return jax.ShapeDtypeStruct(shape, F32)
 
 
+GZ = ("gh", "gx")
+
+
+def z_index():
+    return lax.axis_index("gh") * lax.axis_size("gx") + lax.axis_index("gx")
+
+
+def z_size():
+    return lax.axis_size("gh") * lax.axis_size("gx")
+
+
 def lanes():
     return lax.broadcasted_iota(jnp.int32, (X, Z), 1)
 
@@ -57,7 +68,7 @@
 
 def unpack_kernel(strip_ref, far_ref, near_ref, full_ref, top_ref, bottom_ref):
     place = lanes() % 32
-    odd = lax.axis_index("gz") % 2 == 1
+    odd = z_index() % 2 == 1
     for g in range(PACKS):
         far, near = far_ref[g], near_ref[g]
         after = jnp.where(odd, far, near)
@@ -99,7 +110,8 @@
 COEFFICIENTS = 40
 
 
-def coefficients(hot, courant_ref, diffusion_ref, reaction_ref, quadratic_ref, out_ref):
+def coefficient_kernel(member_ref, courant_ref, diffusion_ref, reaction_ref, quadratic_ref, out_ref):
+    hot = lax.broadcasted_iota(jnp.int32, (1, courant_ref.shape[-1]), 1) == member_ref[0]
 
     def picked(table):
         return jnp.sum(jnp.where(hot, table, 0.0), axis=1, keepdims=True)
@@ -146,9 +158,9 @@
 
 
 def pack_kernel(
-    state_ref, member_ref, courant_ref, diffusion_ref, reaction_ref, quadratic_ref,
-    own_ref, top_ref, bottom_ref, strip_ref, far_ref, near_ref, table_ref,
-    state, courant, diffusion, reaction, quadratic, state_sems, sems,
+    state_ref, courant_ref, diffusion_ref, reaction_ref, quadratic_ref,
+    own_ref, top_ref, bottom_ref, strip_ref, far_ref, near_ref, courant, diffusion, reaction, quadratic,
+    state, state_sems, sems,
 ):
     blocks = [pltpu.make_async_copy(state_ref.at[s], state.at[s], state_sems.at[s]) for s in range(SPECIES)]
     tables = (
@@ -159,7 +171,7 @@
     for copy in blocks + copies:
         copy.start()
     lane = lanes()
-    odd = lax.axis_index("gz") % 2 == 1
+    odd = z_index() % 2 == 1
     place = lane % 32
     for s in range(SPECIES):
         blocks[s].wait()
@@ -189,8 +201,6 @@
         near_ref[g] = jnp.where(odd, lows, highs)
     for copy in copies:
         copy.wait()
-    hot = lax.broadcasted_iota(jnp.int32, (1, courant.shape[-1]), 1) == member_ref[0]
-    coefficients(hot, courant, diffusion, reaction, quadratic, table_ref)
 
 
 def spread(table_ref, row):
@@ -297,8 +307,8 @@
     lane = lanes()
     place = lane % 32
     species = lane // 32
-    first = jnp.where(lax.axis_index("gz") > 0, 1.0, 0.0).astype(F32)
-    last = jnp.where(lax.axis_index("gz") < lax.axis_size("gz") - 1, 1.0, 0.0).astype(F32)
+    first = jnp.where(z_index() > 0, 1.0, 0.0).astype(F32)
+    last = jnp.where(z_index() < z_size() - 1, 1.0, 0.0).astype(F32)
     inside = jnp.where(place < HALO, first, jnp.where(place >= 27, last, 1.0))
     plus = [spread(table_ref, PLUS + d) for d in range(3)]
     minus = [spread(table_ref, MINUS + d) for d in range(3)]
@@ -361,8 +371,7 @@
         both = jnp.where(edge, sums[k], 0.0) + dots_in_ref[k]
         one = jnp.sum(jnp.sum(both, axis=0, keepdims=True), axis=1, keepdims=True)
         total = jnp.where(slot == k, one, total)
-    for i in range(total_ref.shape[0] // 8):
-        total_ref[8 * i : 8 * i + 8, :] = total
+    total_ref[...] = jnp.broadcast_to(total[:1], total_ref.shape)
 
 
 def least_squares(h, r):
@@ -420,14 +429,14 @@
         [None, None, None, h33, h34],
         [None, None, None, None, h44],
     ]
-    y = [jnp.broadcast_to(c, (X, Z)) for c in least_squares(h, sums_ref[0:1, DOTS : DOTS + 1])]
+    y = [jnp.broadcast_to(c, (X, Z)) for c in least_squares(h, 0.5 * sums_ref[0:1, DOTS : DOTS + 1])]
     lane = lanes()
     for row in range(Y):
         strip = y[0] * strip_ref[0, row]
         for k in (1, 2, 3):
             strip = strip + y[k] * strip_ref[k, row]
         strips[row] = strip
-    copies = [pltpu.make_async_copy(held.at[s], out_ref.at[s], sems.at[s]) for s in range(SPECIES)]
+    copies = []
     for s in range(SPECIES):
         for row in range(Y):
             v = y[0] * basis_ref[0, row, s]
@@ -437,7 +446,11 @@
             v = jnp.where(lane < HALO, shift(strip, -(32 * s + HALO)), v)
             v = jnp.where(lane >= Z - HALO, shift(strip, Z - HALO - (32 * s + 22)), v)
             held[s, pl.ds(row, X, stride=Y), :] = v
-        copies[s].start()
+        for half in range(2):
+            part = pl.ds(half * (X * Y // 2), X * Y // 2)
+            copy = pltpu.make_async_copy(held.at[s, part], out_ref.at[s, part], sems.at[2 * s + half])
+            copy.start()
+            copies.append(copy)
     for copy in copies:
         copy.wait()
 
@@ -455,7 +468,8 @@
 
 
 def shards(state, member_set, courant_table, diffusion_table, reaction_table, quadratic_table):
-    gy, gz = lax.axis_size("gy"), lax.axis_size("gz")
+    gy, gh, gx = lax.axis_size("gy"), lax.axis_size("gh"), lax.axis_size("gx")
+    gz = gh * gx
     up = [(i, (i + 1) % gy) for i in range(gy)]
     down = [(b, a) for a, b in up]
     far, near = [], []
@@ -466,21 +480,22 @@
     edge = struct(HALO, SPECIES, X, Z)
     strip_edge = struct(HALO, X, Z)
     pack = struct(PACKS, X, Z)
-    inputs = (
-        flat, member_set, courant_table.T, diffusion_table.T, reaction_table.transpose(1, 2, 0), quadratic_table.T,
-    )
-    own, top, bottom, strip, to_far, to_near, table = call(
+    inputs = (flat, courant_table.T, diffusion_table.T, reaction_table.transpose(1, 2, 0), quadratic_table.T)
+    own, top, bottom, strip, to_far, to_near, *tables = call(
         pack_kernel,
-        (struct(Y, SPECIES, X, Z), edge, edge, struct(Y, X, Z), pack, pack, struct(COEFFICIENTS, Z)),
-        [pltpu.HBM, SMEM] + [pltpu.HBM] * 4,
-        [VMEM(flat.shape, F32)]
-        + [VMEM(t.shape, F32) for t in inputs[2:]]
-        + [pltpu.SemaphoreType.DMA((SPECIES,)), pltpu.SemaphoreType.DMA((len(inputs) - 2,))],
-    )(*(t if t is member_set else pltpu.with_memory_space_constraint(t, pltpu.HBM) for t in inputs))
-    from_far = lax.ppermute(to_far, "gz", far)
-    from_near = lax.ppermute(to_near, "gz", near)
+        (struct(Y, SPECIES, X, Z), edge, edge, struct(Y, X, Z), pack, pack, *(struct(*t.shape) for t in inputs[1:])),
+        [pltpu.HBM] * len(inputs),
+        [
+            VMEM(flat.shape, F32),
+            pltpu.SemaphoreType.DMA((SPECIES,)),
+            pltpu.SemaphoreType.DMA((len(inputs) - 1,)),
+        ],
+    )(*(pltpu.with_memory_space_constraint(t, pltpu.HBM) for t in inputs))
+    from_far = lax.ppermute(to_far, GZ, far)
+    from_near = lax.ppermute(to_near, GZ, near)
     low = lax.ppermute(bottom, "gy", up)
     high = lax.ppermute(top, "gy", down)
+    table = call(coefficient_kernel, struct(COEFFICIENTS, Z), [SMEM] + [VMEM] * 4)(member_set, *tables)
     wide = (SPECIES, X, Z)
     basis, dots = call(
         main_kernel,
@@ -496,26 +511,31 @@
     strip_high = lax.ppermute(strip_top, "gy", down)
     strip_basis, total = call(
         strip_kernel,
-        (struct(4, Y, X, Z), struct(gy * gz, SLOTS)),
+        (struct(4, Y, X, Z), struct(gy * gx, SLOTS)),
         [VMEM] * 5,
         [VMEM((n, X, Z), F32) for n in (ROWS, Y + 8, Y + 6, Y + 4, Y + 2, Y)],
     )(strip, strip_low, strip_high, dots, table)
-    sums = lax.all_to_all(total, ("gy", "gz"), split_axis=0, concat_axis=0, tiled=True)
+    other = lax.ppermute(total, "gh", [(i, 1 - i) for i in range(gh)])
+    sums = lax.all_to_all(total + other, ("gy", "gx"), split_axis=0, concat_axis=0, tiled=True)
     out = call(
         combine_kernel,
         struct(SPECIES, X * Y, Z),
         [VMEM] * 3,
-        [VMEM((SPECIES, X * Y, Z), F32), VMEM((Y, X, Z), F32), pltpu.SemaphoreType.DMA((SPECIES,))],
+        [VMEM((SPECIES, X * Y, Z), F32), VMEM((Y, X, Z), F32), pltpu.SemaphoreType.DMA((2 * SPECIES,))],
         out_space=pltpu.HBM,
     )(sums, basis, strip_basis)
     return out.reshape(state.shape)
 
 
 def solution(mesh):
+    ens, gy, gz = (mesh.shape[a] for a in ("ens", "gy", "gz"))
+    split = jax.sharding.Mesh(mesh.devices.reshape(ens, gy, 2, gz // 2), ("ens", "gy", *GZ))
+    state_spec = P("ens", None, None, "gy", GZ)
+
     return jax.shard_map(
         shards,
-        mesh=mesh,
-        in_specs=(P("ens", None, None, "gy", "gz"), P("ens"), P(), P(), P(), P()),
-        out_specs=P("ens", None, None, "gy", "gz"),
+        mesh=split,
+        in_specs=(state_spec, P("ens"), P(), P(), P(), P()),
+        out_specs=state_spec,
         check_vma=False,
     )

time: 49.4 us -> 48 us (0.972)
  blocking collectives: 26.3 us -> 11.9 us
  starting transfers between devices: 11.6 us -> 22.9 us
  waiting for transfers between devices: 1.82 us -> 3.45 us
    all_to_all x1, blocking collectives: 26.3 us -> 11.9 us  [shards(): lax.all_to_all(total + other, ('gy', 'gx'), split_axis=0, concat_axis=0,...]
    ppermute x2 -> x3, starting transfers between devices: 4.97 us -> 16.3 us  [the longest x1 11.3 us: shards(): other = lax.ppermute(total, 'gh', [(i, 1 - i) for i in range(gh)])]
    ppermute x2 -> x3, waiting for transfers between devices: 1.81 us -> 3.44 us  [the longest x1 1.8 us: shards(): from_near = lax.ppermute(to_near, GZ, near)]
    pallas_call x1 -> x2, Pallas kernels: 1.56 us -> 1.76 us  [the longest x1 1.56 us: shards(): call(strip_kernel, (struct(4, Y, X, Z), struct(gy * gx, SLOTS)), [VMEM] *...]
  transfers between devices with their start and end apart: 6 -> 7, of which waited for: 1 -> 2; matrix products, arithmetic and copies ran while one was open for 0% -> 0% of each run, Pallas kernels for 7% -> 7%
where the time goes in v4:
time: 48 us; the launch traced here: 47.9 us
  starting transfers between devices  22.9 us (48%)
  blocking collectives  11.9 us (25%)
  Pallas kernels  8.84 us (18%)
  waiting for transfers between devices  3.45 us (7%)
  between operations  0.72 us (2%)
    all_to_all x1, blocking collectives, shards(): lax.all_to_all(total + other, ('gy', 'gx'), split_axis=0, concat_axis=0,...  11.9 us
    ppermute x1, starting transfers between devices, shards(): other = lax.ppermute(total, 'gh', [(i, 1 - i) for i in range(gh)])  11.3 us
    ppermute x1, starting transfers between devices, shards(): from_near = lax.ppermute(to_near, GZ, near)  4.31 us
    pallas_call x1, Pallas kernels, shards(): call(main_kernel, (struct(4, Y, *wide), struct(DOTS, 8, Z)), [VMEM] * 4,...  3.25 us
    ppermute x1, starting transfers between devices, shards(): strip_high = lax.ppermute(strip_top, 'gy', down)  2.87 us
    pallas_call x1, Pallas kernels, shards(): call(combine_kernel, struct(SPECIES, X * Y, Z), [VMEM] * 3, [VMEM((SPECIE...  2.08 us
    ppermute x1, waiting for transfers between devices, shards(): from_near = lax.ppermute(to_near, GZ, near)  1.8 us
    ppermute x1, starting transfers between devices, shards(): high = lax.ppermute(top, 'gy', down)  1.66 us
  transfers between devices with their start and end apart: 7, of which 2 were waited for; matrix products, arithmetic and copies ran while one was open for 0% of the time, Pallas kernels for 7%

profile of v4, /device:TPU:32, one launch (start us, length us, event | category | flops | bytes accessed | tf_op | source)
XLA Modules:
  0.0 47.9 jit_solution(15503138393537968302)
XLA Ops:
  0.0 1.6 %shard_map.64 = (f32[16,4,16,128]{3,2,1,0:T(8,128)S(1)}, f32[5,4,16,128]{3,2,1,0:T(8,128)S(1)}, f32[5,4,16,128]{3,2,1,0:T(8,128)S(1)}, f32[16,16,128]{2,1,0:T(8,...) custom-call(f32[4,256,128]{2,1,0:T(8,128)} %bitcast.11, ...), custom_call_target="tpu_custom_call" | custom-call | flops 1000 | bytes 1048576 | tf_op jit(solution)/shard_map/pallas_call | solution.py:484
  1.6 1.7 %collective-permute-start.4 = (f32[5,4,16,128]{3,2,1,0:T(8,128)S(1)}, f32[5,4,16,128]{3,2,1,0:T(8,128)S(1)}, u32[]{:S(2)}, u32[]{:S(2)}) collective-permute-start(f32[5,4,16,128]{3,2,1,0:T(8,128)S(1)} %get-tuple-element.29), channel_id=1, source_target_pairs={{0,8},{8,16},{16,24},{24,0},{1,9},{9,17},{17,25},{25,1},{2,10},{10... | collective-permute-start | bytes 491528 | tf_op jit(solution)/shard_map/ppermute | solution.py:496
  3.3 1.7 %collective-permute-start.5 = (f32[5,4,16,128]{3,2,1,0:T(8,128)S(1)}, f32[5,4,16,128]{3,2,1,0:T(8,128)S(1)}, u32[]{:S(2)}, u32[]{:S(2)}) collective-permute-start(f32[5,4,16,128]{3,2,1,0:T(8,128)S(1)} %get-tuple-element.30), channel_id=1, source_target_pairs={{8,0},{16,8},{24,16},{0,24},{9,1},{17,9},{25,17},{1,25},{10,2},{18... | collective-permute-start | bytes 491528 | tf_op jit(solution)/shard_map/ppermute | solution.py:497
  4.9 0.7 %collective-permute-start = (f32[3,16,128]{2,1,0:T(8,128)S(1)}, f32[3,16,128]{2,1,0:T(8,128)S(1)}, u32[]{:S(2)}, u32[]{:S(2)}) collective-permute-start(f32[3,16,128]{2,1,0:T(8,128)S(1)} %get-tuple-element.23), channel_id=1, source_target_pairs={{1,2},{2,1},{3,4},{4,3},{5,6},{6,5},{9,10},{10,9},{11,12},{12,11},... | collective-permute-start | bytes 73736 | tf_op jit(solution)/shard_map/ppermute | solution.py:494
  5.6 4.3 %collective-permute-start.1 = (f32[3,16,128]{2,1,0:T(8,128)S(1)}, f32[3,16,128]{2,1,0:T(8,128)S(1)}, u32[]{:S(2)}, u32[]{:S(2)}) collective-permute-start(f32[3,16,128]{2,1,0:T(8,128)S(1)} %get-tuple-element.24), channel_id=1, source_target_pairs={{0,1},{1,0},{2,3},{3,2},{4,5},{5,4},{6,7},{7,6},{8,9},{9,8},{10,11... | collective-permute-start | bytes 73736 | tf_op jit(solution)/shard_map/ppermute | solution.py:495
  9.9 0.0 collective-permute-done.far_ref
  9.9 1.8 %collective-permute-done.1.near_ref = f32[3,16,128]{2,1,0:T(8,128)S(1)} collective-permute-done((f32[3,16,128]{2,1,0:T(8,128)S(1)}, f32[3,16,128]{2,1,0:T(8,128)S(1)}, u32[]{:S(2)}, u32[]{:S(2)}) %collective-permute-start.1) | collective-permute-done | bytes 24608 | tf_op jit(solution)/shard_map/ppermute | solution.py:495
  11.7 0.1 shard_map.65
  11.9 0.4 collective-permute-start.2
  12.3 2.9 %collective-permute-start.3 = (f32[5,16,128]{2,1,0:T(8,128)S(1)}, f32[5,16,128]{2,1,0:T(8,128)S(1)}, u32[]{:S(2)}, u32[]{:S(2)}) collective-permute-start(f32[5,16,128]{2,1,0:T(8,128)S(1)} %get-tuple-element.27), channel_id=1, source_target_pairs={{8,0},{16,8},{24,16},{0,24},{9,1},{17,9},{25,17},{1,25},{10,2},{18... | collective-permute-start | bytes 122888 | tf_op jit(solution)/shard_map/ppermute | solution.py:511
  15.8 0.2 shard_map.66.table_ref
  16.0 0.0 collective-permute-done.4.low_ref
  16.0 0.0 collective-permute-done.5.high_ref
  16.0 3.2 %shard_map.67 = (f32[4,16,4,16,128]{4,3,2,1,0:T(8,128)S(1)}, f32[13,8,128]{2,1,0:T(8,128)S(1)}) custom-call(f32[16,4,16,128]{3,2,1,0:T(8,128)S(1)} %get-tuple-element.28.own_ref, f32[5,4,16,128]{3,2,1,0:T(8,128)S(1)} %collective-permute-done.4.low_ref, f32[5,4,16,128]{3,2,1,0:T(8,128)S(1)} %collective-permute-done.5.high_ref, f32[40,128]{1,0:T(8,128)S(1)} %shard_map.66.table_ref), custom_call_target="tpu_custom_call" | custom-call | flops 10000000 | bytes 1048576 | tf_op jit(solution)/shard_map/pallas_call | solution.py:500
  19.3 0.0 collective-permute-done.2.low_ref
  19.3 0.0 collective-permute-done.3.high_ref
  19.3 1.6 %shard_map.68 = (f32[4,16,16,128]{3,2,1,0:T(8,128)S(1)}, f32[16,16]{1,0:T(8,128)S(1)}) custom-call(f32[16,16,128]{2,1,0:T(8,128)S(1)} %get-tuple-element.25.strip_ref, f32[5,16,128]{2,1,0:T(8,128)S(1)} %collective-permute-done.2.low_ref, f32[5,16,128]{2,1,0:T(8,128)S(1)} %collective-permute-done.3.high_ref, f32[13,8,128]{2,1,0:T(8,128)S(1)} %get-tuple-element.35.dots_in_ref, ...), custom_call_target="tpu_custom_call" | custom-call | flops 1000 | bytes 1048576 | tf_op jit(solution)/shard_map/pallas_call | solution.py:512
  20.9 11.3 %collective-permute-start.6 = (f32[16,16]{1,0:T(8,128)S(1)}, f32[16,16]{1,0:T(8,128)S(1)}, u32[]{:S(2)}, u32[]{:S(2)}) collective-permute-start(f32[16,16]{1,0:T(8,128)S(1)} %get-tuple-element.36), channel_id=1, source_target_pairs={{0,4},{4,0},{1,5},{5,1},{2,6},{6,2},{3,7},{7,3},{8,12},{12,8},{9,1... | collective-permute-start | bytes 3080 | tf_op jit(solution)/shard_map/ppermute | solution.py:518
  32.2 1.6 %collective-permute-done.6 = f32[16,16]{1,0:T(8,128)S(1)} collective-permute-done((f32[16,16]{1,0:T(8,128)S(1)}, f32[16,16]{1,0:T(8,128)S(1)}, u32[]{:S(2)}, u32[]{:S(2)}) %collective-permute-start.6) | collective-permute-done | bytes 1056 | tf_op jit(solution)/shard_map/ppermute | solution.py:518
  33.9 11.9 %all_to_all.11 = f32[16,1,16]{2,1,0:T(1,128)S(1)} all-to-all(f32[16,1,16]{2,1,0:T(1,128)S(1)} %bitcast.12), channel_id=1, replica_groups=mesh['ens'=8,'gy'=4,'gh'=2,'gx'=4] {'gy','gx'}, dimensions={0} | all-to-all | bytes 2048 | tf_op jit(solution)/shard_map/all_to_all | solution.py:519
  45.8 2.1 %shard_map.69 = f32[4,256,128]{2,1,0:T(8,128)} custom-call(f32[16,16]{1,0:T(8,128)S(1)} %bitcast.10, f32[4,16,4,16,128]{4,3,2,1,0:T(8,128)S(1)} %get-tuple-element.37.basis_ref, f32[4,16,16,128]{3,2,1,0:T(8,128)S(1)} %get-tuple-element.38.strip_ref), custom_call_target="tpu_custom_call" | custom-call | flops 1000 | bytes 1048576 | tf_op jit(solution)/shard_map/pallas_call | solution.py:520
  (1 shorter events, 0.0 us)
Async XLA Ops:
  1.6 14.4 %collective-permute-start.4 = (f32[5,4,16,128]{3,2,1,0:T(8,128)S(1)}, f32[5,4,16,128]{3,2,1,0:T(8,128)S(1)}, u32[]{:S(2)}, u32[]{:S(2)}) collective-permute-start(f32[5,4,16,128]{3,2,1,0:T(8,128)S(1)} %get-tuple-element.29), channel_id=1, source_target_pairs={{0,8},{8,16},{16,24},{24,0},{1,9},{9,17},{17,25},{25,1},{2,10},{10... | collective-permute-start | bytes 491528 | tf_op jit(solution)/shard_map/ppermute | solution.py:496
  3.3 12.7 %collective-permute-start.5 = (f32[5,4,16,128]{3,2,1,0:T(8,128)S(1)}, f32[5,4,16,128]{3,2,1,0:T(8,128)S(1)}, u32[]{:S(2)}, u32[]{:S(2)}) collective-permute-start(f32[5,4,16,128]{3,2,1,0:T(8,128)S(1)} %get-tuple-element.30), channel_id=1, source_target_pairs={{8,0},{16,8},{24,16},{0,24},{9,1},{17,9},{25,17},{1,25},{10,2},{18... | collective-permute-start | bytes 491528 | tf_op jit(solution)/shard_map/ppermute | solution.py:497
  4.9 5.0 %collective-permute-start = (f32[3,16,128]{2,1,0:T(8,128)S(1)}, f32[3,16,128]{2,1,0:T(8,128)S(1)}, u32[]{:S(2)}, u32[]{:S(2)}) collective-permute-start(f32[3,16,128]{2,1,0:T(8,128)S(1)} %get-tuple-element.23), channel_id=1, source_target_pairs={{1,2},{2,1},{3,4},{4,3},{5,6},{6,5},{9,10},{10,9},{11,12},{12,11},... | collective-permute-start | bytes 73736 | tf_op jit(solution)/shard_map/ppermute | solution.py:494
  5.6 6.1 %collective-permute-start.1 = (f32[3,16,128]{2,1,0:T(8,128)S(1)}, f32[3,16,128]{2,1,0:T(8,128)S(1)}, u32[]{:S(2)}, u32[]{:S(2)}) collective-permute-start(f32[3,16,128]{2,1,0:T(8,128)S(1)} %get-tuple-element.24), channel_id=1, source_target_pairs={{0,1},{1,0},{2,3},{3,2},{4,5},{5,4},{6,7},{7,6},{8,9},{9,8},{10,11... | collective-permute-start | bytes 73736 | tf_op jit(solution)/shard_map/ppermute | solution.py:495
  11.9 7.4 %collective-permute-start.2 = (f32[5,16,128]{2,1,0:T(8,128)S(1)}, f32[5,16,128]{2,1,0:T(8,128)S(1)}, u32[]{:S(2)}, u32[]{:S(2)}) collective-permute-start(f32[5,16,128]{2,1,0:T(8,128)S(1)} %get-tuple-element.26), channel_id=1, source_target_pairs={{0,8},{8,16},{16,24},{24,0},{1,9},{9,17},{17,25},{25,1},{2,10},{10... | collective-permute-start | bytes 122888 | tf_op jit(solution)/shard_map/ppermute | solution.py:510
  12.3 7.0 %collective-permute-start.3 = (f32[5,16,128]{2,1,0:T(8,128)S(1)}, f32[5,16,128]{2,1,0:T(8,128)S(1)}, u32[]{:S(2)}, u32[]{:S(2)}) collective-permute-start(f32[5,16,128]{2,1,0:T(8,128)S(1)} %get-tuple-element.27), channel_id=1, source_target_pairs={{8,0},{16,8},{24,16},{0,24},{9,1},{17,9},{25,17},{1,25},{10,2},{18... | collective-permute-start | bytes 122888 | tf_op jit(solution)/shard_map/ppermute | solution.py:511
  20.9 13.0 %collective-permute-start.6 = (f32[16,16]{1,0:T(8,128)S(1)}, f32[16,16]{1,0:T(8,128)S(1)}, u32[]{:S(2)}, u32[]{:S(2)}) collective-permute-start(f32[16,16]{1,0:T(8,128)S(1)} %get-tuple-element.36), channel_id=1, source_target_pairs={{0,4},{4,0},{1,5},{5,1},{2,6},{6,2},{3,7},{7,3},{8,12},{12,8},{9,1... | collective-permute-start | bytes 3080 | tf_op jit(solution)/shard_map/ppermute | solution.py:518

commit v5 on v4

--- a/solution.py
+++ b/solution.py
@@ -399,15 +399,15 @@
             column.append(sum(terms[1:], terms[0]))
         columns.append(column)
     target = [root[0][0]]
-    cosines, sines = [], []
+    cosines, sines, inverses = [], [], []
     for j in range(4):
         e = columns[j]
         for i in range(j):
             e[i], e[i + 1] = cosines[i] * e[i] + sines[i] * e[i + 1], cosines[i] * e[i + 1] - sines[i] * e[i]
         inverse = lax.rsqrt(e[j] * e[j] + e[j + 1] * e[j + 1])
+        inverses.append(inverse)
         cosines.append(e[j] * inverse)
         sines.append(e[j + 1] * inverse)
-        e[j] = cosines[j] * e[j] + sines[j] * e[j + 1]
         target.append(-sines[j] * target[j])
         target[j] = cosines[j] * target[j]
     y = [None] * 4
@@ -415,12 +415,12 @@
         t = target[j]
         for k in range(j + 1, 4):
             t = t - columns[k][j] * y[k]
-        y[j] = t / columns[j][j]
+        y[j] = t * inverses[j]
     return y
 
 
-def combine_kernel(sums_ref, basis_ref, strip_ref, out_ref, held, strips, sems):
-    total = jnp.sum(sums_ref[...], axis=0, keepdims=True)
+def combine_kernel(sums_ref, others_ref, basis_ref, strip_ref, out_ref, held, strips, sems):
+    total = jnp.sum(sums_ref[...] + others_ref[...], axis=0, keepdims=True)
     h00, h01, h03, h04, h11, h12, h13, h14, h22, h23, h33, h34, h44 = (total[:, k : k + 1] for k in range(DOTS))
     h = [
         [h00, h01, h11, h03, h04],
@@ -429,7 +429,7 @@
         [None, None, None, h33, h34],
         [None, None, None, None, h44],
     ]
-    y = [jnp.broadcast_to(c, (X, Z)) for c in least_squares(h, 0.5 * sums_ref[0:1, DOTS : DOTS + 1])]
+    y = [jnp.broadcast_to(c, (X, Z)) for c in least_squares(h, sums_ref[0:1, DOTS : DOTS + 1])]
     lane = lanes()
     for row in range(Y):
         strip = y[0] * strip_ref[0, row]
@@ -515,15 +515,15 @@
         [VMEM] * 5,
         [VMEM((n, X, Z), F32) for n in (ROWS, Y + 8, Y + 6, Y + 4, Y + 2, Y)],
     )(strip, strip_low, strip_high, dots, table)
-    other = lax.ppermute(total, "gh", [(i, 1 - i) for i in range(gh)])
-    sums = lax.all_to_all(total + other, ("gy", "gx"), split_axis=0, concat_axis=0, tiled=True)
+    sums = lax.all_to_all(total, ("gy", "gx"), split_axis=0, concat_axis=0, tiled=True)
+    others = lax.ppermute(sums, "gh", [(i, 1 - i) for i in range(gh)])
     out = call(
         combine_kernel,
         struct(SPECIES, X * Y, Z),
-        [VMEM] * 3,
+        [VMEM] * 4,
         [VMEM((SPECIES, X * Y, Z), F32), VMEM((Y, X, Z), F32), pltpu.SemaphoreType.DMA((2 * SPECIES,))],
         out_space=pltpu.HBM,
-    )(sums, basis, strip_basis)
+    )(sums, others, basis, strip_basis)
     return out.reshape(state.shape)
 
 

time: 48 us -> 47.8 us (level)
  starting transfers between devices: 22.9 us -> 15.7 us
  blocking collectives: 11.9 us -> 17.3 us
  waiting for transfers between devices: 3.45 us -> 5.27 us
    ppermute x1, starting transfers between devices: 11.3 us -> 4.1 us  [shards(): others = lax.ppermute(sums, 'gh', [(i, 1 - i) for i in range(gh)])]
    all_to_all x1, blocking collectives: 11.9 us -> 17.3 us  [shards(): lax.all_to_all(total, ('gy', 'gx'), split_axis=0, concat_axis=0, tiled=True)]
    ppermute x1, waiting for transfers between devices: 1.63 us -> 3.45 us  [shards(): others = lax.ppermute(sums, 'gh', [(i, 1 - i) for i in range(gh)])]
where the time goes in v5:
time: 47.8 us; the launch traced here: 47.7 us
  blocking collectives  17.3 us (36%)
  starting transfers between devices  15.7 us (33%)
  Pallas kernels  8.72 us (18%)
  waiting for transfers between devices  5.27 us (11%)
  between operations  0.72 us (2%)
    all_to_all x1, blocking collectives, shards(): lax.all_to_all(total, ('gy', 'gx'), split_axis=0, concat_axis=0, tiled=True)  17.3 us
    ppermute x1, starting transfers between devices, shards(): from_near = lax.ppermute(to_near, GZ, near)  4.31 us
    ppermute x1, starting transfers between devices, shards(): others = lax.ppermute(sums, 'gh', [(i, 1 - i) for i in range(gh)])  4.1 us
    ppermute x1, waiting for transfers between devices, shards(): others = lax.ppermute(sums, 'gh', [(i, 1 - i) for i in range(gh)])  3.45 us
    pallas_call x1, Pallas kernels, shards(): call(main_kernel, (struct(4, Y, *wide), struct(DOTS, 8, Z)), [VMEM] * 4,...  3.25 us
    ppermute x1, starting transfers between devices, shards(): strip_high = lax.ppermute(strip_top, 'gy', down)  2.87 us
    pallas_call x1, Pallas kernels, shards(): call(combine_kernel, struct(SPECIES, X * Y, Z), [VMEM] * 4, [VMEM((SPECIE...  1.97 us
    ppermute x1, waiting for transfers between devices, shards(): from_near = lax.ppermute(to_near, GZ, near)  1.8 us
  transfers between devices with their start and end apart: 7, of which 2 were waited for; matrix products, arithmetic and copies ran while one was open for 0% of the time, Pallas kernels for 7%

profile of v5, /device:TPU:32, one launch (start us, length us, event | category | flops | bytes accessed | tf_op | source)
XLA Modules:
  0.0 47.7 jit_solution(9270824457452701512)
XLA Ops:
  0.0 1.6 %shard_map.64 = (f32[16,4,16,128]{3,2,1,0:T(8,128)S(1)}, f32[5,4,16,128]{3,2,1,0:T(8,128)S(1)}, f32[5,4,16,128]{3,2,1,0:T(8,128)S(1)}, f32[16,16,128]{2,1,0:T(8,...) custom-call(f32[4,256,128]{2,1,0:T(8,128)} %bitcast.13, ...), custom_call_target="tpu_custom_call" | custom-call | flops 1000 | bytes 1048576 | tf_op jit(solution)/shard_map/pallas_call | solution.py:484
  1.6 1.7 %collective-permute-start.4 = (f32[5,4,16,128]{3,2,1,0:T(8,128)S(1)}, f32[5,4,16,128]{3,2,1,0:T(8,128)S(1)}, u32[]{:S(2)}, u32[]{:S(2)}) collective-permute-start(f32[5,4,16,128]{3,2,1,0:T(8,128)S(1)} %get-tuple-element.29), channel_id=1, source_target_pairs={{0,8},{8,16},{16,24},{24,0},{1,9},{9,17},{17,25},{25,1},{2,10},{10... | collective-permute-start | bytes 491528 | tf_op jit(solution)/shard_map/ppermute | solution.py:496
  3.3 1.7 %collective-permute-start.5 = (f32[5,4,16,128]{3,2,1,0:T(8,128)S(1)}, f32[5,4,16,128]{3,2,1,0:T(8,128)S(1)}, u32[]{:S(2)}, u32[]{:S(2)}) collective-permute-start(f32[5,4,16,128]{3,2,1,0:T(8,128)S(1)} %get-tuple-element.30), channel_id=1, source_target_pairs={{8,0},{16,8},{24,16},{0,24},{9,1},{17,9},{25,17},{1,25},{10,2},{18... | collective-permute-start | bytes 491528 | tf_op jit(solution)/shard_map/ppermute | solution.py:497
  4.9 0.7 %collective-permute-start = (f32[3,16,128]{2,1,0:T(8,128)S(1)}, f32[3,16,128]{2,1,0:T(8,128)S(1)}, u32[]{:S(2)}, u32[]{:S(2)}) collective-permute-start(f32[3,16,128]{2,1,0:T(8,128)S(1)} %get-tuple-element.23), channel_id=1, source_target_pairs={{1,2},{2,1},{3,4},{4,3},{5,6},{6,5},{9,10},{10,9},{11,12},{12,11},... | collective-permute-start | bytes 73736 | tf_op jit(solution)/shard_map/ppermute | solution.py:494
  5.6 4.3 %collective-permute-start.1 = (f32[3,16,128]{2,1,0:T(8,128)S(1)}, f32[3,16,128]{2,1,0:T(8,128)S(1)}, u32[]{:S(2)}, u32[]{:S(2)}) collective-permute-start(f32[3,16,128]{2,1,0:T(8,128)S(1)} %get-tuple-element.24), channel_id=1, source_target_pairs={{0,1},{1,0},{2,3},{3,2},{4,5},{5,4},{6,7},{7,6},{8,9},{9,8},{10,11... | collective-permute-start | bytes 73736 | tf_op jit(solution)/shard_map/ppermute | solution.py:495
  9.9 0.0 collective-permute-done.far_ref
  9.9 1.8 %collective-permute-done.1.near_ref = f32[3,16,128]{2,1,0:T(8,128)S(1)} collective-permute-done((f32[3,16,128]{2,1,0:T(8,128)S(1)}, f32[3,16,128]{2,1,0:T(8,128)S(1)}, u32[]{:S(2)}, u32[]{:S(2)}) %collective-permute-start.1) | collective-permute-done | bytes 24608 | tf_op jit(solution)/shard_map/ppermute | solution.py:495
  11.7 0.1 shard_map.65
  11.9 0.4 collective-permute-start.2
  12.3 2.9 %collective-permute-start.3 = (f32[5,16,128]{2,1,0:T(8,128)S(1)}, f32[5,16,128]{2,1,0:T(8,128)S(1)}, u32[]{:S(2)}, u32[]{:S(2)}) collective-permute-start(f32[5,16,128]{2,1,0:T(8,128)S(1)} %get-tuple-element.27), channel_id=1, source_target_pairs={{8,0},{16,8},{24,16},{0,24},{9,1},{17,9},{25,17},{1,25},{10,2},{18... | collective-permute-start | bytes 122888 | tf_op jit(solution)/shard_map/ppermute | solution.py:511
  15.8 0.2 shard_map.66.table_ref
  16.0 0.0 collective-permute-done.4.low_ref
  16.0 0.0 collective-permute-done.5.high_ref
  16.0 3.2 %shard_map.67 = (f32[4,16,4,16,128]{4,3,2,1,0:T(8,128)S(1)}, f32[13,8,128]{2,1,0:T(8,128)S(1)}) custom-call(f32[16,4,16,128]{3,2,1,0:T(8,128)S(1)} %get-tuple-element.28.own_ref, f32[5,4,16,128]{3,2,1,0:T(8,128)S(1)} %collective-permute-done.4.low_ref, f32[5,4,16,128]{3,2,1,0:T(8,128)S(1)} %collective-permute-done.5.high_ref, f32[40,128]{1,0:T(8,128)S(1)} %shard_map.66.table_ref), custom_call_target="tpu_custom_call" | custom-call | flops 10000000 | bytes 1048576 | tf_op jit(solution)/shard_map/pallas_call | solution.py:500
  19.3 0.0 collective-permute-done.2.low_ref
  19.3 0.0 collective-permute-done.3.high_ref
  19.3 1.6 %shard_map.68 = (f32[4,16,16,128]{3,2,1,0:T(8,128)S(1)}, f32[16,16]{1,0:T(8,128)S(1)}) custom-call(f32[16,16,128]{2,1,0:T(8,128)S(1)} %get-tuple-element.25.strip_ref, f32[5,16,128]{2,1,0:T(8,128)S(1)} %collective-permute-done.2.low_ref, f32[5,16,128]{2,1,0:T(8,128)S(1)} %collective-permute-done.3.high_ref, f32[13,8,128]{2,1,0:T(8,128)S(1)} %get-tuple-element.35.dots_in_ref, ...), custom_call_target="tpu_custom_call" | custom-call | flops 1000 | bytes 1048576 | tf_op jit(solution)/shard_map/pallas_call | solution.py:512
  20.9 17.3 %all_to_all.11 = f32[16,1,16]{2,1,0:T(1,128)S(1)} all-to-all(f32[16,1,16]{2,1,0:T(1,128)S(1)} %bitcast.12), channel_id=1, replica_groups=mesh['ens'=8,'gy'=4,'gh'=2,'gx'=4] {'gy','gx'}, dimensions={0} | all-to-all | bytes 2048 | tf_op jit(solution)/shard_map/all_to_all | solution.py:518
  38.2 4.1 %collective-permute-start.6 = (f32[16,16]{1,0:T(8,128)S(1)}, f32[16,16]{1,0:T(8,128)S(1)}, u32[]{:S(2)}, u32[]{:S(2)}) collective-permute-start(f32[16,16]{1,0:T(8,128)S(1)} %bitcast.10), channel_id=1, source_target_pairs={{0,4},{4,0},{1,5},{5,1},{2,6},{6,2},{3,7},{7,3},{8,12},{12,8},{9,1... | collective-permute-start | bytes 3080 | tf_op jit(solution)/shard_map/ppermute | solution.py:519
  42.3 3.5 %collective-permute-done.6.others_ref = f32[16,16]{1,0:T(8,128)S(1)} collective-permute-done((f32[16,16]{1,0:T(8,128)S(1)}, f32[16,16]{1,0:T(8,128)S(1)}, u32[]{:S(2)}, u32[]{:S(2)}) %collective-permute-start.6) | collective-permute-done | bytes 1056 | tf_op jit(solution)/shard_map/ppermute | solution.py:519
  45.7 2.0 %shard_map.69 = f32[4,256,128]{2,1,0:T(8,128)} custom-call(f32[16,16]{1,0:T(8,128)S(1)} %bitcast.11, f32[16,16]{1,0:T(8,128)S(1)} %collective-permute-done.6.others_ref, f32[4,16,4,16,128]{4,3,2,1,0:T(8,128)S(1)} %get-tuple-element.37.basis_ref, f32[4,16,16,128]{3,2,1,0:T(8,128)S(1)} %get-tuple-element.38.strip_ref), custom_call_target="tpu_custom_call" | custom-call | flops 1000 | bytes 1048576 | tf_op jit(solution)/shard_map/pallas_call | solution.py:520
Async XLA Ops:
  1.6 14.4 %collective-permute-start.4 = (f32[5,4,16,128]{3,2,1,0:T(8,128)S(1)}, f32[5,4,16,128]{3,2,1,0:T(8,128)S(1)}, u32[]{:S(2)}, u32[]{:S(2)}) collective-permute-start(f32[5,4,16,128]{3,2,1,0:T(8,128)S(1)} %get-tuple-element.29), channel_id=1, source_target_pairs={{0,8},{8,16},{16,24},{24,0},{1,9},{9,17},{17,25},{25,1},{2,10},{10... | collective-permute-start | bytes 491528 | tf_op jit(solution)/shard_map/ppermute | solution.py:496
  3.3 12.7 %collective-permute-start.5 = (f32[5,4,16,128]{3,2,1,0:T(8,128)S(1)}, f32[5,4,16,128]{3,2,1,0:T(8,128)S(1)}, u32[]{:S(2)}, u32[]{:S(2)}) collective-permute-start(f32[5,4,16,128]{3,2,1,0:T(8,128)S(1)} %get-tuple-element.30), channel_id=1, source_target_pairs={{8,0},{16,8},{24,16},{0,24},{9,1},{17,9},{25,17},{1,25},{10,2},{18... | collective-permute-start | bytes 491528 | tf_op jit(solution)/shard_map/ppermute | solution.py:497
  4.9 5.0 %collective-permute-start = (f32[3,16,128]{2,1,0:T(8,128)S(1)}, f32[3,16,128]{2,1,0:T(8,128)S(1)}, u32[]{:S(2)}, u32[]{:S(2)}) collective-permute-start(f32[3,16,128]{2,1,0:T(8,128)S(1)} %get-tuple-element.23), channel_id=1, source_target_pairs={{1,2},{2,1},{3,4},{4,3},{5,6},{6,5},{9,10},{10,9},{11,12},{12,11},... | collective-permute-start | bytes 73736 | tf_op jit(solution)/shard_map/ppermute | solution.py:494
  5.6 6.1 %collective-permute-start.1 = (f32[3,16,128]{2,1,0:T(8,128)S(1)}, f32[3,16,128]{2,1,0:T(8,128)S(1)}, u32[]{:S(2)}, u32[]{:S(2)}) collective-permute-start(f32[3,16,128]{2,1,0:T(8,128)S(1)} %get-tuple-element.24), channel_id=1, source_target_pairs={{0,1},{1,0},{2,3},{3,2},{4,5},{5,4},{6,7},{7,6},{8,9},{9,8},{10,11... | collective-permute-start | bytes 73736 | tf_op jit(solution)/shard_map/ppermute | solution.py:495
  11.9 7.4 %collective-permute-start.2 = (f32[5,16,128]{2,1,0:T(8,128)S(1)}, f32[5,16,128]{2,1,0:T(8,128)S(1)}, u32[]{:S(2)}, u32[]{:S(2)}) collective-permute-start(f32[5,16,128]{2,1,0:T(8,128)S(1)} %get-tuple-element.26), channel_id=1, source_target_pairs={{0,8},{8,16},{16,24},{24,0},{1,9},{9,17},{17,25},{25,1},{2,10},{10... | collective-permute-start | bytes 122888 | tf_op jit(solution)/shard_map/ppermute | solution.py:510
  12.3 7.0 %collective-permute-start.3 = (f32[5,16,128]{2,1,0:T(8,128)S(1)}, f32[5,16,128]{2,1,0:T(8,128)S(1)}, u32[]{:S(2)}, u32[]{:S(2)}) collective-permute-start(f32[5,16,128]{2,1,0:T(8,128)S(1)} %get-tuple-element.27), channel_id=1, source_target_pairs={{8,0},{16,8},{24,16},{0,24},{9,1},{17,9},{25,17},{1,25},{10,2},{18... | collective-permute-start | bytes 122888 | tf_op jit(solution)/shard_map/ppermute | solution.py:511
  38.2 7.6 %collective-permute-start.6 = (f32[16,16]{1,0:T(8,128)S(1)}, f32[16,16]{1,0:T(8,128)S(1)}, u32[]{:S(2)}, u32[]{:S(2)}) collective-permute-start(f32[16,16]{1,0:T(8,128)S(1)} %bitcast.10), channel_id=1, source_target_pairs={{0,4},{4,0},{1,5},{5,1},{2,6},{6,2},{3,7},{7,3},{8,12},{12,8},{9,1... | collective-permute-start | bytes 3080 | tf_op jit(solution)/shard_map/ppermute | solution.py:519

commit v6 on v5

--- a/solution.py
+++ b/solution.py
@@ -419,8 +419,8 @@
     return y
 
 
-def combine_kernel(sums_ref, others_ref, basis_ref, strip_ref, out_ref, held, strips, sems):
-    total = jnp.sum(sums_ref[...] + others_ref[...], axis=0, keepdims=True)
+def combine_kernel(sums_ref, basis_ref, strip_ref, out_ref, held, strips, sems):
+    total = jnp.sum(sums_ref[...], axis=0, keepdims=True)
     h00, h01, h03, h04, h11, h12, h13, h14, h22, h23, h33, h34, h44 = (total[:, k : k + 1] for k in range(DOTS))
     h = [
         [h00, h01, h11, h03, h04],
@@ -511,19 +511,18 @@
     strip_high = lax.ppermute(strip_top, "gy", down)
     strip_basis, total = call(
         strip_kernel,
-        (struct(4, Y, X, Z), struct(gy * gx, SLOTS)),
+        (struct(4, Y, X, Z), struct(gy * gz, SLOTS)),
         [VMEM] * 5,
         [VMEM((n, X, Z), F32) for n in (ROWS, Y + 8, Y + 6, Y + 4, Y + 2, Y)],
     )(strip, strip_low, strip_high, dots, table)
-    sums = lax.all_to_all(total, ("gy", "gx"), split_axis=0, concat_axis=0, tiled=True)
-    others = lax.ppermute(sums, "gh", [(i, 1 - i) for i in range(gh)])
+    sums = lax.all_to_all(total, ("gy", *GZ), split_axis=0, concat_axis=0, tiled=True)
     out = call(
         combine_kernel,
         struct(SPECIES, X * Y, Z),
-        [VMEM] * 4,
+        [VMEM] * 3,
         [VMEM((SPECIES, X * Y, Z), F32), VMEM((Y, X, Z), F32), pltpu.SemaphoreType.DMA((2 * SPECIES,))],
         out_space=pltpu.HBM,
-    )(sums, others, basis, strip_basis)
+    )(sums, basis, strip_basis)
     return out.reshape(state.shape)
 
 

time: 47.8 us -> 48.4 us (1.013)
  blocking collectives: 17.3 us -> 25.4 us
  starting transfers between devices: 15.7 us -> 11.6 us
  waiting for transfers between devices: 5.27 us -> 1.82 us
    all_to_all x1, blocking collectives: 17.3 us -> 25.4 us  [shards(): lax.all_to_all(total, ('gy', *GZ), split_axis=0, concat_axis=0, tiled=True)]
    ppermute x1 -> x0, starting transfers between devices: 4.1 us -> none  [shards(): others = lax.ppermute(sums, 'gh', [(i, 1 - i) for i in range(gh)])]
    ppermute x1 -> x0, waiting for transfers between devices: 3.45 us -> none  [shards(): others = lax.ppermute(sums, 'gh', [(i, 1 - i) for i in range(gh)])]
  transfers between devices with their start and end apart: 7 -> 6, of which waited for: 2 -> 1; matrix products, arithmetic and copies ran while one was open for 0% -> 0% of each run, Pallas kernels for 7% -> 7%
where the time goes in v6:
time: 48.4 us; the launch traced here: 48.3 us
  blocking collectives  25.4 us (52%)
  starting transfers between devices  11.6 us (24%)
  Pallas kernels  8.72 us (18%)
  waiting for transfers between devices  1.82 us (4%)
  between operations  0.72 us (1%)
    all_to_all x1, blocking collectives, shards(): lax.all_to_all(total, ('gy', *GZ), split_axis=0, concat_axis=0, tiled=True)  25.4 us
    ppermute x1, starting transfers between devices, shards(): from_near = lax.ppermute(to_near, GZ, near)  4.31 us
    pallas_call x1, Pallas kernels, shards(): call(main_kernel, (struct(4, Y, *wide), struct(DOTS, 8, Z)), [VMEM] * 4,...  3.25 us
    ppermute x1, starting transfers between devices, shards(): strip_high = lax.ppermute(strip_top, 'gy', down)  2.87 us
    pallas_call x1, Pallas kernels, shards(): call(combine_kernel, struct(SPECIES, X * Y, Z), [VMEM] * 3, [VMEM((SPECIE...  1.97 us
    ppermute x1, waiting for transfers between devices, shards(): from_near = lax.ppermute(to_near, GZ, near)  1.8 us
    ppermute x1, starting transfers between devices, shards(): high = lax.ppermute(top, 'gy', down)  1.66 us
    ppermute x1, starting transfers between devices, shards(): low = lax.ppermute(bottom, 'gy', up)  1.65 us
  transfers between devices with their start and end apart: 6, of which 1 were waited for; matrix products, arithmetic and copies ran while one was open for 0% of the time, Pallas kernels for 7%

profile of v6, /device:TPU:32, one launch (start us, length us, event | category | flops | bytes accessed | tf_op | source)
XLA Modules:
  0.0 48.3 jit_solution(17039648894947731656)
XLA Ops:
  0.0 1.6 %shard_map.64 = (f32[16,4,16,128]{3,2,1,0:T(8,128)S(1)}, f32[5,4,16,128]{3,2,1,0:T(8,128)S(1)}, f32[5,4,16,128]{3,2,1,0:T(8,128)S(1)}, f32[16,16,128]{2,1,0:T(8,...) custom-call(f32[4,256,128]{2,1,0:T(8,128)} %bitcast.12, ...), custom_call_target="tpu_custom_call" | custom-call | flops 1000 | bytes 1048576 | tf_op jit(solution)/shard_map/pallas_call | solution.py:484
  1.6 1.7 %collective-permute-start.4 = (f32[5,4,16,128]{3,2,1,0:T(8,128)S(1)}, f32[5,4,16,128]{3,2,1,0:T(8,128)S(1)}, u32[]{:S(2)}, u32[]{:S(2)}) collective-permute-start(f32[5,4,16,128]{3,2,1,0:T(8,128)S(1)} %get-tuple-element.29), channel_id=1, source_target_pairs={{0,8},{8,16},{16,24},{24,0},{1,9},{9,17},{17,25},{25,1},{2,10},{10... | collective-permute-start | bytes 491528 | tf_op jit(solution)/shard_map/ppermute | solution.py:496
  3.3 1.7 %collective-permute-start.5 = (f32[5,4,16,128]{3,2,1,0:T(8,128)S(1)}, f32[5,4,16,128]{3,2,1,0:T(8,128)S(1)}, u32[]{:S(2)}, u32[]{:S(2)}) collective-permute-start(f32[5,4,16,128]{3,2,1,0:T(8,128)S(1)} %get-tuple-element.30), channel_id=1, source_target_pairs={{8,0},{16,8},{24,16},{0,24},{9,1},{17,9},{25,17},{1,25},{10,2},{18... | collective-permute-start | bytes 491528 | tf_op jit(solution)/shard_map/ppermute | solution.py:497
  4.9 0.7 %collective-permute-start = (f32[3,16,128]{2,1,0:T(8,128)S(1)}, f32[3,16,128]{2,1,0:T(8,128)S(1)}, u32[]{:S(2)}, u32[]{:S(2)}) collective-permute-start(f32[3,16,128]{2,1,0:T(8,128)S(1)} %get-tuple-element.23), channel_id=1, source_target_pairs={{1,2},{2,1},{3,4},{4,3},{5,6},{6,5},{9,10},{10,9},{11,12},{12,11},... | collective-permute-start | bytes 73736 | tf_op jit(solution)/shard_map/ppermute | solution.py:494
  5.6 4.3 %collective-permute-start.1 = (f32[3,16,128]{2,1,0:T(8,128)S(1)}, f32[3,16,128]{2,1,0:T(8,128)S(1)}, u32[]{:S(2)}, u32[]{:S(2)}) collective-permute-start(f32[3,16,128]{2,1,0:T(8,128)S(1)} %get-tuple-element.24), channel_id=1, source_target_pairs={{0,1},{1,0},{2,3},{3,2},{4,5},{5,4},{6,7},{7,6},{8,9},{9,8},{10,11... | collective-permute-start | bytes 73736 | tf_op jit(solution)/shard_map/ppermute | solution.py:495
  9.9 0.0 collective-permute-done.far_ref
  9.9 1.8 %collective-permute-done.1.near_ref = f32[3,16,128]{2,1,0:T(8,128)S(1)} collective-permute-done((f32[3,16,128]{2,1,0:T(8,128)S(1)}, f32[3,16,128]{2,1,0:T(8,128)S(1)}, u32[]{:S(2)}, u32[]{:S(2)}) %collective-permute-start.1) | collective-permute-done | bytes 24608 | tf_op jit(solution)/shard_map/ppermute | solution.py:495
  11.7 0.1 shard_map.65
  11.9 0.4 collective-permute-start.2
  12.3 2.9 %collective-permute-start.3 = (f32[5,16,128]{2,1,0:T(8,128)S(1)}, f32[5,16,128]{2,1,0:T(8,128)S(1)}, u32[]{:S(2)}, u32[]{:S(2)}) collective-permute-start(f32[5,16,128]{2,1,0:T(8,128)S(1)} %get-tuple-element.27), channel_id=1, source_target_pairs={{8,0},{16,8},{24,16},{0,24},{9,1},{17,9},{25,17},{1,25},{10,2},{18... | collective-permute-start | bytes 122888 | tf_op jit(solution)/shard_map/ppermute | solution.py:511
  15.8 0.2 shard_map.66.table_ref
  16.0 0.0 collective-permute-done.4.low_ref
  16.0 0.0 collective-permute-done.5.high_ref
  16.0 3.2 %shard_map.67 = (f32[4,16,4,16,128]{4,3,2,1,0:T(8,128)S(1)}, f32[13,8,128]{2,1,0:T(8,128)S(1)}) custom-call(f32[16,4,16,128]{3,2,1,0:T(8,128)S(1)} %get-tuple-element.28.own_ref, f32[5,4,16,128]{3,2,1,0:T(8,128)S(1)} %collective-permute-done.4.low_ref, f32[5,4,16,128]{3,2,1,0:T(8,128)S(1)} %collective-permute-done.5.high_ref, f32[40,128]{1,0:T(8,128)S(1)} %shard_map.66.table_ref), custom_call_target="tpu_custom_call" | custom-call | flops 10000000 | bytes 1048576 | tf_op jit(solution)/shard_map/pallas_call | solution.py:500
  19.3 0.0 collective-permute-done.2.low_ref
  19.3 0.0 collective-permute-done.3.high_ref
  19.3 1.6 %shard_map.68 = (f32[4,16,16,128]{3,2,1,0:T(8,128)S(1)}, f32[32,16]{1,0:T(8,128)S(1)}) custom-call(f32[16,16,128]{2,1,0:T(8,128)S(1)} %get-tuple-element.25.strip_ref, f32[5,16,128]{2,1,0:T(8,128)S(1)} %collective-permute-done.2.low_ref, f32[5,16,128]{2,1,0:T(8,128)S(1)} %collective-permute-done.3.high_ref, f32[13,8,128]{2,1,0:T(8,128)S(1)} %get-tuple-element.35.dots_in_ref, ...), custom_call_target="tpu_custom_call" | custom-call | flops 1000 | bytes 1048576 | tf_op jit(solution)/shard_map/pallas_call | solution.py:512
  20.9 25.4 %all_to_all.11 = f32[32,1,16]{2,1,0:T(1,128)S(1)} all-to-all(f32[32,1,16]{2,1,0:T(1,128)S(1)} %bitcast.11), channel_id=1, replica_groups=mesh['ens'=8,'gy'=4,'gh'=2,'gx'=4] {'gy','gh','gx'}, dimensions={0} | all-to-all | bytes 4096 | tf_op jit(solution)/shard_map/all_to_all | solution.py:518
  46.3 2.0 %shard_map.69 = f32[4,256,128]{2,1,0:T(8,128)} custom-call(f32[32,16]{1,0:T(8,128)S(1)} %bitcast.10, f32[4,16,4,16,128]{4,3,2,1,0:T(8,128)S(1)} %get-tuple-element.37.basis_ref, f32[4,16,16,128]{3,2,1,0:T(8,128)S(1)} %get-tuple-element.38.strip_ref), custom_call_target="tpu_custom_call" | custom-call | flops 1000 | bytes 1048576 | tf_op jit(solution)/shard_map/pallas_call | solution.py:519
Async XLA Ops:
  1.6 14.4 %collective-permute-start.4 = (f32[5,4,16,128]{3,2,1,0:T(8,128)S(1)}, f32[5,4,16,128]{3,2,1,0:T(8,128)S(1)}, u32[]{:S(2)}, u32[]{:S(2)}) collective-permute-start(f32[5,4,16,128]{3,2,1,0:T(8,128)S(1)} %get-tuple-element.29), channel_id=1, source_target_pairs={{0,8},{8,16},{16,24},{24,0},{1,9},{9,17},{17,25},{25,1},{2,10},{10... | collective-permute-start | bytes 491528 | tf_op jit(solution)/shard_map/ppermute | solution.py:496
  3.3 12.7 %collective-permute-start.5 = (f32[5,4,16,128]{3,2,1,0:T(8,128)S(1)}, f32[5,4,16,128]{3,2,1,0:T(8,128)S(1)}, u32[]{:S(2)}, u32[]{:S(2)}) collective-permute-start(f32[5,4,16,128]{3,2,1,0:T(8,128)S(1)} %get-tuple-element.30), channel_id=1, source_target_pairs={{8,0},{16,8},{24,16},{0,24},{9,1},{17,9},{25,17},{1,25},{10,2},{18... | collective-permute-start | bytes 491528 | tf_op jit(solution)/shard_map/ppermute | solution.py:497
  4.9 5.0 %collective-permute-start = (f32[3,16,128]{2,1,0:T(8,128)S(1)}, f32[3,16,128]{2,1,0:T(8,128)S(1)}, u32[]{:S(2)}, u32[]{:S(2)}) collective-permute-start(f32[3,16,128]{2,1,0:T(8,128)S(1)} %get-tuple-element.23), channel_id=1, source_target_pairs={{1,2},{2,1},{3,4},{4,3},{5,6},{6,5},{9,10},{10,9},{11,12},{12,11},... | collective-permute-start | bytes 73736 | tf_op jit(solution)/shard_map/ppermute | solution.py:494
  5.6 6.1 %collective-permute-start.1 = (f32[3,16,128]{2,1,0:T(8,128)S(1)}, f32[3,16,128]{2,1,0:T(8,128)S(1)}, u32[]{:S(2)}, u32[]{:S(2)}) collective-permute-start(f32[3,16,128]{2,1,0:T(8,128)S(1)} %get-tuple-element.24), channel_id=1, source_target_pairs={{0,1},{1,0},{2,3},{3,2},{4,5},{5,4},{6,7},{7,6},{8,9},{9,8},{10,11... | collective-permute-start | bytes 73736 | tf_op jit(solution)/shard_map/ppermute | solution.py:495
  11.9 7.4 %collective-permute-start.2 = (f32[5,16,128]{2,1,0:T(8,128)S(1)}, f32[5,16,128]{2,1,0:T(8,128)S(1)}, u32[]{:S(2)}, u32[]{:S(2)}) collective-permute-start(f32[5,16,128]{2,1,0:T(8,128)S(1)} %get-tuple-element.26), channel_id=1, source_target_pairs={{0,8},{8,16},{16,24},{24,0},{1,9},{9,17},{17,25},{25,1},{2,10},{10... | collective-permute-start | bytes 122888 | tf_op jit(solution)/shard_map/ppermute | solution.py:510
  12.3 7.0 %collective-permute-start.3 = (f32[5,16,128]{2,1,0:T(8,128)S(1)}, f32[5,16,128]{2,1,0:T(8,128)S(1)}, u32[]{:S(2)}, u32[]{:S(2)}) collective-permute-start(f32[5,16,128]{2,1,0:T(8,128)S(1)} %get-tuple-element.27), channel_id=1, source_target_pairs={{8,0},{16,8},{24,16},{0,24},{9,1},{17,9},{25,17},{1,25},{10,2},{18... | collective-permute-start | bytes 122888 | tf_op jit(solution)/shard_map/ppermute | solution.py:511

commit v7 on v6

--- a/solution.py
+++ b/solution.py
@@ -16,8 +16,8 @@
 ROWS = Y + 2 * HALO
 DOTS = 13
 SLOTS = 16
-MAIN_SOURCE, MAIN_LEVEL, MAIN_DOT = 8, (11, 10, 9, 8), 4
-STRIP_SOURCE, STRIP_LEVEL, STRIP_DOT = 12, (11, 10, 9, 8), 4
+MAIN_SOURCE, MAIN_LEVEL, MAIN_DOT = 24, (22, 20, 18, 16), 16
+STRIP_SOURCE, STRIP_LEVEL, STRIP_DOT = 24, (22, 20, 18, 16), 4
 
 F32 = jnp.float32
 VMEM = pltpu.VMEM
@@ -421,7 +421,11 @@
 
 def combine_kernel(sums_ref, basis_ref, strip_ref, out_ref, held, strips, sems):
     total = jnp.sum(sums_ref[...], axis=0, keepdims=True)
-    h00, h01, h03, h04, h11, h12, h13, h14, h22, h23, h33, h34, h44 = (total[:, k : k + 1] for k in range(DOTS))
+    slot = lax.broadcasted_iota(jnp.int32, (1, SLOTS), 1)
+    total = jnp.where(slot == DOTS, sums_ref[0:1, :], total)
+    h00, h01, h03, h04, h11, h12, h13, h14, h22, h23, h33, h34, h44, reach = (
+        jnp.broadcast_to(total[:, k : k + 1], (8, Z)) for k in range(DOTS + 1)
+    )
     h = [
         [h00, h01, h11, h03, h04],
         [None, h11, h12, h13, h14],
@@ -429,7 +433,7 @@
         [None, None, None, h33, h34],
         [None, None, None, None, h44],
     ]
-    y = [jnp.broadcast_to(c, (X, Z)) for c in least_squares(h, sums_ref[0:1, DOTS : DOTS + 1])]
+    y = [jnp.concatenate([c, c]) for c in least_squares(h, reach)]
     lane = lanes()
     for row in range(Y):
         strip = y[0] * strip_ref[0, row]

time: 48.4 us -> 47.1 us (0.973)
  Pallas kernels: 8.72 us -> 6.52 us
  blocking collectives: 25.4 us -> 26.3 us
    pallas_call x1, Pallas kernels: 3.25 us -> 2.43 us  [shards(): call(main_kernel, (struct(4, Y, *wide), struct(DOTS, 8, Z)), [VMEM] * 4,...]
    all_to_all x1, blocking collectives: 25.4 us -> 26.3 us  [shards(): lax.all_to_all(total, ('gy', *GZ), split_axis=0, concat_axis=0, tiled=True)]
    pallas_call x1, Pallas kernels: 1.97 us -> 1.25 us  [shards(): call(combine_kernel, struct(SPECIES, X * Y, Z), [VMEM] * 3, [VMEM((SPECIE...]
    pallas_call x1, Pallas kernels: 1.56 us -> 0.91 us  [shards(): call(strip_kernel, (struct(4, Y, X, Z), struct(gy * gz, SLOTS)), [VMEM] *...]
  transfers between devices with their start and end apart: 6 -> 6, of which waited for: 1 -> 1; matrix products, arithmetic and copies ran while one was open for 0% -> 0% of each run, Pallas kernels for 7% -> 6%
where the time goes in v7:
time: 47.1 us; the launch traced here: 46.9 us
  blocking collectives  26.3 us (56%)
  starting transfers between devices  11.6 us (25%)
  Pallas kernels  6.52 us (14%)
  waiting for transfers between devices  1.82 us (4%)
  between operations  0.71 us (2%)
    all_to_all x1, blocking collectives, shards(): lax.all_to_all(total, ('gy', *GZ), split_axis=0, concat_axis=0, tiled=True)  26.3 us
    ppermute x1, starting transfers between devices, shards(): from_near = lax.ppermute(to_near, GZ, near)  4.31 us
    ppermute x1, starting transfers between devices, shards(): strip_high = lax.ppermute(strip_top, 'gy', down)  2.87 us
    pallas_call x1, Pallas kernels, shards(): call(main_kernel, (struct(4, Y, *wide), struct(DOTS, 8, Z)), [VMEM] * 4,...  2.43 us
    ppermute x1, waiting for transfers between devices, shards(): from_near = lax.ppermute(to_near, GZ, near)  1.8 us
    ppermute x1, starting transfers between devices, shards(): high = lax.ppermute(top, 'gy', down)  1.66 us
    ppermute x1, starting transfers between devices, shards(): low = lax.ppermute(bottom, 'gy', up)  1.65 us
    pallas_call x1, Pallas kernels, shards(): call(pack_kernel, (struct(Y, SPECIES, X, Z), edge, edge, struct(Y, X, Z),...  1.62 us
  transfers between devices with their start and end apart: 6, of which 1 were waited for; matrix products, arithmetic and copies ran while one was open for 0% of the time, Pallas kernels for 6%

profile of v7, /device:TPU:32, one launch (start us, length us, event | category | flops | bytes accessed | tf_op | source)
XLA Modules:
  0.0 46.9 jit_solution(3464758405581565623)
XLA Ops:
  0.0 1.6 %shard_map.64 = (f32[16,4,16,128]{3,2,1,0:T(8,128)S(1)}, f32[5,4,16,128]{3,2,1,0:T(8,128)S(1)}, f32[5,4,16,128]{3,2,1,0:T(8,128)S(1)}, f32[16,16,128]{2,1,0:T(8,...) custom-call(f32[4,256,128]{2,1,0:T(8,128)} %bitcast.12, ...), custom_call_target="tpu_custom_call" | custom-call | flops 1000 | bytes 1048576 | tf_op jit(solution)/shard_map/pallas_call | solution.py:488
  1.6 1.7 %collective-permute-start.4 = (f32[5,4,16,128]{3,2,1,0:T(8,128)S(1)}, f32[5,4,16,128]{3,2,1,0:T(8,128)S(1)}, u32[]{:S(2)}, u32[]{:S(2)}) collective-permute-start(f32[5,4,16,128]{3,2,1,0:T(8,128)S(1)} %get-tuple-element.29), channel_id=1, source_target_pairs={{0,8},{8,16},{16,24},{24,0},{1,9},{9,17},{17,25},{25,1},{2,10},{10... | collective-permute-start | bytes 491528 | tf_op jit(solution)/shard_map/ppermute | solution.py:500
  3.3 1.7 %collective-permute-start.5 = (f32[5,4,16,128]{3,2,1,0:T(8,128)S(1)}, f32[5,4,16,128]{3,2,1,0:T(8,128)S(1)}, u32[]{:S(2)}, u32[]{:S(2)}) collective-permute-start(f32[5,4,16,128]{3,2,1,0:T(8,128)S(1)} %get-tuple-element.30), channel_id=1, source_target_pairs={{8,0},{16,8},{24,16},{0,24},{9,1},{17,9},{25,17},{1,25},{10,2},{18... | collective-permute-start | bytes 491528 | tf_op jit(solution)/shard_map/ppermute | solution.py:501
  4.9 0.7 %collective-permute-start = (f32[3,16,128]{2,1,0:T(8,128)S(1)}, f32[3,16,128]{2,1,0:T(8,128)S(1)}, u32[]{:S(2)}, u32[]{:S(2)}) collective-permute-start(f32[3,16,128]{2,1,0:T(8,128)S(1)} %get-tuple-element.23), channel_id=1, source_target_pairs={{1,2},{2,1},{3,4},{4,3},{5,6},{6,5},{9,10},{10,9},{11,12},{12,11},... | collective-permute-start | bytes 73736 | tf_op jit(solution)/shard_map/ppermute | solution.py:498
  5.6 4.3 %collective-permute-start.1 = (f32[3,16,128]{2,1,0:T(8,128)S(1)}, f32[3,16,128]{2,1,0:T(8,128)S(1)}, u32[]{:S(2)}, u32[]{:S(2)}) collective-permute-start(f32[3,16,128]{2,1,0:T(8,128)S(1)} %get-tuple-element.24), channel_id=1, source_target_pairs={{0,1},{1,0},{2,3},{3,2},{4,5},{5,4},{6,7},{7,6},{8,9},{9,8},{10,11... | collective-permute-start | bytes 73736 | tf_op jit(solution)/shard_map/ppermute | solution.py:499
  9.9 0.0 collective-permute-done.far_ref
  9.9 1.8 %collective-permute-done.1.near_ref = f32[3,16,128]{2,1,0:T(8,128)S(1)} collective-permute-done((f32[3,16,128]{2,1,0:T(8,128)S(1)}, f32[3,16,128]{2,1,0:T(8,128)S(1)}, u32[]{:S(2)}, u32[]{:S(2)}) %collective-permute-start.1) | collective-permute-done | bytes 24608 | tf_op jit(solution)/shard_map/ppermute | solution.py:499
  11.7 0.1 shard_map.65
  11.9 0.4 collective-permute-start.2
  12.3 2.9 %collective-permute-start.3 = (f32[5,16,128]{2,1,0:T(8,128)S(1)}, f32[5,16,128]{2,1,0:T(8,128)S(1)}, u32[]{:S(2)}, u32[]{:S(2)}) collective-permute-start(f32[5,16,128]{2,1,0:T(8,128)S(1)} %get-tuple-element.27), channel_id=1, source_target_pairs={{8,0},{16,8},{24,16},{0,24},{9,1},{17,9},{25,17},{1,25},{10,2},{18... | collective-permute-start | bytes 122888 | tf_op jit(solution)/shard_map/ppermute | solution.py:515
  15.8 0.2 shard_map.66.table_ref
  16.0 0.0 collective-permute-done.4.low_ref
  16.0 0.0 collective-permute-done.5.high_ref
  16.0 2.4 %shard_map.67 = (f32[4,16,4,16,128]{4,3,2,1,0:T(8,128)S(1)}, f32[13,8,128]{2,1,0:T(8,128)S(1)}) custom-call(f32[16,4,16,128]{3,2,1,0:T(8,128)S(1)} %get-tuple-element.28.own_ref, f32[5,4,16,128]{3,2,1,0:T(8,128)S(1)} %collective-permute-done.4.low_ref, f32[5,4,16,128]{3,2,1,0:T(8,128)S(1)} %collective-permute-done.5.high_ref, f32[40,128]{1,0:T(8,128)S(1)} %shard_map.66.table_ref), custom_call_target="tpu_custom_call" | custom-call | flops 10000000 | bytes 1048576 | tf_op jit(solution)/shard_map/pallas_call | solution.py:504
  18.5 0.0 collective-permute-done.2.low_ref
  18.5 0.0 collective-permute-done.3.high_ref
  18.5 0.9 %shard_map.68 = (f32[4,16,16,128]{3,2,1,0:T(8,128)S(1)}, f32[32,16]{1,0:T(8,128)S(1)}) custom-call(f32[16,16,128]{2,1,0:T(8,128)S(1)} %get-tuple-element.25.strip_ref, f32[5,16,128]{2,1,0:T(8,128)S(1)} %collective-permute-done.2.low_ref, f32[5,16,128]{2,1,0:T(8,128)S(1)} %collective-permute-done.3.high_ref, f32[13,8,128]{2,1,0:T(8,128)S(1)} %get-tuple-element.35.dots_in_ref, ...), custom_call_target="tpu_custom_call" | custom-call | flops 1000 | bytes 1048576 | tf_op jit(solution)/shard_map/pallas_call | solution.py:516
  19.4 26.3 %all_to_all.11 = f32[32,1,16]{2,1,0:T(1,128)S(1)} all-to-all(f32[32,1,16]{2,1,0:T(1,128)S(1)} %bitcast.11), channel_id=1, replica_groups=mesh['ens'=8,'gy'=4,'gh'=2,'gx'=4] {'gy','gh','gx'}, dimensions={0} | all-to-all | bytes 4096 | tf_op jit(solution)/shard_map/all_to_all | solution.py:522
  45.7 1.3 %shard_map.69 = f32[4,256,128]{2,1,0:T(8,128)} custom-call(f32[32,16]{1,0:T(8,128)S(1)} %bitcast.10, f32[4,16,4,16,128]{4,3,2,1,0:T(8,128)S(1)} %get-tuple-element.37.basis_ref, f32[4,16,16,128]{3,2,1,0:T(8,128)S(1)} %get-tuple-element.38.strip_ref), custom_call_target="tpu_custom_call" | custom-call | flops 1000 | bytes 1048576 | tf_op jit(solution)/shard_map/pallas_call | solution.py:523
Async XLA Ops:
  1.6 14.4 %collective-permute-start.4 = (f32[5,4,16,128]{3,2,1,0:T(8,128)S(1)}, f32[5,4,16,128]{3,2,1,0:T(8,128)S(1)}, u32[]{:S(2)}, u32[]{:S(2)}) collective-permute-start(f32[5,4,16,128]{3,2,1,0:T(8,128)S(1)} %get-tuple-element.29), channel_id=1, source_target_pairs={{0,8},{8,16},{16,24},{24,0},{1,9},{9,17},{17,25},{25,1},{2,10},{10... | collective-permute-start | bytes 491528 | tf_op jit(solution)/shard_map/ppermute | solution.py:500
  3.3 12.7 %collective-permute-start.5 = (f32[5,4,16,128]{3,2,1,0:T(8,128)S(1)}, f32[5,4,16,128]{3,2,1,0:T(8,128)S(1)}, u32[]{:S(2)}, u32[]{:S(2)}) collective-permute-start(f32[5,4,16,128]{3,2,1,0:T(8,128)S(1)} %get-tuple-element.30), channel_id=1, source_target_pairs={{8,0},{16,8},{24,16},{0,24},{9,1},{17,9},{25,17},{1,25},{10,2},{18... | collective-permute-start | bytes 491528 | tf_op jit(solution)/shard_map/ppermute | solution.py:501
  4.9 5.0 %collective-permute-start = (f32[3,16,128]{2,1,0:T(8,128)S(1)}, f32[3,16,128]{2,1,0:T(8,128)S(1)}, u32[]{:S(2)}, u32[]{:S(2)}) collective-permute-start(f32[3,16,128]{2,1,0:T(8,128)S(1)} %get-tuple-element.23), channel_id=1, source_target_pairs={{1,2},{2,1},{3,4},{4,3},{5,6},{6,5},{9,10},{10,9},{11,12},{12,11},... | collective-permute-start | bytes 73736 | tf_op jit(solution)/shard_map/ppermute | solution.py:498
  5.6 6.1 %collective-permute-start.1 = (f32[3,16,128]{2,1,0:T(8,128)S(1)}, f32[3,16,128]{2,1,0:T(8,128)S(1)}, u32[]{:S(2)}, u32[]{:S(2)}) collective-permute-start(f32[3,16,128]{2,1,0:T(8,128)S(1)} %get-tuple-element.24), channel_id=1, source_target_pairs={{0,1},{1,0},{2,3},{3,2},{4,5},{5,4},{6,7},{7,6},{8,9},{9,8},{10,11... | collective-permute-start | bytes 73736 | tf_op jit(solution)/shard_map/ppermute | solution.py:499
  11.9 6.6 %collective-permute-start.2 = (f32[5,16,128]{2,1,0:T(8,128)S(1)}, f32[5,16,128]{2,1,0:T(8,128)S(1)}, u32[]{:S(2)}, u32[]{:S(2)}) collective-permute-start(f32[5,16,128]{2,1,0:T(8,128)S(1)} %get-tuple-element.26), channel_id=1, source_target_pairs={{0,8},{8,16},{16,24},{24,0},{1,9},{9,17},{17,25},{25,1},{2,10},{10... | collective-permute-start | bytes 122888 | tf_op jit(solution)/shard_map/ppermute | solution.py:514
  12.3 6.2 %collective-permute-start.3 = (f32[5,16,128]{2,1,0:T(8,128)S(1)}, f32[5,16,128]{2,1,0:T(8,128)S(1)}, u32[]{:S(2)}, u32[]{:S(2)}) collective-permute-start(f32[5,16,128]{2,1,0:T(8,128)S(1)} %get-tuple-element.27), channel_id=1, source_target_pairs={{8,0},{16,8},{24,16},{0,24},{9,1},{17,9},{25,17},{1,25},{10,2},{18... | collective-permute-start | bytes 122888 | tf_op jit(solution)/shard_map/ppermute | solution.py:515

commit v8 on v7

--- a/solution.py
+++ b/solution.py
@@ -104,6 +104,10 @@
         return low if row < before else high if row >= before + Y else 1.0
     flag = jnp.where(row < before, low, 1.0)
     return jnp.where(row >= before + Y, high, flag)
+
+
+def times(value, flag):
+    return value if isinstance(flag, float) else value * flag
 
 
 PLUS, MINUS, LINEAR, QUAD, SCALE, TURNED, STRIP_QUAD, STRIP_SCALE, RANGE = 0, 3, 6, 22, 26, 30, 34, 35, 36
@@ -157,48 +161,48 @@
     put(RANGE, reach)
 
 
-def pack_kernel(
-    state_ref, courant_ref, diffusion_ref, reaction_ref, quadratic_ref,
-    own_ref, top_ref, bottom_ref, strip_ref, far_ref, near_ref, courant, diffusion, reaction, quadratic,
-    state, state_sems, sems,
-):
-    blocks = [pltpu.make_async_copy(state_ref.at[s], state.at[s], state_sems.at[s]) for s in range(SPECIES)]
-    tables = (
-        (courant_ref, courant), (diffusion_ref, diffusion), (reaction_ref, reaction),
-        (quadratic_ref, quadratic),
-    )
-    copies = [pltpu.make_async_copy(a, b, sems.at[i]) for i, (a, b) in enumerate(tables)]
-    for copy in blocks + copies:
-        copy.start()
+def edge_kernel(state_ref, strip_ref, far_ref, near_ref):
     lane = lanes()
     odd = z_index() % 2 == 1
     place = lane % 32
-    for s in range(SPECIES):
-        blocks[s].wait()
-        for y in range(Y):
-            v = state[s, pl.ds(y, X, stride=Y), :]
+    lows = [jnp.zeros((X, Z), F32)] * PACKS
+    highs = [jnp.zeros((X, Z), F32)] * PACKS
+    for y in range(Y):
+        total = jnp.zeros((X, Z), F32)
+        for s in range(SPECIES):
+            v = state_ref[s, pl.ds(y, X, stride=Y), :]
+            low = shift(v, 32 * s + HALO)
+            high = shift(v, 32 * s + 16 - (Z - 11))
+            total = jnp.where((lane >= 32 * s + HALO) & (lane < 32 * s + 16), low, total)
+            total = jnp.where((lane >= 32 * s + 16) & (lane < 32 * s + 27), high, total)
+        strip_ref[y] = total
+    for g in range(PACKS):
+        for i in range(GROUP):
+            if g * GROUP + i < Y:
+                v = strip_ref[g * GROUP + i]
+                here = (place >= i * HALO) & (place < (i + 1) * HALO)
+                lows[g] = jnp.where(here, shift(v, i * HALO - HALO), lows[g])
+                highs[g] = jnp.where(here, shift(v, i * HALO - 22), highs[g])
+        far_ref[g] = jnp.where(odd, highs[g], lows[g])
+        near_ref[g] = jnp.where(odd, lows[g], highs[g])
+
+
+def row_kernel(
+    state_ref, courant_ref, diffusion_ref, reaction_ref, quadratic_ref,
+    own_ref, top_ref, bottom_ref, courant, diffusion, reaction, quadratic, sems,
+):
+    tables = ((courant_ref, courant), (diffusion_ref, diffusion), (reaction_ref, reaction), (quadratic_ref, quadratic))
+    copies = [pltpu.make_async_copy(a, b, sems.at[i]) for i, (a, b) in enumerate(tables)]
+    for copy in copies:
+        copy.start()
+    for y in range(Y):
+        for s in range(SPECIES):
+            v = state_ref[s, pl.ds(y, X, stride=Y), :]
             own_ref[y, s] = v
             if y < HALO:
                 top_ref[y, s] = v
             if y >= Y - HALO:
                 bottom_ref[y - (Y - HALO), s] = v
-            total = strip_ref[y] if s else jnp.zeros((X, Z), F32)
-            low = shift(v, 32 * s + HALO)
-            high = shift(v, 32 * s + 16 - (Z - 11))
-            total = jnp.where((lane >= 32 * s + HALO) & (lane < 32 * s + 16), low, total)
-            total = jnp.where((lane >= 32 * s + 16) & (lane < 32 * s + 27), high, total)
-            strip_ref[y] = total
-    for g in range(PACKS):
-        lows = jnp.zeros((X, Z), F32)
-        highs = jnp.zeros((X, Z), F32)
-        for i in range(GROUP):
-            if g * GROUP + i < Y:
-                v = strip_ref[g * GROUP + i]
-                here = (place >= i * HALO) & (place < (i + 1) * HALO)
-                lows = jnp.where(here, shift(v, i * HALO - HALO), lows)
-                highs = jnp.where(here, shift(v, i * HALO - 22), highs)
-        far_ref[g] = jnp.where(odd, highs, lows)
-        near_ref[g] = jnp.where(odd, lows, highs)
     for copy in copies:
         copy.wait()
 
@@ -251,7 +255,7 @@
             out = out + (plus[2] * shift(v[k], 1) - minus[2] * shift(v[k], -1))
             for l in range(SPECIES):
                 out = out + linear[k][l] * v[l]
-            b0[row, k] = (out + quad[k] * coupled) * flag
+            b0[row, k] = times(out + quad[k] * coupled, flag)
         return _
 
     over_rows(Y + 8, MAIN_SOURCE, source_row)
@@ -273,7 +277,7 @@
             for s in range(SPECIES):
                 image, v = image_of(buffers[k - 1], row, s)
                 value = level_value(k, image, v, buffers[2][row + 2, s] if k == 4 else None)
-                buffers[k][row, s] = value * flag if before else value
+                buffers[k][row, s] = times(value, flag)
             return _
 
         over_rows(Y + 2 * before, MAIN_LEVEL[k - 1], level_row)
@@ -330,7 +334,7 @@
         out = out + (plus[2] * shift(v, 1) - minus[2] * shift(v, -1))
         for t in range(SPECIES):
             out = out + linear[t] * turned[t]
-        b0[row] = (out + quad * coupled) * (flag * inside)
+        b0[row] = times(out + quad * coupled, flag) * inside
         return _
 
     over_rows(Y + 8, STRIP_SOURCE, source_row)
@@ -351,7 +355,7 @@
             flag = row_flag(row, before, low, high)
             image, v = image_of(buffers[k - 1], row)
             value = level_value(k, image, v, buffers[2][row + 2] if k == 4 else None)
-            buffers[k][row] = value * (flag * inside) if before else value
+            buffers[k][row] = times(value, flag) * inside if before else value
             return _
 
         over_rows(Y + 2 * before, STRIP_LEVEL[k - 1], level_row)
@@ -484,17 +488,14 @@
     edge = struct(HALO, SPECIES, X, Z)
     strip_edge = struct(HALO, X, Z)
     pack = struct(PACKS, X, Z)
-    inputs = (flat, courant_table.T, diffusion_table.T, reaction_table.transpose(1, 2, 0), quadratic_table.T)
-    own, top, bottom, strip, to_far, to_near, *tables = call(
-        pack_kernel,
-        (struct(Y, SPECIES, X, Z), edge, edge, struct(Y, X, Z), pack, pack, *(struct(*t.shape) for t in inputs[1:])),
-        [pltpu.HBM] * len(inputs),
-        [
-            VMEM(flat.shape, F32),
-            pltpu.SemaphoreType.DMA((SPECIES,)),
-            pltpu.SemaphoreType.DMA((len(inputs) - 1,)),
-        ],
-    )(*(pltpu.with_memory_space_constraint(t, pltpu.HBM) for t in inputs))
+    inputs = (courant_table.T, diffusion_table.T, reaction_table.transpose(1, 2, 0), quadratic_table.T)
+    strip, to_far, to_near = call(edge_kernel, (struct(Y, X, Z), pack, pack), [VMEM])(flat)
+    own, top, bottom, *tables = call(
+        row_kernel,
+        (struct(Y, SPECIES, X, Z), edge, edge, *(struct(*t.shape) for t in inputs)),
+        [VMEM] + [pltpu.HBM] * len(inputs),
+        [pltpu.SemaphoreType.DMA((len(inputs),))],
+    )(flat, *(pltpu.with_memory_space_constraint(t, pltpu.HBM) for t in inputs))
     from_far = lax.ppermute(to_far, GZ, far)
     from_near = lax.ppermute(to_near, GZ, near)
     low = lax.ppermute(bottom, "gy", up)

time: 47.1 us -> 47.7 us (1.013)
  local copies, waits for them, and re-layouts: 0 us -> 1.04 us
    unnamed x0 -> x2, local copies, waits for them, and re-layouts: none -> 1.04 us
    pallas_call x1 -> x2, Pallas kernels: 1.62 us -> 1.17 us  [the longest x1 0.76 us: shards(): call(row_kernel, (struct(Y, SPECIES, X, Z), edge, edge, *(struct(*t.shape...]
  transfers between devices with their start and end apart: 6 -> 6, of which waited for: 1 -> 1; matrix products, arithmetic and copies ran while one was open for 0% -> 0% of each run, Pallas kernels for 6% -> 7%
where the time goes in v8:
time: 47.7 us; the launch traced here: 47.5 us
  blocking collectives  26.3 us (55%)
  starting transfers between devices  11.6 us (24%)
  Pallas kernels  6.09 us (13%)
  waiting for transfers between devices  1.82 us (4%)
  local copies, waits for them, and re-layouts  1.04 us (2%)
  between operations  0.72 us (2%)
    all_to_all x1, blocking collectives, shards(): lax.all_to_all(total, ('gy', *GZ), split_axis=0, concat_axis=0, tiled=True)  26.3 us
    ppermute x1, starting transfers between devices, shards(): from_near = lax.ppermute(to_near, GZ, near)  4.31 us
    ppermute x1, starting transfers between devices, shards(): strip_high = lax.ppermute(strip_top, 'gy', down)  2.87 us
    pallas_call x1, Pallas kernels, shards(): call(main_kernel, (struct(4, Y, *wide), struct(DOTS, 8, Z)), [VMEM] * 4,...  2.43 us
    ppermute x1, waiting for transfers between devices, shards(): from_near = lax.ppermute(to_near, GZ, near)  1.8 us
    ppermute x1, starting transfers between devices, shards(): high = lax.ppermute(top, 'gy', down)  1.66 us
    ppermute x1, starting transfers between devices, shards(): low = lax.ppermute(bottom, 'gy', up)  1.65 us
    pallas_call x1, Pallas kernels, shards(): call(combine_kernel, struct(SPECIES, X * Y, Z), [VMEM] * 3, [VMEM((SPECIE...  1.25 us
  transfers between devices with their start and end apart: 6, of which 1 were waited for; matrix products, arithmetic and copies ran while one was open for 0% of the time, Pallas kernels for 7%

profile of v8, /device:TPU:32, one launch (start us, length us, event | category | flops | bytes accessed | tf_op | source)
XLA Modules:
  0.0 47.5 jit_solution(10865758287652775443)
XLA Ops:
  0.0 0.0 copy-start
  0.0 1.0 %copy-done = f32[1,4,16,16,128]{4,3,2,1,0:T(8,128)S(1)} copy-done((f32[1,4,16,16,128]{4,3,2,1,0:T(8,128)S(1)}, f32[1,4,16,16,128]{4,3,2,1,0:T(8,128)}, u32[]{:S(2)}) %copy-start) | copy-done | bytes 524312
  1.0 0.8 %shard_map.66 = (f32[16,4,16,128]{3,2,1,0:T(8,128)S(1)}, f32[5,4,16,128]{3,2,1,0:T(8,128)S(1)}, f32[5,4,16,128]{3,2,1,0:T(8,128)S(1)}, f32[3,16]{1,0:T(4,128)S(1...) custom-call(f32[4,256,128]{2,1,0:T(8,128)S(1)} %bitcast.10, f32[3,16]{1,0:T(4,128)} %bitcast.15, ...), custom_call_target="tpu_custom_call" | custom-call | flops 1000 | bytes 1048576 | tf_op jit(solution)/shard_map/pallas_call | solution.py:493
  1.8 1.7 %collective-permute-start.4 = (f32[5,4,16,128]{3,2,1,0:T(8,128)S(1)}, f32[5,4,16,128]{3,2,1,0:T(8,128)S(1)}, u32[]{:S(2)}, u32[]{:S(2)}) collective-permute-start(f32[5,4,16,128]{3,2,1,0:T(8,128)S(1)} %get-tuple-element.29), channel_id=1, source_target_pairs={{0,8},{8,16},{16,24},{24,0},{1,9},{9,17},{17,25},{25,1},{2,10},{10... | collective-permute-start | bytes 491528 | tf_op jit(solution)/shard_map/ppermute | solution.py:501
  3.5 1.7 %collective-permute-start.5 = (f32[5,4,16,128]{3,2,1,0:T(8,128)S(1)}, f32[5,4,16,128]{3,2,1,0:T(8,128)S(1)}, u32[]{:S(2)}, u32[]{:S(2)}) collective-permute-start(f32[5,4,16,128]{3,2,1,0:T(8,128)S(1)} %get-tuple-element.30), channel_id=1, source_target_pairs={{8,0},{16,8},{24,16},{0,24},{9,1},{17,9},{25,17},{1,25},{10,2},{18... | collective-permute-start | bytes 491528 | tf_op jit(solution)/shard_map/ppermute | solution.py:502
  5.1 0.4 shard_map.64
  5.5 0.7 %collective-permute-start = (f32[3,16,128]{2,1,0:T(8,128)S(1)}, f32[3,16,128]{2,1,0:T(8,128)S(1)}, u32[]{:S(2)}, u32[]{:S(2)}) collective-permute-start(f32[3,16,128]{2,1,0:T(8,128)S(1)} %get-tuple-element.23), channel_id=1, source_target_pairs={{1,2},{2,1},{3,4},{4,3},{5,6},{6,5},{9,10},{10,9},{11,12},{12,11},... | collective-permute-start | bytes 73736 | tf_op jit(solution)/shard_map/ppermute | solution.py:499
  6.2 4.3 %collective-permute-start.1 = (f32[3,16,128]{2,1,0:T(8,128)S(1)}, f32[3,16,128]{2,1,0:T(8,128)S(1)}, u32[]{:S(2)}, u32[]{:S(2)}) collective-permute-start(f32[3,16,128]{2,1,0:T(8,128)S(1)} %get-tuple-element.24), channel_id=1, source_target_pairs={{0,1},{1,0},{2,3},{3,2},{4,5},{5,4},{6,7},{7,6},{8,9},{9,8},{10,11... | collective-permute-start | bytes 73736 | tf_op jit(solution)/shard_map/ppermute | solution.py:500
  10.5 0.0 collective-permute-done.far_ref
  10.5 1.8 %collective-permute-done.1.near_ref = f32[3,16,128]{2,1,0:T(8,128)S(1)} collective-permute-done((f32[3,16,128]{2,1,0:T(8,128)S(1)}, f32[3,16,128]{2,1,0:T(8,128)S(1)}, u32[]{:S(2)}, u32[]{:S(2)}) %collective-permute-start.1) | collective-permute-done | bytes 24608 | tf_op jit(solution)/shard_map/ppermute | solution.py:500
  12.3 0.1 shard_map.65
  12.5 0.4 collective-permute-start.2
  12.9 2.9 %collective-permute-start.3 = (f32[5,16,128]{2,1,0:T(8,128)S(1)}, f32[5,16,128]{2,1,0:T(8,128)S(1)}, u32[]{:S(2)}, u32[]{:S(2)}) collective-permute-start(f32[5,16,128]{2,1,0:T(8,128)S(1)} %get-tuple-element.27), channel_id=1, source_target_pairs={{8,0},{16,8},{24,16},{0,24},{9,1},{17,9},{25,17},{1,25},{10,2},{18... | collective-permute-start | bytes 122888 | tf_op jit(solution)/shard_map/ppermute | solution.py:516
  16.4 0.2 shard_map.67.table_ref
  16.6 0.0 collective-permute-done.4.low_ref
  16.6 0.0 collective-permute-done.5.high_ref
  16.6 2.4 %shard_map.68 = (f32[4,16,4,16,128]{4,3,2,1,0:T(8,128)S(1)}, f32[13,8,128]{2,1,0:T(8,128)S(1)}) custom-call(f32[16,4,16,128]{3,2,1,0:T(8,128)S(1)} %get-tuple-element.28.own_ref, f32[5,4,16,128]{3,2,1,0:T(8,128)S(1)} %collective-permute-done.4.low_ref, f32[5,4,16,128]{3,2,1,0:T(8,128)S(1)} %collective-permute-done.5.high_ref, f32[40,128]{1,0:T(8,128)S(1)} %shard_map.67.table_ref), custom_call_target="tpu_custom_call" | custom-call | flops 10000000 | bytes 1048576 | tf_op jit(solution)/shard_map/pallas_call | solution.py:505
  19.1 0.0 collective-permute-done.2.low_ref
  19.1 0.0 collective-permute-done.3.high_ref
  19.1 0.9 %shard_map.69 = (f32[4,16,16,128]{3,2,1,0:T(8,128)S(1)}, f32[32,16]{1,0:T(8,128)S(1)}) custom-call(f32[16,16,128]{2,1,0:T(8,128)S(1)} %get-tuple-element.25.strip_ref, f32[5,16,128]{2,1,0:T(8,128)S(1)} %collective-permute-done.2.low_ref, f32[5,16,128]{2,1,0:T(8,128)S(1)} %collective-permute-done.3.high_ref, f32[13,8,128]{2,1,0:T(8,128)S(1)} %get-tuple-element.35.dots_in_ref, ...), custom_call_target="tpu_custom_call" | custom-call | flops 1000 | bytes 1048576 | tf_op jit(solution)/shard_map/pallas_call | solution.py:517
  20.0 26.3 %all_to_all.11 = f32[32,1,16]{2,1,0:T(1,128)S(1)} all-to-all(f32[32,1,16]{2,1,0:T(1,128)S(1)} %bitcast.13), channel_id=1, replica_groups=mesh['ens'=8,'gy'=4,'gh'=2,'gx'=4] {'gy','gh','gx'}, dimensions={0} | all-to-all | bytes 4096 | tf_op jit(solution)/shard_map/all_to_all | solution.py:523
  46.3 1.3 %shard_map.70 = f32[4,256,128]{2,1,0:T(8,128)} custom-call(f32[32,16]{1,0:T(8,128)S(1)} %bitcast.12, f32[4,16,4,16,128]{4,3,2,1,0:T(8,128)S(1)} %get-tuple-element.37.basis_ref, f32[4,16,16,128]{3,2,1,0:T(8,128)S(1)} %get-tuple-element.38.strip_ref), custom_call_target="tpu_custom_call" | custom-call | flops 1000 | bytes 1048576 | tf_op jit(solution)/shard_map/pallas_call | solution.py:524
Async XLA Ops:
  0.0 1.0 %copy-start = (f32[1,4,16,16,128]{4,3,2,1,0:T(8,128)S(1)}, f32[1,4,16,16,128]{4,3,2,1,0:T(8,128)}, u32[]{:S(2)}) copy-start(f32[1,4,16,16,128]{4,3,2,1,0:T(8,128)} %param.6) | copy-start | bytes 1572868
  1.8 14.8 %collective-permute-start.4 = (f32[5,4,16,128]{3,2,1,0:T(8,128)S(1)}, f32[5,4,16,128]{3,2,1,0:T(8,128)S(1)}, u32[]{:S(2)}, u32[]{:S(2)}) collective-permute-start(f32[5,4,16,128]{3,2,1,0:T(8,128)S(1)} %get-tuple-element.29), channel_id=1, source_target_pairs={{0,8},{8,16},{16,24},{24,0},{1,9},{9,17},{17,25},{25,1},{2,10},{10... | collective-permute-start | bytes 491528 | tf_op jit(solution)/shard_map/ppermute | solution.py:501
  3.5 13.2 %collective-permute-start.5 = (f32[5,4,16,128]{3,2,1,0:T(8,128)S(1)}, f32[5,4,16,128]{3,2,1,0:T(8,128)S(1)}, u32[]{:S(2)}, u32[]{:S(2)}) collective-permute-start(f32[5,4,16,128]{3,2,1,0:T(8,128)S(1)} %get-tuple-element.30), channel_id=1, source_target_pairs={{8,0},{16,8},{24,16},{0,24},{9,1},{17,9},{25,17},{1,25},{10,2},{18... | collective-permute-start | bytes 491528 | tf_op jit(solution)/shard_map/ppermute | solution.py:502
  5.5 5.0 %collective-permute-start = (f32[3,16,128]{2,1,0:T(8,128)S(1)}, f32[3,16,128]{2,1,0:T(8,128)S(1)}, u32[]{:S(2)}, u32[]{:S(2)}) collective-permute-start(f32[3,16,128]{2,1,0:T(8,128)S(1)} %get-tuple-element.23), channel_id=1, source_target_pairs={{1,2},{2,1},{3,4},{4,3},{5,6},{6,5},{9,10},{10,9},{11,12},{12,11},... | collective-permute-start | bytes 73736 | tf_op jit(solution)/shard_map/ppermute | solution.py:499
  6.2 6.1 %collective-permute-start.1 = (f32[3,16,128]{2,1,0:T(8,128)S(1)}, f32[3,16,128]{2,1,0:T(8,128)S(1)}, u32[]{:S(2)}, u32[]{:S(2)}) collective-permute-start(f32[3,16,128]{2,1,0:T(8,128)S(1)} %get-tuple-element.24), channel_id=1, source_target_pairs={{0,1},{1,0},{2,3},{3,2},{4,5},{5,4},{6,7},{7,6},{8,9},{9,8},{10,11... | collective-permute-start | bytes 73736 | tf_op jit(solution)/shard_map/ppermute | solution.py:500
  12.5 6.6 %collective-permute-start.2 = (f32[5,16,128]{2,1,0:T(8,128)S(1)}, f32[5,16,128]{2,1,0:T(8,128)S(1)}, u32[]{:S(2)}, u32[]{:S(2)}) collective-permute-start(f32[5,16,128]{2,1,0:T(8,128)S(1)} %get-tuple-element.26), channel_id=1, source_target_pairs={{0,8},{8,16},{16,24},{24,0},{1,9},{9,17},{17,25},{25,1},{2,10},{10... | collective-permute-start | bytes 122888 | tf_op jit(solution)/shard_map/ppermute | solution.py:515
  12.9 6.2 %collective-permute-start.3 = (f32[5,16,128]{2,1,0:T(8,128)S(1)}, f32[5,16,128]{2,1,0:T(8,128)S(1)}, u32[]{:S(2)}, u32[]{:S(2)}) collective-permute-start(f32[5,16,128]{2,1,0:T(8,128)S(1)} %get-tuple-element.27), channel_id=1, source_target_pairs={{8,0},{16,8},{24,16},{0,24},{9,1},{17,9},{25,17},{1,25},{10,2},{18... | collective-permute-start | bytes 122888 | tf_op jit(solution)/shard_map/ppermute | solution.py:516

commit v9 on v8

--- a/solution.py
+++ b/solution.py
@@ -87,9 +87,9 @@
 
 
 def beside_x(v):
-    row = lax.broadcasted_iota(jnp.int32, (X, Z), 0)
-    below = jnp.where(row == 0, 0.0, pltpu.roll(v, 1, 0))
-    above = jnp.where(row == X - 1, 0.0, pltpu.roll(v, X - 1, 0))
+    edge = jnp.zeros((1, Z), F32)
+    below = jnp.concatenate([edge, v[: X - 1]])
+    above = jnp.concatenate([v[1:], edge])
     return below, above
 
 

time: 47.7 us -> 47.7 us (level)
  transfers between devices with their start and end apart: 6 -> 6, of which waited for: 1 -> 1; matrix products, arithmetic and copies ran while one was open for 0% -> 0% of each run, Pallas kernels for 7% -> 6%
where the time goes in v9:
time: 47.7 us; the launch traced here: 47.5 us
  blocking collectives  26.4 us (55%)
  starting transfers between devices  11.6 us (24%)
  Pallas kernels  5.96 us (12%)
  waiting for transfers between devices  1.82 us (4%)
  local copies, waits for them, and re-layouts  1.04 us (2%)
  between operations  0.72 us (2%)
    all_to_all x1, blocking collectives, shards(): lax.all_to_all(total, ('gy', *GZ), split_axis=0, concat_axis=0, tiled=True)  26.4 us
    ppermute x1, starting transfers between devices, shards(): from_near = lax.ppermute(to_near, GZ, near)  4.31 us
    ppermute x1, starting transfers between devices, shards(): strip_high = lax.ppermute(strip_top, 'gy', down)  2.87 us
    pallas_call x1, Pallas kernels, shards(): call(main_kernel, (struct(4, Y, *wide), struct(DOTS, 8, Z)), [VMEM] * 4,...  2.31 us
    ppermute x1, waiting for transfers between devices, shards(): from_near = lax.ppermute(to_near, GZ, near)  1.8 us
    ppermute x1, starting transfers between devices, shards(): high = lax.ppermute(top, 'gy', down)  1.66 us
    ppermute x1, starting transfers between devices, shards(): low = lax.ppermute(bottom, 'gy', up)  1.65 us
    pallas_call x1, Pallas kernels, shards(): call(combine_kernel, struct(SPECIES, X * Y, Z), [VMEM] * 3, [VMEM((SPECIE...  1.25 us
  transfers between devices with their start and end apart: 6, of which 1 were waited for; matrix products, arithmetic and copies ran while one was open for 0% of the time, Pallas kernels for 6%

profile of v9, /device:TPU:32, one launch (start us, length us, event | category | flops | bytes accessed | tf_op | source)
XLA Modules:
  0.0 47.5 jit_solution(14227174662817581928)
XLA Ops:
  0.0 0.0 copy-start
  0.0 1.0 %copy-done = f32[1,4,16,16,128]{4,3,2,1,0:T(8,128)S(1)} copy-done((f32[1,4,16,16,128]{4,3,2,1,0:T(8,128)S(1)}, f32[1,4,16,16,128]{4,3,2,1,0:T(8,128)}, u32[]{:S(2)}) %copy-start) | copy-done | bytes 524312
  1.0 0.8 %shard_map.66 = (f32[16,4,16,128]{3,2,1,0:T(8,128)S(1)}, f32[5,4,16,128]{3,2,1,0:T(8,128)S(1)}, f32[5,4,16,128]{3,2,1,0:T(8,128)S(1)}, f32[3,16]{1,0:T(4,128)S(1...) custom-call(f32[4,256,128]{2,1,0:T(8,128)S(1)} %bitcast.10, f32[3,16]{1,0:T(4,128)} %bitcast.15, ...), custom_call_target="tpu_custom_call" | custom-call | flops 1000 | bytes 1048576 | tf_op jit(solution)/shard_map/pallas_call | solution.py:493
  1.8 1.7 %collective-permute-start.4 = (f32[5,4,16,128]{3,2,1,0:T(8,128)S(1)}, f32[5,4,16,128]{3,2,1,0:T(8,128)S(1)}, u32[]{:S(2)}, u32[]{:S(2)}) collective-permute-start(f32[5,4,16,128]{3,2,1,0:T(8,128)S(1)} %get-tuple-element.29), channel_id=1, source_target_pairs={{0,8},{8,16},{16,24},{24,0},{1,9},{9,17},{17,25},{25,1},{2,10},{10... | collective-permute-start | bytes 491528 | tf_op jit(solution)/shard_map/ppermute | solution.py:501
  3.5 1.7 %collective-permute-start.5 = (f32[5,4,16,128]{3,2,1,0:T(8,128)S(1)}, f32[5,4,16,128]{3,2,1,0:T(8,128)S(1)}, u32[]{:S(2)}, u32[]{:S(2)}) collective-permute-start(f32[5,4,16,128]{3,2,1,0:T(8,128)S(1)} %get-tuple-element.30), channel_id=1, source_target_pairs={{8,0},{16,8},{24,16},{0,24},{9,1},{17,9},{25,17},{1,25},{10,2},{18... | collective-permute-start | bytes 491528 | tf_op jit(solution)/shard_map/ppermute | solution.py:502
  5.1 0.4 shard_map.64
  5.5 0.7 %collective-permute-start = (f32[3,16,128]{2,1,0:T(8,128)S(1)}, f32[3,16,128]{2,1,0:T(8,128)S(1)}, u32[]{:S(2)}, u32[]{:S(2)}) collective-permute-start(f32[3,16,128]{2,1,0:T(8,128)S(1)} %get-tuple-element.23), channel_id=1, source_target_pairs={{1,2},{2,1},{3,4},{4,3},{5,6},{6,5},{9,10},{10,9},{11,12},{12,11},... | collective-permute-start | bytes 73736 | tf_op jit(solution)/shard_map/ppermute | solution.py:499
  6.2 4.3 %collective-permute-start.1 = (f32[3,16,128]{2,1,0:T(8,128)S(1)}, f32[3,16,128]{2,1,0:T(8,128)S(1)}, u32[]{:S(2)}, u32[]{:S(2)}) collective-permute-start(f32[3,16,128]{2,1,0:T(8,128)S(1)} %get-tuple-element.24), channel_id=1, source_target_pairs={{0,1},{1,0},{2,3},{3,2},{4,5},{5,4},{6,7},{7,6},{8,9},{9,8},{10,11... | collective-permute-start | bytes 73736 | tf_op jit(solution)/shard_map/ppermute | solution.py:500
  10.5 0.0 collective-permute-done.far_ref
  10.5 1.8 %collective-permute-done.1.near_ref = f32[3,16,128]{2,1,0:T(8,128)S(1)} collective-permute-done((f32[3,16,128]{2,1,0:T(8,128)S(1)}, f32[3,16,128]{2,1,0:T(8,128)S(1)}, u32[]{:S(2)}, u32[]{:S(2)}) %collective-permute-start.1) | collective-permute-done | bytes 24608 | tf_op jit(solution)/shard_map/ppermute | solution.py:500
  12.3 0.1 shard_map.65
  12.5 0.4 collective-permute-start.2
  12.9 2.9 %collective-permute-start.3 = (f32[5,16,128]{2,1,0:T(8,128)S(1)}, f32[5,16,128]{2,1,0:T(8,128)S(1)}, u32[]{:S(2)}, u32[]{:S(2)}) collective-permute-start(f32[5,16,128]{2,1,0:T(8,128)S(1)} %get-tuple-element.27), channel_id=1, source_target_pairs={{8,0},{16,8},{24,16},{0,24},{9,1},{17,9},{25,17},{1,25},{10,2},{18... | collective-permute-start | bytes 122888 | tf_op jit(solution)/shard_map/ppermute | solution.py:516
  16.4 0.2 shard_map.67.table_ref
  16.6 0.0 collective-permute-done.4.low_ref
  16.6 0.0 collective-permute-done.5.high_ref
  16.6 2.3 %shard_map.68 = (f32[4,16,4,16,128]{4,3,2,1,0:T(8,128)S(1)}, f32[13,8,128]{2,1,0:T(8,128)S(1)}) custom-call(f32[16,4,16,128]{3,2,1,0:T(8,128)S(1)} %get-tuple-element.28.own_ref, f32[5,4,16,128]{3,2,1,0:T(8,128)S(1)} %collective-permute-done.4.low_ref, f32[5,4,16,128]{3,2,1,0:T(8,128)S(1)} %collective-permute-done.5.high_ref, f32[40,128]{1,0:T(8,128)S(1)} %shard_map.67.table_ref), custom_call_target="tpu_custom_call" | custom-call | flops 10000000 | bytes 1048576 | tf_op jit(solution)/shard_map/pallas_call | solution.py:505
  19.0 0.0 collective-permute-done.2.low_ref
  19.0 0.0 collective-permute-done.3.high_ref
  19.0 0.9 %shard_map.69 = (f32[4,16,16,128]{3,2,1,0:T(8,128)S(1)}, f32[32,16]{1,0:T(8,128)S(1)}) custom-call(f32[16,16,128]{2,1,0:T(8,128)S(1)} %get-tuple-element.25.strip_ref, f32[5,16,128]{2,1,0:T(8,128)S(1)} %collective-permute-done.2.low_ref, f32[5,16,128]{2,1,0:T(8,128)S(1)} %collective-permute-done.3.high_ref, f32[13,8,128]{2,1,0:T(8,128)S(1)} %get-tuple-element.35.dots_in_ref, ...), custom_call_target="tpu_custom_call" | custom-call | flops 1000 | bytes 1048576 | tf_op jit(solution)/shard_map/pallas_call | solution.py:517
  19.9 26.4 %all_to_all.11 = f32[32,1,16]{2,1,0:T(1,128)S(1)} all-to-all(f32[32,1,16]{2,1,0:T(1,128)S(1)} %bitcast.13), channel_id=1, replica_groups=mesh['ens'=8,'gy'=4,'gh'=2,'gx'=4] {'gy','gh','gx'}, dimensions={0} | all-to-all | bytes 4096 | tf_op jit(solution)/shard_map/all_to_all | solution.py:523
  46.3 1.3 %shard_map.70 = f32[4,256,128]{2,1,0:T(8,128)} custom-call(f32[32,16]{1,0:T(8,128)S(1)} %bitcast.12, f32[4,16,4,16,128]{4,3,2,1,0:T(8,128)S(1)} %get-tuple-element.37.basis_ref, f32[4,16,16,128]{3,2,1,0:T(8,128)S(1)} %get-tuple-element.38.strip_ref), custom_call_target="tpu_custom_call" | custom-call | flops 1000 | bytes 1048576 | tf_op jit(solution)/shard_map/pallas_call | solution.py:524
Async XLA Ops:
  0.0 1.0 %copy-start = (f32[1,4,16,16,128]{4,3,2,1,0:T(8,128)S(1)}, f32[1,4,16,16,128]{4,3,2,1,0:T(8,128)}, u32[]{:S(2)}) copy-start(f32[1,4,16,16,128]{4,3,2,1,0:T(8,128)} %param.6) | copy-start | bytes 1572868
  1.8 14.8 %collective-permute-start.4 = (f32[5,4,16,128]{3,2,1,0:T(8,128)S(1)}, f32[5,4,16,128]{3,2,1,0:T(8,128)S(1)}, u32[]{:S(2)}, u32[]{:S(2)}) collective-permute-start(f32[5,4,16,128]{3,2,1,0:T(8,128)S(1)} %get-tuple-element.29), channel_id=1, source_target_pairs={{0,8},{8,16},{16,24},{24,0},{1,9},{9,17},{17,25},{25,1},{2,10},{10... | collective-permute-start | bytes 491528 | tf_op jit(solution)/shard_map/ppermute | solution.py:501
  3.5 13.2 %collective-permute-start.5 = (f32[5,4,16,128]{3,2,1,0:T(8,128)S(1)}, f32[5,4,16,128]{3,2,1,0:T(8,128)S(1)}, u32[]{:S(2)}, u32[]{:S(2)}) collective-permute-start(f32[5,4,16,128]{3,2,1,0:T(8,128)S(1)} %get-tuple-element.30), channel_id=1, source_target_pairs={{8,0},{16,8},{24,16},{0,24},{9,1},{17,9},{25,17},{1,25},{10,2},{18... | collective-permute-start | bytes 491528 | tf_op jit(solution)/shard_map/ppermute | solution.py:502
  5.5 5.0 %collective-permute-start = (f32[3,16,128]{2,1,0:T(8,128)S(1)}, f32[3,16,128]{2,1,0:T(8,128)S(1)}, u32[]{:S(2)}, u32[]{:S(2)}) collective-permute-start(f32[3,16,128]{2,1,0:T(8,128)S(1)} %get-tuple-element.23), channel_id=1, source_target_pairs={{1,2},{2,1},{3,4},{4,3},{5,6},{6,5},{9,10},{10,9},{11,12},{12,11},... | collective-permute-start | bytes 73736 | tf_op jit(solution)/shard_map/ppermute | solution.py:499
  6.2 6.1 %collective-permute-start.1 = (f32[3,16,128]{2,1,0:T(8,128)S(1)}, f32[3,16,128]{2,1,0:T(8,128)S(1)}, u32[]{:S(2)}, u32[]{:S(2)}) collective-permute-start(f32[3,16,128]{2,1,0:T(8,128)S(1)} %get-tuple-element.24), channel_id=1, source_target_pairs={{0,1},{1,0},{2,3},{3,2},{4,5},{5,4},{6,7},{7,6},{8,9},{9,8},{10,11... | collective-permute-start | bytes 73736 | tf_op jit(solution)/shard_map/ppermute | solution.py:500
  12.5 6.5 %collective-permute-start.2 = (f32[5,16,128]{2,1,0:T(8,128)S(1)}, f32[5,16,128]{2,1,0:T(8,128)S(1)}, u32[]{:S(2)}, u32[]{:S(2)}) collective-permute-start(f32[5,16,128]{2,1,0:T(8,128)S(1)} %get-tuple-element.26), channel_id=1, source_target_pairs={{0,8},{8,16},{16,24},{24,0},{1,9},{9,17},{17,25},{25,1},{2,10},{10... | collective-permute-start | bytes 122888 | tf_op jit(solution)/shard_map/ppermute | solution.py:515
  12.9 6.1 %collective-permute-start.3 = (f32[5,16,128]{2,1,0:T(8,128)S(1)}, f32[5,16,128]{2,1,0:T(8,128)S(1)}, u32[]{:S(2)}, u32[]{:S(2)}) collective-permute-start(f32[5,16,128]{2,1,0:T(8,128)S(1)} %get-tuple-element.27), channel_id=1, source_target_pairs={{8,0},{16,8},{24,16},{0,24},{9,1},{17,9},{25,17},{1,25},{10,2},{18... | collective-permute-start | bytes 122888 | tf_op jit(solution)/shard_map/ppermute | solution.py:516
